TPU v7x, 128 devices: a whole 4x4x4 slice. The times are simulated.
128 devices in a mesh: dp: 1, cp: 128 (over z, y, x, core).
Axes of the slice: x: 4, y: 4, z: 4, core: 2. Of those that a mesh axis runs over, the one named last changes fastest.
Arguments:
- q_rope: bfloat16 [1, 65536, 12, 128], P('dp', 'cp')
- k_rope: bfloat16 [1, 65536, 2, 128], P('dp', 'cp')
- values: bfloat16 [1, 65536, 2, 128], P('dp', 'cp')
- d_out: bfloat16 [1, 65536, 12, 128], P('dp', 'cp')
Outputs:
- output 1: bfloat16 [1, 65536, 12, 128], P('dp', 'cp')
- output 2: bfloat16 [1, 65536, 12, 128], P('dp', 'cp')
- output 3: bfloat16 [1, 65536, 2, 128], P('dp', 'cp')
- output 4: bfloat16 [1, 65536, 2, 128], P('dp', 'cp')
All inputs are finite; a program needn't handle non-finite values.
Results may differ from a plain program's by a relative error of at most 0.00898008.
Values are sent between devices in bfloat16 or wider.
A program may use at most 1 GiB of HBM per device.

v0:
```python
import jax
import jax.numpy as jnp
from jax import lax
from jax.sharding import PartitionSpec as P

BLOCK = 64
LOCAL = 16
STRIDE = 8


def residue_table(kv_heads, group_size):
    head_ids = jnp.arange(kv_heads)[:, None] * group_size + jnp.arange(group_size)[None, :]
    return (-1 - head_ids) % STRIDE


def select_matrix(kv_heads, group_size):
    residues = residue_table(kv_heads, group_size)
    return (jnp.arange(STRIDE)[None, None, :] == residues[:, :, None]).astype(jnp.bfloat16)


def compact(keys_in, group_size):
    n_batch, seq_len, kv_heads, head_dim = keys_in.shape
    grouped = keys_in.reshape(n_batch, seq_len // (BLOCK * STRIDE), STRIDE, BLOCK, kv_heads, head_dim)
    picked = jnp.einsum('bmsigd,gus->bmigud', grouped, select_matrix(kv_heads, group_size), preferred_element_type=jnp.float32)
    return picked.astype(jnp.bfloat16).reshape(n_batch, seq_len // STRIDE, kv_heads, group_size, head_dim)


def expand(grads, group_size):
    n_batch, str_len, kv_heads = grads.shape[0], grads.shape[1], grads.shape[2]
    head_dim = grads.shape[4]
    grouped = grads.reshape(n_batch, str_len // BLOCK, BLOCK, kv_heads, group_size, head_dim)
    spread = jnp.einsum('bmigud,gus->bmsigd', grouped, select_matrix(kv_heads, group_size).astype(jnp.float32))
    return spread.reshape(n_batch, str_len * STRIDE, kv_heads, head_dim)


def shard_attention(q_rope, d_out, k_ext, v_ext, k_str, v_str, shard_idx):
    n_batch, seq_loc, heads, head_dim = q_rope.shape
    kv_heads = k_ext.shape[2]
    group_size = heads // kv_heads
    n_blocks = seq_loc // BLOCK
    halo = (LOCAL - 1) * BLOCK
    window = LOCAL * BLOCK
    scale = 1.0 / head_dim
    str_block = (jnp.arange(k_str.shape[1]) // BLOCK)[None, None, :] * STRIDE + residue_table(kv_heads, group_size)[:, :, None]
    row_ids = jnp.arange(BLOCK)[:, None]
    col_ids = jnp.arange(window)[None, :]
    blk_shape = (n_batch, BLOCK, kv_heads, group_size, head_dim)

    def body(carry, blk_idx):
        dk_ext, dv_ext, dk_str, dv_str = carry
        win_start = blk_idx * BLOCK
        q_blk = lax.dynamic_slice_in_dim(q_rope, win_start, BLOCK, axis=1).reshape(blk_shape)
        do_blk = lax.dynamic_slice_in_dim(d_out, win_start, BLOCK, axis=1).reshape(blk_shape)
        k_win = lax.dynamic_slice_in_dim(k_ext, win_start, window, axis=1)
        v_win = lax.dynamic_slice_in_dim(v_ext, win_start, window, axis=1)
        q_global = shard_idx * n_blocks + blk_idx
        loc_mask = (col_ids <= row_ids + halo) & (col_ids >= halo - q_global * BLOCK)
        str_mask = (str_block <= q_global - LOCAL)[:, :, None, :]
        s_loc = jnp.einsum('bigud,bjgd->bguij', q_blk, k_win, preferred_element_type=jnp.float32) * scale
        s_str = jnp.einsum('bigud,bjgud->bguij', q_blk, k_str, preferred_element_type=jnp.float32) * scale
        s_loc = jnp.where(loc_mask, s_loc, -jnp.inf)
        s_str = jnp.where(str_mask, s_str, -jnp.inf)
        row_max = jnp.maximum(jnp.max(s_loc, axis=-1), jnp.max(s_str, axis=-1))[..., None]
        e_loc = jnp.exp(s_loc - row_max)
        e_str = jnp.exp(s_str - row_max)
        row_sum = jnp.sum(e_loc, axis=-1, keepdims=True) + jnp.sum(e_str, axis=-1, keepdims=True)
        p_loc = e_loc / row_sum
        p_str = e_str / row_sum
        pb_loc = p_loc.astype(jnp.bfloat16)
        pb_str = p_str.astype(jnp.bfloat16)
        o_blk = (jnp.einsum('bguij,bjgd->bigud', pb_loc, v_win, preferred_element_type=jnp.float32)
                 + jnp.einsum('bguij,bjgud->bigud', pb_str, v_str, preferred_element_type=jnp.float32))
        row_delta = jnp.einsum('bigud,bigud->bgui', do_blk.astype(jnp.float32), o_blk)[..., None]
        dp_loc = jnp.einsum('bigud,bjgd->bguij', do_blk, v_win, preferred_element_type=jnp.float32)
        dp_str = jnp.einsum('bigud,bjgud->bguij', do_blk, v_str, preferred_element_type=jnp.float32)
        ds_loc = (p_loc * (dp_loc - row_delta)).astype(jnp.bfloat16)
        ds_str = (p_str * (dp_str - row_delta)).astype(jnp.bfloat16)
        dq_blk = (jnp.einsum('bguij,bjgd->bigud', ds_loc, k_win, preferred_element_type=jnp.float32)
                  + jnp.einsum('bguij,bjgud->bigud', ds_str, k_str, preferred_element_type=jnp.float32)) * scale
        dk_win = jnp.einsum('bguij,bigud->bjgd', ds_loc, q_blk, preferred_element_type=jnp.float32) * scale
        dv_win = jnp.einsum('bguij,bigud->bjgd', pb_loc, do_blk, preferred_element_type=jnp.float32)
        dk_ext = lax.dynamic_update_slice_in_dim(dk_ext, lax.dynamic_slice_in_dim(dk_ext, win_start, window, axis=1) + dk_win, win_start, axis=1)
        dv_ext = lax.dynamic_update_slice_in_dim(dv_ext, lax.dynamic_slice_in_dim(dv_ext, win_start, window, axis=1) + dv_win, win_start, axis=1)
        dk_str = dk_str + jnp.einsum('bguij,bigud->bjgud', ds_str, q_blk, preferred_element_type=jnp.float32) * scale
        dv_str = dv_str + jnp.einsum('bguij,bigud->bjgud', pb_str, do_blk, preferred_element_type=jnp.float32)
        return (dk_ext, dv_ext, dk_str, dv_str), (o_blk.astype(jnp.bfloat16), dq_blk.astype(jnp.bfloat16))

    init = (jnp.zeros(k_ext.shape, jnp.float32), jnp.zeros(v_ext.shape, jnp.float32), jnp.zeros(k_str.shape, jnp.float32), jnp.zeros(v_str.shape, jnp.float32))
    carry, stacked = lax.scan(body, init, jnp.arange(n_blocks))
    out_shape = (n_batch, seq_loc, heads, head_dim)
    attn_out = jnp.moveaxis(stacked[0], 0, 1).reshape(out_shape)
    d_q = jnp.moveaxis(stacked[1], 0, 1).reshape(out_shape)
    return (attn_out, d_q) + carry


def halo_lengths(seq_loc):
    halo = (LOCAL - 1) * BLOCK
    hop_count = -(-halo // seq_loc)
    return [seq_loc] * (hop_count - 1) + [halo - (hop_count - 1) * seq_loc]


def fetch_halo(local_part, lengths, cp_size):
    seq_loc = local_part.shape[1]
    pieces = []
    for dist in range(len(lengths), 0, -1):
        tail_part = local_part[:, seq_loc - lengths[dist - 1]:]
        if dist < cp_size:
            pieces.append(lax.ppermute(tail_part, 'cp', [(sender, sender + dist) for sender in range(cp_size - dist)]))
        else:
            pieces.append(jnp.zeros_like(tail_part))
    return jnp.concatenate(pieces + [local_part], axis=1)


def return_halo(halo_grad, lengths, cp_size, seq_loc):
    result = jnp.zeros(halo_grad.shape[:1] + (seq_loc,) + halo_grad.shape[2:], jnp.float32)
    offset = 0
    for dist in range(len(lengths), 0, -1):
        size_d = lengths[dist - 1]
        seg_part = halo_grad[:, offset:offset + size_d]
        offset = offset + size_d
        if dist < cp_size:
            arrived = lax.ppermute(seg_part.astype(jnp.bfloat16), 'cp', [(sender + dist, sender) for sender in range(cp_size - dist)])
            result = result + jnp.pad(arrived, ((0, 0), (seq_loc - size_d, 0), (0, 0), (0, 0))).astype(jnp.float32)
    return result


def owner_sum(contrib, cp_size):
    received = lax.all_to_all(contrib.astype(jnp.bfloat16), 'cp', 1, 1, tiled=True)
    split_shape = received.shape[:1] + (cp_size, received.shape[1] // cp_size) + received.shape[2:]
    return jnp.sum(received.reshape(split_shape), axis=1, dtype=jnp.float32)


def solution(mesh):
    cp_size = mesh.shape['cp']
    spec = P('dp', 'cp', None, None)

    def per_device(q_rope, k_rope, values, d_out):
        seq_loc = q_rope.shape[1]
        group_size = q_rope.shape[2] // k_rope.shape[2]
        halo = (LOCAL - 1) * BLOCK
        lengths = halo_lengths(seq_loc)
        shard_idx = lax.axis_index('cp')
        k_ext = fetch_halo(k_rope, lengths, cp_size)
        v_ext = fetch_halo(values, lengths, cp_size)
        k_str = lax.all_gather(compact(k_rope, group_size), 'cp', axis=1, tiled=True)
        v_str = lax.all_gather(compact(values, group_size), 'cp', axis=1, tiled=True)
        attn_out, d_q, dk_ext, dv_ext, dk_str, dv_str = shard_attention(q_rope, d_out, k_ext, v_ext, k_str, v_str, shard_idx)
        d_k = dk_ext[:, halo:] + return_halo(dk_ext[:, :halo], lengths, cp_size, seq_loc) + expand(owner_sum(dk_str, cp_size), group_size)
        d_v = dv_ext[:, halo:] + return_halo(dv_ext[:, :halo], lengths, cp_size, seq_loc) + expand(owner_sum(dv_str, cp_size), group_size)
        return attn_out, d_q, d_k.astype(jnp.bfloat16), d_v.astype(jnp.bfloat16)

    return jax.shard_map(per_device, mesh=mesh, in_specs=(spec, spec, spec, spec), out_specs=(spec, spec, spec, spec), check_vma=False)
```

profile of v0, /device:TPU:85, one launch (start us, length us, event | category | flops | bytes accessed | tf_op | source)
XLA Modules:
  0.0 2710.3 jit_solution(16533035622990141875)
XLA Ops:
  36.6 82.5 %all-gather.7.cloned.1.call-done = bf16[1,1,8192,2,6,128]{5,4,2,3,1,0:T(8,128)(2,1)} async-done(((bf16[1,1,64,2,6,128]{5,4,2,3,1,0:T(8,128)(2,1)}), bf16[1,1,8192,2,6,128]{5,4,2,3,1,0:T(8,128)(2,1)}) %all-gather.7.cloned.1.call-update) | async-done | bytes 25165840 | tf_op jit(solution)/shard_map/all_gather | solution.py:146
  119.1 24.0 copy.89
  143.1 85.1 %all-gather.5.cloned.1.call-done = bf16[1,1,8192,2,6,128]{5,4,2,3,1,0:T(8,128)(2,1)} async-done(((bf16[1,1,64,2,6,128]{5,4,2,3,1,0:T(8,128)(2,1)}), bf16[1,1,8192,2,6,128]{5,4,2,3,1,0:T(8,128)(2,1)}) %all-gather.5.cloned.1.call-update) | async-done | bytes 25165840 | tf_op jit(solution)/shard_map/all_gather | solution.py:145
  228.2 24.0 copy.88
  253.6 1546.3 %while.24 = (s32[]{:T(128)}, f32[1,1472,2,128]{3,1,2,0:T(8,128)}, f32[1,1472,2,128]{3,1,2,0:T(8,128)S(1)}, f32[1,8192,2,6,128]{1,4,3,2,0:T(8,128)}, f32[1,8192,2...) while((s32[]{:T(128)}, f32[1,1472,2,128]{3,1,2,0:T(8,128)}, ...), condition=%wide.region_5.6_spmd.clone.clone, body=%wide.region_0.5_spmd.clone.clone.sunk | while | flops 11106319360 | bytes 550006848 | solution.py:89
  264.3 22.6 fusion.193
  369.4 26.7 bitcast_add_fusion.5
  428.5 22.6 fusion.193
  533.6 43.1 %bitcast_add_fusion.5 = f32[1,8192,2,6,128]{1,4,3,2,0:T(8,128)} fusion(f32[1,8192,2,6,128]{1,4,3,2,0:T(8,128)} %get-tuple-element.614, pred[]{:T(512)S(6)} %compare.13, bf16[64,2,6,128]{3,0,2,1:T(8,128)(2,1)S(1)} %bitcast.340, f32[2,6,64,8192]{3,2,1,0:T(8,128)} %get-tuple-element.581, f32[2,6,64]{2,1,0:T(8,128)S(1)} %add.339, ...), kind=kOutput, calls=%fused_computation.3.clone.1 | convolution fusion | flops 1667235840 | bytes 126130176 | tf_op jit(solution)/shard_map/while/body/eval_jaxpr/bguij,bigud->bjgud/dot_general | solution.py:85
  576.7 38.5 %bitcast_add_fusion.4 = f32[1,8192,2,6,128]{1,4,3,2,0:T(8,128)} fusion(f32[1,8192,2,6,128]{1,4,3,2,0:T(8,128)} %get-tuple-element.613, pred[]{:T(512)S(6)} %compare.13, bf16[64,2,6,128]{3,0,2,1:T(8,128)(2,1)S(1)} %bitcast.331, bf16[2,6,64,8192]{3,2,1,0:T(8,128)(2,1)} %multiply_convert_fusion.2), kind=kOutput, calls=%fused_computation.4.clone.1 | convolution fusion | flops 1648361472 | bytes 113442816 | tf_op jit(solution)/shard_map/while/body/eval_jaxpr/bguij,bigud->bjgud/dot_general | solution.py:84
  626.0 22.6 fusion.193
  731.0 43.1 %bitcast_add_fusion.5 = f32[1,8192,2,6,128]{1,4,3,2,0:T(8,128)} fusion(f32[1,8192,2,6,128]{1,4,3,2,0:T(8,128)} %get-tuple-element.614, pred[]{:T(512)S(6)} %compare.13, bf16[64,2,6,128]{3,0,2,1:T(8,128)(2,1)S(1)} %bitcast.340, f32[2,6,64,8192]{3,2,1,0:T(8,128)} %get-tuple-element.581, f32[2,6,64]{2,1,0:T(8,128)S(1)} %add.339, ...), kind=kOutput, calls=%fused_computation.3.clone.1 | convolution fusion | flops 1667235840 | bytes 126130176 | tf_op jit(solution)/shard_map/while/body/eval_jaxpr/bguij,bigud->bjgud/dot_general | solution.py:85
  774.1 38.5 %bitcast_add_fusion.4 = f32[1,8192,2,6,128]{1,4,3,2,0:T(8,128)} fusion(f32[1,8192,2,6,128]{1,4,3,2,0:T(8,128)} %get-tuple-element.613, pred[]{:T(512)S(6)} %compare.13, bf16[64,2,6,128]{3,0,2,1:T(8,128)(2,1)S(1)} %bitcast.331, bf16[2,6,64,8192]{3,2,1,0:T(8,128)(2,1)} %multiply_convert_fusion.2), kind=kOutput, calls=%fused_computation.4.clone.1 | convolution fusion | flops 1648361472 | bytes 113442816 | tf_op jit(solution)/shard_map/while/body/eval_jaxpr/bguij,bigud->bjgud/dot_general | solution.py:84
  823.4 22.6 fusion.193
  928.4 43.1 %bitcast_add_fusion.5 = f32[1,8192,2,6,128]{1,4,3,2,0:T(8,128)} fusion(f32[1,8192,2,6,128]{1,4,3,2,0:T(8,128)} %get-tuple-element.614, pred[]{:T(512)S(6)} %compare.13, bf16[64,2,6,128]{3,0,2,1:T(8,128)(2,1)S(1)} %bitcast.340, f32[2,6,64,8192]{3,2,1,0:T(8,128)} %get-tuple-element.581, f32[2,6,64]{2,1,0:T(8,128)S(1)} %add.339, ...), kind=kOutput, calls=%fused_computation.3.clone.1 | convolution fusion | flops 1667235840 | bytes 126130176 | tf_op jit(solution)/shard_map/while/body/eval_jaxpr/bguij,bigud->bjgud/dot_general | solution.py:85
  971.5 38.5 %bitcast_add_fusion.4 = f32[1,8192,2,6,128]{1,4,3,2,0:T(8,128)} fusion(f32[1,8192,2,6,128]{1,4,3,2,0:T(8,128)} %get-tuple-element.613, pred[]{:T(512)S(6)} %compare.13, bf16[64,2,6,128]{3,0,2,1:T(8,128)(2,1)S(1)} %bitcast.331, bf16[2,6,64,8192]{3,2,1,0:T(8,128)(2,1)} %multiply_convert_fusion.2), kind=kOutput, calls=%fused_computation.4.clone.1 | convolution fusion | flops 1648361472 | bytes 113442816 | tf_op jit(solution)/shard_map/while/body/eval_jaxpr/bguij,bigud->bjgud/dot_general | solution.py:84
  1020.8 22.6 fusion.193
  1125.8 43.1 %bitcast_add_fusion.5 = f32[1,8192,2,6,128]{1,4,3,2,0:T(8,128)} fusion(f32[1,8192,2,6,128]{1,4,3,2,0:T(8,128)} %get-tuple-element.614, pred[]{:T(512)S(6)} %compare.13, bf16[64,2,6,128]{3,0,2,1:T(8,128)(2,1)S(1)} %bitcast.340, f32[2,6,64,8192]{3,2,1,0:T(8,128)} %get-tuple-element.581, f32[2,6,64]{2,1,0:T(8,128)S(1)} %add.339, ...), kind=kOutput, calls=%fused_computation.3.clone.1 | convolution fusion | flops 1667235840 | bytes 126130176 | tf_op jit(solution)/shard_map/while/body/eval_jaxpr/bguij,bigud->bjgud/dot_general | solution.py:85
  1168.9 38.5 %bitcast_add_fusion.4 = f32[1,8192,2,6,128]{1,4,3,2,0:T(8,128)} fusion(f32[1,8192,2,6,128]{1,4,3,2,0:T(8,128)} %get-tuple-element.613, pred[]{:T(512)S(6)} %compare.13, bf16[64,2,6,128]{3,0,2,1:T(8,128)(2,1)S(1)} %bitcast.331, bf16[2,6,64,8192]{3,2,1,0:T(8,128)(2,1)} %multiply_convert_fusion.2), kind=kOutput, calls=%fused_computation.4.clone.1 | convolution fusion | flops 1648361472 | bytes 113442816 | tf_op jit(solution)/shard_map/while/body/eval_jaxpr/bguij,bigud->bjgud/dot_general | solution.py:84
  1218.2 22.6 fusion.193
  1323.2 43.1 %bitcast_add_fusion.5 = f32[1,8192,2,6,128]{1,4,3,2,0:T(8,128)} fusion(f32[1,8192,2,6,128]{1,4,3,2,0:T(8,128)} %get-tuple-element.614, pred[]{:T(512)S(6)} %compare.13, bf16[64,2,6,128]{3,0,2,1:T(8,128)(2,1)S(1)} %bitcast.340, f32[2,6,64,8192]{3,2,1,0:T(8,128)} %get-tuple-element.581, f32[2,6,64]{2,1,0:T(8,128)S(1)} %add.339, ...), kind=kOutput, calls=%fused_computation.3.clone.1 | convolution fusion | flops 1667235840 | bytes 126130176 | tf_op jit(solution)/shard_map/while/body/eval_jaxpr/bguij,bigud->bjgud/dot_general | solution.py:85
  1366.3 38.5 %bitcast_add_fusion.4 = f32[1,8192,2,6,128]{1,4,3,2,0:T(8,128)} fusion(f32[1,8192,2,6,128]{1,4,3,2,0:T(8,128)} %get-tuple-element.613, pred[]{:T(512)S(6)} %compare.13, bf16[64,2,6,128]{3,0,2,1:T(8,128)(2,1)S(1)} %bitcast.331, bf16[2,6,64,8192]{3,2,1,0:T(8,128)(2,1)} %multiply_convert_fusion.2), kind=kOutput, calls=%fused_computation.4.clone.1 | convolution fusion | flops 1648361472 | bytes 113442816 | tf_op jit(solution)/shard_map/while/body/eval_jaxpr/bguij,bigud->bjgud/dot_general | solution.py:84
  1415.6 22.6 fusion.193
  1520.6 43.1 %bitcast_add_fusion.5 = f32[1,8192,2,6,128]{1,4,3,2,0:T(8,128)} fusion(f32[1,8192,2,6,128]{1,4,3,2,0:T(8,128)} %get-tuple-element.614, pred[]{:T(512)S(6)} %compare.13, bf16[64,2,6,128]{3,0,2,1:T(8,128)(2,1)S(1)} %bitcast.340, f32[2,6,64,8192]{3,2,1,0:T(8,128)} %get-tuple-element.581, f32[2,6,64]{2,1,0:T(8,128)S(1)} %add.339, ...), kind=kOutput, calls=%fused_computation.3.clone.1 | convolution fusion | flops 1667235840 | bytes 126130176 | tf_op jit(solution)/shard_map/while/body/eval_jaxpr/bguij,bigud->bjgud/dot_general | solution.py:85
  1563.7 38.5 %bitcast_add_fusion.4 = f32[1,8192,2,6,128]{1,4,3,2,0:T(8,128)} fusion(f32[1,8192,2,6,128]{1,4,3,2,0:T(8,128)} %get-tuple-element.613, pred[]{:T(512)S(6)} %compare.13, bf16[64,2,6,128]{3,0,2,1:T(8,128)(2,1)S(1)} %bitcast.331, bf16[2,6,64,8192]{3,2,1,0:T(8,128)(2,1)} %multiply_convert_fusion.2), kind=kOutput, calls=%fused_computation.4.clone.1 | convolution fusion | flops 1648361472 | bytes 113442816 | tf_op jit(solution)/shard_map/while/body/eval_jaxpr/bguij,bigud->bjgud/dot_general | solution.py:84
  1613.0 22.6 fusion.193
  1718.0 43.1 %bitcast_add_fusion.5 = f32[1,8192,2,6,128]{1,4,3,2,0:T(8,128)} fusion(f32[1,8192,2,6,128]{1,4,3,2,0:T(8,128)} %get-tuple-element.614, pred[]{:T(512)S(6)} %compare.13, bf16[64,2,6,128]{3,0,2,1:T(8,128)(2,1)S(1)} %bitcast.340, f32[2,6,64,8192]{3,2,1,0:T(8,128)} %get-tuple-element.581, f32[2,6,64]{2,1,0:T(8,128)S(1)} %add.339, ...), kind=kOutput, calls=%fused_computation.3.clone.1 | convolution fusion | flops 1667235840 | bytes 126130176 | tf_op jit(solution)/shard_map/while/body/eval_jaxpr/bguij,bigud->bjgud/dot_general | solution.py:85
  1761.2 38.5 %bitcast_add_fusion.4 = f32[1,8192,2,6,128]{1,4,3,2,0:T(8,128)} fusion(f32[1,8192,2,6,128]{1,4,3,2,0:T(8,128)} %get-tuple-element.613, pred[]{:T(512)S(6)} %compare.13, bf16[64,2,6,128]{3,0,2,1:T(8,128)(2,1)S(1)} %bitcast.331, bf16[2,6,64,8192]{3,2,1,0:T(8,128)(2,1)} %multiply_convert_fusion.2), kind=kOutput, calls=%fused_computation.4.clone.1 | convolution fusion | flops 1648361472 | bytes 113442816 | tf_op jit(solution)/shard_map/while/body/eval_jaxpr/bguij,bigud->bjgud/dot_general | solution.py:84
  1799.9 69.5 %copy.94 = bf16[1,8192,2,6,128]{4,2,3,0,1:T(2,128)(2,1)} copy(f32[1,8192,2,6,128]{1,4,3,2,0:T(8,128)} %get-tuple-element.238) | data formatting | bytes 75497472 | tf_op jit(solution)/shard_map/while | solution.py:89
  1879.4 69.5 %copy.100 = bf16[1,8192,2,6,128]{4,2,3,0,1:T(2,128)(2,1)} copy(f32[1,8192,2,6,128]{1,4,3,2,0:T(8,128)} %get-tuple-element.240) | data formatting | bytes 75497472 | tf_op jit(solution)/shard_map/while | solution.py:89
  1948.9 321.2 %all-to-all-done = bf16[1,8192,2,6,128]{4,2,3,0,1:T(2,128)(2,1)} async-done(((bf16[1,8192,2,6,128]{4,2,3,0,1:T(2,128)(2,1)}), bf16[1,8192,2,6,128]{4,2,3,0,1:T(2,128)(2,1)}, u32[]{:S(2)}, u32[]{:S(2)}) %all-to-all-start) | async-done | bytes 25165856 | tf_op jit(solution)/shard_map/all_to_all | solution.py:128
  2313.3 367.5 %all-to-all-done.1 = bf16[1,8192,2,6,128]{4,2,3,0,1:T(2,128)(2,1)} async-done(((bf16[1,8192,2,6,128]{4,2,3,0,1:T(2,128)(2,1)}), bf16[1,8192,2,6,128]{4,2,3,0,1:T(2,128)(2,1)}, u32[]{:S(2)}, u32[]{:S(2)}) %all-to-all-start.1) | async-done | bytes 25165856 | tf_op jit(solution)/shard_map/all_to_all | solution.py:128
  (591 shorter events, 861.0 us)
Async XLA Ops:
  7.2 111.9 %all-gather.7.cloned.1.call-start = ((), (), s32[]{:S(2)}) async-start(), calls=%async_computation.3 | async-start | bytes 33816576 | tf_op jit(solution)/shard_map/all_gather | solution.py:146
  9.4 218.9 %all-gather.5.cloned.1.call-start = ((), (), s32[]{:S(2)}) async-start(), calls=%async_computation.2 | async-start | bytes 33816576 | tf_op jit(solution)/shard_map/all_gather | solution.py:145
  12.5 12.7 collective-permute-start.3
  15.9 9.2 collective-permute-start.2
  19.8 15.9 collective-permute-start.1
  22.0 13.7 collective-permute-start
  576.7 38.5 %copy-start.11 = (s32[8192]{0:T(1024)S(1)}, s32[8192]{0:T(1024)}, u32[]{:S(2)}) copy-start(s32[8192]{0:T(1024)} %copy-done.10) | copy-start | bytes 98308 | tf_op jit(solution)/shard_map/while
  576.7 38.5 %copy-start.14 = (s32[2,6]{1,0:T(2,128)S(1)}, s32[2,6]{1,0:T(2,128)}, u32[]{:S(2)}) copy-start(s32[2,6]{1,0:T(2,128)} %copy-done.13) | copy-start | bytes 148 | tf_op jit(solution)/shard_map/while
  576.7 38.5 %copy-start.18 = (s32[8]{0:T(128)S(1)}, s32[8]{0:T(128)}, u32[]{:S(2)}) copy-start(s32[8]{0:T(128)} %copy-done.17) | copy-start | bytes 100 | tf_op jit(solution)/shard_map/while
  774.1 38.5 %copy-start.11 = (s32[8192]{0:T(1024)S(1)}, s32[8192]{0:T(1024)}, u32[]{:S(2)}) copy-start(s32[8192]{0:T(1024)} %copy-done.10) | copy-start | bytes 98308 | tf_op jit(solution)/shard_map/while
  774.1 38.5 %copy-start.14 = (s32[2,6]{1,0:T(2,128)S(1)}, s32[2,6]{1,0:T(2,128)}, u32[]{:S(2)}) copy-start(s32[2,6]{1,0:T(2,128)} %copy-done.13) | copy-start | bytes 148 | tf_op jit(solution)/shard_map/while
  774.1 38.5 %copy-start.18 = (s32[8]{0:T(128)S(1)}, s32[8]{0:T(128)}, u32[]{:S(2)}) copy-start(s32[8]{0:T(128)} %copy-done.17) | copy-start | bytes 100 | tf_op jit(solution)/shard_map/while
  971.5 38.5 %copy-start.11 = (s32[8192]{0:T(1024)S(1)}, s32[8192]{0:T(1024)}, u32[]{:S(2)}) copy-start(s32[8192]{0:T(1024)} %copy-done.10) | copy-start | bytes 98308 | tf_op jit(solution)/shard_map/while
  971.5 38.5 %copy-start.14 = (s32[2,6]{1,0:T(2,128)S(1)}, s32[2,6]{1,0:T(2,128)}, u32[]{:S(2)}) copy-start(s32[2,6]{1,0:T(2,128)} %copy-done.13) | copy-start | bytes 148 | tf_op jit(solution)/shard_map/while
  971.5 38.5 %copy-start.18 = (s32[8]{0:T(128)S(1)}, s32[8]{0:T(128)}, u32[]{:S(2)}) copy-start(s32[8]{0:T(128)} %copy-done.17) | copy-start | bytes 100 | tf_op jit(solution)/shard_map/while
  1168.9 38.5 %copy-start.14 = (s32[2,6]{1,0:T(2,128)S(1)}, s32[2,6]{1,0:T(2,128)}, u32[]{:S(2)}) copy-start(s32[2,6]{1,0:T(2,128)} %copy-done.13) | copy-start | bytes 148 | tf_op jit(solution)/shard_map/while
  1168.9 38.5 %copy-start.18 = (s32[8]{0:T(128)S(1)}, s32[8]{0:T(128)}, u32[]{:S(2)}) copy-start(s32[8]{0:T(128)} %copy-done.17) | copy-start | bytes 100 | tf_op jit(solution)/shard_map/while
  1366.3 38.5 %copy-start.14 = (s32[2,6]{1,0:T(2,128)S(1)}, s32[2,6]{1,0:T(2,128)}, u32[]{:S(2)}) copy-start(s32[2,6]{1,0:T(2,128)} %copy-done.13) | copy-start | bytes 148 | tf_op jit(solution)/shard_map/while
  1366.3 38.5 %copy-start.18 = (s32[8]{0:T(128)S(1)}, s32[8]{0:T(128)}, u32[]{:S(2)}) copy-start(s32[8]{0:T(128)} %copy-done.17) | copy-start | bytes 100 | tf_op jit(solution)/shard_map/while
  1563.7 38.5 %copy-start.11 = (s32[8192]{0:T(1024)S(1)}, s32[8192]{0:T(1024)}, u32[]{:S(2)}) copy-start(s32[8192]{0:T(1024)} %copy-done.10) | copy-start | bytes 98308 | tf_op jit(solution)/shard_map/while
  1563.7 38.5 %copy-start.14 = (s32[2,6]{1,0:T(2,128)S(1)}, s32[2,6]{1,0:T(2,128)}, u32[]{:S(2)}) copy-start(s32[2,6]{1,0:T(2,128)} %copy-done.13) | copy-start | bytes 148 | tf_op jit(solution)/shard_map/while
  1563.7 38.5 %copy-start.18 = (s32[8]{0:T(128)S(1)}, s32[8]{0:T(128)}, u32[]{:S(2)}) copy-start(s32[8]{0:T(128)} %copy-done.17) | copy-start | bytes 100 | tf_op jit(solution)/shard_map/while
  1761.1 38.5 %copy-start.11 = (s32[8192]{0:T(1024)S(1)}, s32[8192]{0:T(1024)}, u32[]{:S(2)}) copy-start(s32[8192]{0:T(1024)} %copy-done.10) | copy-start | bytes 98308 | tf_op jit(solution)/shard_map/while
  1761.1 38.5 %copy-start.14 = (s32[2,6]{1,0:T(2,128)S(1)}, s32[2,6]{1,0:T(2,128)}, u32[]{:S(2)}) copy-start(s32[2,6]{1,0:T(2,128)} %copy-done.13) | copy-start | bytes 148 | tf_op jit(solution)/shard_map/while
  1761.1 38.5 %copy-start.18 = (s32[8]{0:T(128)S(1)}, s32[8]{0:T(128)}, u32[]{:S(2)}) copy-start(s32[8]{0:T(128)} %copy-done.17) | copy-start | bytes 100 | tf_op jit(solution)/shard_map/while
  1799.9 69.5 %copy-start.15 = (s32[2,6]{1,0:T(2,128)}, s32[2,6]{1,0:T(2,128)S(1)}, u32[]{:S(2)}) copy-start(s32[2,6]{1,0:T(2,128)S(1)} %get-tuple-element.685) | copy-start | bytes 148
  1869.4 400.7 %all-to-all-start = ((bf16[1,8192,2,6,128]{4,2,3,0,1:T(2,128)(2,1)}), bf16[1,8192,2,6,128]{4,2,3,0,1:T(2,128)(2,1)}, u32[]{:S(2)}, u32[]{:S(2)}) async-start(bf16[1,8192,2,6,128]{4,2,3,0,1:T(2,128)(2,1)} %copy.94), calls=%async_computation | async-start | bytes 50331648 | tf_op jit(solution)/shard_map/all_to_all | solution.py:128
  2270.1 410.7 %all-to-all-start.1 = ((bf16[1,8192,2,6,128]{4,2,3,0,1:T(2,128)(2,1)}), bf16[1,8192,2,6,128]{4,2,3,0,1:T(2,128)(2,1)}, u32[]{:S(2)}, u32[]{:S(2)}) async-start(bf16[1,8192,2,6,128]{4,2,3,0,1:T(2,128)(2,1)} %copy.100), calls=%async_computation.1 | async-start | bytes 50331648 | tf_op jit(solution)/shard_map/all_to_all | solution.py:128
  2283.3 416.5 %collective-permute-start.4 = (bf16[1,448,2,128]{3,1,2,0:T(8,128)(2,1)}, bf16[1,448,2,128]{3,1,2,0:T(8,128)(2,1)S(1)}, u32[]{:S(2)}, u32[]{:S(2)}) collective-permute-start(bf16[1,448,2,128]{3,1,2,0:T(8,128)(2,1)} %slice.44), channel_id=1, source_target_pairs={{2,0},{3,1},{4,2},{5,3},{6,4},{7,5},{8,6},{9,7},{10,8},{11,9},{12,... | collective-permute-start | bytes 688136 | tf_op jit(solution)/shard_map/ppermute | solution.py:122
  2285.5 414.4 %collective-permute-start.5 = (bf16[1,512,2,128]{3,1,2,0:T(8,128)(2,1)S(1)}, bf16[1,512,2,128]{3,1,2,0:T(8,128)(2,1)S(1)}, u32[]{:S(2)}, u32[]{:S(2)}) collective-permute-start(bf16[1,512,2,128]{3,1,2,0:T(8,128)(2,1)S(1)} %slice.45), channel_id=1, source_target_pairs={{1,0},{2,1},{3,2},{4,3},{5,4},{6,5},{7,6},{8,7},{9,8},{10,9},{11,1... | collective-permute-start | bytes 786440 | tf_op jit(solution)/shard_map/ppermute | solution.py:122
  2288.1 414.3 %collective-permute-start.6 = (bf16[1,448,2,128]{3,1,2,0:T(8,128)(2,1)S(1)}, bf16[1,448,2,128]{3,1,2,0:T(8,128)(2,1)S(1)}, u32[]{:S(2)}, u32[]{:S(2)}) collective-permute-start(bf16[1,448,2,128]{3,1,2,0:T(8,128)(2,1)S(1)} %slice.46), channel_id=1, source_target_pairs={{2,0},{3,1},{4,2},{5,3},{6,4},{7,5},{8,6},{9,7},{10,8},{11,9},{12,... | collective-permute-start | bytes 688136 | tf_op jit(solution)/shard_map/ppermute | solution.py:122
  2290.3 412.1 %collective-permute-start.7 = (bf16[1,512,2,128]{3,1,2,0:T(8,128)(2,1)S(1)}, bf16[1,512,2,128]{3,1,2,0:T(8,128)(2,1)S(1)}, u32[]{:S(2)}, u32[]{:S(2)}) collective-permute-start(bf16[1,512,2,128]{3,1,2,0:T(8,128)(2,1)S(1)} %slice.47), channel_id=1, source_target_pairs={{1,0},{2,1},{3,2},{4,3},{5,4},{6,5},{7,6},{8,7},{9,8},{10,9},{11,1... | collective-permute-start | bytes 786440 | tf_op jit(solution)/shard_map/ppermute | solution.py:122
  (134 other events, 1376.1 us)
Sparse Core Ops, SparseCore 0:
  11.6 107.4 all-gather.6
  122.7 105.5 all-gather.4
where the time goes:
time: 2720 us; the launch traced here: 2710 us
  matrix products  1320 us (49%)
  waiting for transfers between devices  866 us (32%)
  local copies, waits for them, and re-layouts  329 us (12%)
  other arithmetic  122 us (4%)
  starting transfers between devices  43.7 us (2%)
    all_to_all x2, waiting for transfers between devices, owner_sum(): lax.all_to_all(contrib.astype(jnp.bfloat16), 'cp', 1, 1, tiled=True)  689 us
    dot_general x8, matrix products, body(): jnp.einsum('bguij,bigud->bjgud', pb_str, do_blk, preferred_element_type=j...  328 us
    dot_general x8, matrix products, body(): jnp.einsum('bguij,bigud->bjgud', ds_str, q_blk, preferred_element_type=jn...  291 us
    dot_general x8, matrix products, body(): jnp.einsum('bigud,bjgud->bguij', q_blk, k_str, preferred_element_type=jnp...  181 us
    dot_general x8, matrix products, body(): jnp.einsum('bigud,bjgud->bguij', do_blk, v_str, preferred_element_type=jn...  176 us
    dot_general x8, matrix products, body(): jnp.einsum('bguij,bjgud->bigud', pb_str, v_str, preferred_element_type=jn...  152 us
    while x2, local copies, waits for them, and re-layouts, shard_attention(): carry, stacked = lax.scan(body, init, jnp.arange(n_blocks))  139 us
    dot_general x8, matrix products, body(): jnp.einsum('bguij,bjgud->bigud', ds_str, k_str, preferred_element_type=jn...  119 us
  transfers between devices with their start and end apart: 12, of which 5 were waited for; matrix products, arithmetic and copies ran while one was open for 5% of the time, Pallas kernels for 0%

commit v1 on v0

v1 whole, which is shorter than its diff:
```python
import functools
import math

import jax
import jax.numpy as jnp
from jax import lax
from jax.experimental import pallas as pl
from jax.experimental.pallas import tpu as pltpu
from jax.sharding import PartitionSpec as P


BLOCK = 64
LOCAL = 16
STRIDE = 8
NX = 4
TRIPLE = 3
HALF = 256
RUN = 512
HALO = 1024
CHUNK = 512
F32 = jnp.float32
BF16 = jnp.bfloat16


def dev(z, y, x, c):
    return ((z * 4 + y) * NX + x) * 2 + c


def zof(zp, zm):
    return zp if zm == 0 else 3 - zp


GROUP_Q = [[dev(zof(zp, zm), y, x, c) for zm in range(2) for x in range(NX)] for zp in range(2) for y in range(4) for c in range(2)]
GROUP_X = [[dev(z, y, x, c) for x in range(NX)] for z in range(4) for y in range(4) for c in range(2)]
GROUP_ZYC = [[dev(z, y, x, c) for z in range(4) for y in range(4) for c in range(2)] for x in range(NX)]
GROUP_WG = [[dev(zof(zp, zm), y, 2 * xh + xl, c) for zm in range(2) for xl in range(2) for c in range(2)] for zp in range(2) for y in range(4) for xh in range(2)]
GROUP_W = [[dev(zof(zp, zm), y, x, c) for zm in range(2) for x in range(NX) for c in range(2)] for zp in range(2) for y in range(4)]


def residue(head):
    return (-1 - head) % STRIDE


def nt(a, b):
    return lax.dot_general(a, b, (((1,), (1,)), ((), ())), preferred_element_type=F32)


def tn(a, b):
    return lax.dot_general(a, b, (((0,), (0,)), ((), ())), preferred_element_type=F32)


def nn(a, b):
    return lax.dot_general(a, b, (((1,), (0,)), ((), ())), preferred_element_type=F32)


def attn_kernel(info, q_ref, do_ref, ks_ref, vs_ref, kw_ref, o_ref, dq_ref, dkv_ref, dkw_ref,
                e_s, dp_s, m_s, e_l, dp_l, dk_s, dv_s):
    tile = pl.program_id(0)
    member = tile // NX
    xsrc = tile % NX
    scale = 1.0 / 128
    cexp = scale * math.log2(math.e)
    group = info[member]
    core = info[2]
    half = info[3]
    res = info[4]
    t0 = RUN * (2 * xsrc + core) + HALF * half
    blk0 = group * 64 + t0 // BLOCK
    first_valid = HALO - (group * 4096 + t0)
    q = q_ref[0, 0]
    do = do_ref[0, 0]
    n_chunk = group + 1
    nl = (HALO + HALF) // HALF

    @pl.when(tile == 0)
    def _():
        dk_s[...] = jnp.zeros_like(dk_s)
        dv_s[...] = jnp.zeros_like(dv_s)

    @pl.when(xsrc == 0)
    def _():
        dkw_ref[...] = jnp.zeros_like(dkw_ref)

    qcol = lax.broadcasted_iota(jnp.int32, (HALF, HALF), 1)
    krow = lax.broadcasted_iota(jnp.int32, (HALF, HALF), 0)

    def win(i):
        return pl.ds(pl.multiple_of(t0 + i * HALF, HALF), HALF)

    m = jnp.full((1, HALF), -jnp.inf, F32)
    l = jnp.zeros((1, HALF), F32)
    for i in reversed(range(nl)):
        s = nt(kw_ref[0, 0, win(i)], q)
        ok = krow + i * HALF >= first_valid
        if i == 0:
            ok &= krow // BLOCK >= qcol // BLOCK + 1
        if i == nl - 1:
            ok &= krow <= qcol
        s = jnp.where(ok, s, -jnp.inf)
        m_new = jnp.maximum(m, jnp.max(s, axis=0, keepdims=True))
        e = jnp.exp2((s - m_new) * cexp)
        e_l[i] = e
        l = l * jnp.exp2((m - m_new) * cexp) + jnp.sum(e, axis=0, keepdims=True)
        m_s[16 + i] = jnp.broadcast_to(m_new, (8, HALF))
        m = m_new

    limit = blk0 - LOCAL - res

    def score(i, carry, masked):
        m, l = carry
        s = nt(ks_ref[pl.ds(2 * i, 2)].reshape(CHUNK, 128), q)
        if masked:
            kr = lax.broadcasted_iota(jnp.int32, (CHUNK, HALF), 0)
            qc = lax.broadcasted_iota(jnp.int32, (CHUNK, HALF), 1)
            run = 2 * ((kr // BLOCK) % NX) + kr // (BLOCK * NX)
            s = jnp.where(64 * i + 8 * run <= limit + qc // BLOCK, s, -jnp.inf)
        m_new = jnp.maximum(m, jnp.max(s, axis=0, keepdims=True))
        e = jnp.exp2((s - m_new) * cexp)
        e_s[i] = e
        l = l * jnp.exp2((m - m_new) * cexp) + jnp.sum(e, axis=0, keepdims=True)
        m_s[i] = jnp.broadcast_to(m_new, (8, HALF))
        return m_new, l

    carry = lax.fori_loop(0, jnp.maximum(group - 1, 0), functools.partial(score, masked=False), (m, l))
    m, l = lax.fori_loop(jnp.maximum(group - 1, 0), n_chunk, functools.partial(score, masked=True), carry)
    inv = 1.0 / l

    def factor(slot):
        return jnp.exp2((m_s[slot][0:1] - m) * cexp) * inv

    ot = jnp.zeros((128, HALF), F32)
    for i in range(nl):
        pb = (e_l[i] * factor(16 + i)).astype(BF16)
        v = kw_ref[0, 1, win(i)]
        ot += tn(v, pb)
        dkw_ref[0, 1, win(i)] += nn(pb, do)
        dp_l[i] = nt(v, do)

    def value(i, ot):
        pb = (e_s[i] * factor(i)).astype(BF16)
        v = vs_ref[pl.ds(2 * i, 2)].reshape(CHUNK, 128)
        rows = pl.ds(pl.multiple_of(i * CHUNK, CHUNK), CHUNK)
        dv_s[rows] += nn(pb, do)
        dp_s[i] = nt(v, do)
        return ot + tn(v, pb)

    ot = lax.fori_loop(0, n_chunk, value, ot)
    delta = jnp.sum(ot * do.astype(F32).T, axis=0, keepdims=True)
    o_ref[0] = ot.T.astype(BF16)

    dqt = jnp.zeros((128, HALF), F32)
    for i in range(nl):
        p = e_l[i] * factor(16 + i)
        ds = (p * (dp_l[i] - delta)).astype(BF16)
        dqt += tn(kw_ref[0, 0, win(i)], ds)
        dkw_ref[0, 0, win(i)] += nn(ds, q) * scale

    def grad(i, dqt):
        p = e_s[i] * factor(i)
        ds = (p * (dp_s[i] - delta)).astype(BF16)
        rows = pl.ds(pl.multiple_of(i * CHUNK, CHUNK), CHUNK)
        dk_s[rows] += nn(ds, q)
        return dqt + tn(ks_ref[pl.ds(2 * i, 2)].reshape(CHUNK, 128), ds)

    dqt = lax.fori_loop(0, n_chunk, grad, dqt)
    dq_ref[0] = (dqt * scale).T.astype(BF16)

    @pl.when(tile == pl.num_programs(0) - 1)
    def _():
        dkv_ref[:, 0] = (dk_s[...] * scale).astype(BF16).reshape(32, NX, BLOCK, 128)
        dkv_ref[:, 1] = dv_s[...].astype(BF16).reshape(32, NX, BLOCK, 128)


def head_attention(info, q_r, do_r, k_str, v_str, kv_win, u):
    whole = pl.BlockSpec((32, NX, BLOCK, 128), lambda t, s: (0, 0, 0, 0), pipeline_mode=pl.Buffered(1))
    qspec = pl.BlockSpec((1, 1, HALF, 128), lambda t, s: (t, u, 0, 0))
    ospec = pl.BlockSpec((1, HALF, 128), lambda t, s: (t, 0, 0))
    wspec = pl.BlockSpec((1, 2, HALO + 4096, 128), lambda t, s: (t // NX, 0, 0, 0))
    nslot = (HALO + HALF) // HALF
    pairs = 2048 * 5400
    return pl.pallas_call(
        attn_kernel,
        grid_spec=pltpu.PrefetchScalarGridSpec(
            num_scalar_prefetch=1,
            grid=(8,),
            in_specs=[qspec, qspec, whole, whole, wspec],
            out_specs=[ospec, ospec,
                       pl.BlockSpec((32, 2, NX, BLOCK, 128), lambda t, s: (0, 0, 0, 0, 0)),
                       wspec],
            scratch_shapes=[
                pltpu.VMEM((16, CHUNK, HALF), F32),
                pltpu.VMEM((16, CHUNK, HALF), F32),
                pltpu.VMEM((16 + nslot, 8, HALF), F32),
                pltpu.VMEM((nslot, HALF, HALF), F32),
                pltpu.VMEM((nslot, HALF, HALF), F32),
                pltpu.VMEM((8192, 128), F32),
                pltpu.VMEM((8192, 128), F32),
            ],
        ),
        out_shape=[jax.ShapeDtypeStruct((8, HALF, 128), BF16),
                   jax.ShapeDtypeStruct((8, HALF, 128), BF16),
                   jax.ShapeDtypeStruct((32, 2, NX, BLOCK, 128), BF16),
                   jax.ShapeDtypeStruct(kv_win.shape, F32)],
        compiler_params=pltpu.CompilerParams(vmem_limit_bytes=62 * 1024 * 1024),
        cost_estimate=pl.CostEstimate(flops=pairs * 6 * 256, bytes_accessed=40 * 1024 * 1024, transcendentals=pairs),
        name='head_attention',
    )(info, q_r, do_r, k_str, v_str, kv_win)


def halo_pairs(i, back):
    pairs = []
    for g in range(15):
        for c in range(2):
            src, dst = g * 8 + 6 + c, (g + 1) * 8 + 2 * i + c
            pairs.append((dst, src) if back else (src, dst))
    return pairs


def solution(mesh):
    spec = P('dp', 'cp', None, None)

    def layer(q_rope, k_rope, values, d_out):
        me = lax.axis_index('cp')
        core, x, y, z = me % 2, (me // 2) % NX, (me // 8) % 4, me // 32
        half = jnp.where(z >= 2, 1, 0)
        zp = jnp.where(z >= 2, 3 - z, z)
        g_kv = x // 2
        a2a = functools.partial(lax.all_to_all, axis_name='cp', split_axis=0, concat_axis=0, tiled=True)

        def pack(a):
            a = a[0].reshape(2, HALF, NX, TRIPLE, 128)
            return a.transpose(0, 2, 3, 1, 4).reshape(8, TRIPLE, HALF, 128)

        kv = jnp.stack([k_rope[0], values[0]])
        kv = kv.transpose(2, 0, 1, 3)

        blocks = kv.reshape(2, 2, STRIDE, BLOCK, 128)
        sent = jnp.stack([jnp.stack([blocks[t // 2, :, residue(TRIPLE * t + u)] for u in range(TRIPLE)]) for t in range(NX)])
        mine = a2a(sent, axis_index_groups=GROUP_X)
        gathered = []
        for u in range(TRIPLE):
            gathered.append(lax.all_gather(mine[:, u].transpose(1, 0, 2, 3), 'cp', axis=1, axis_index_groups=GROUP_ZYC))

        q_r = a2a(pack(q_rope), axis_index_groups=GROUP_Q)
        do_r = a2a(pack(d_out), axis_index_groups=GROUP_Q)

        piece = jnp.zeros((2, 2, 128, 128), BF16)
        for i in range(NX):
            piece = piece + lax.ppermute(kv[:, :, i * 128:(i + 1) * 128], 'cp', halo_pairs(i, False))
        ext = jnp.concatenate([kv, piece], axis=2)
        keep = lax.dynamic_index_in_dim(ext, g_kv, axis=0, keepdims=False)
        got = lax.ppermute(lax.dynamic_index_in_dim(ext, 1 - g_kv, axis=0, keepdims=False), 'cp', [(d, d ^ 4) for d in range(128)])
        two = jnp.stack([jnp.where(g_kv == 0, keep, got), jnp.where(g_kv == 0, got, keep)])
        allw = lax.all_gather(two, 'cp', axis=0, axis_index_groups=GROUP_WG)
        sel = allw.reshape(2, 2, 2, 2, 2, 640, 128)
        body = sel[:, :, :, :, :, :RUN].transpose(0, 4, 3, 1, 2, 5, 6).reshape(2, 2, 4096, 128)
        head_part = sel[:, :, :, :, :, RUN:].transpose(0, 4, 2, 3, 1, 5, 6).reshape(2, 2, HALO, 128)
        kv_win = jnp.concatenate([head_part, body], axis=2)

        member = half * NX + x

        def swap(parts):
            got = []
            for k in range(8):
                part = lax.dynamic_index_in_dim(parts, member ^ k, axis=0, keepdims=False)
                if k:
                    part = lax.ppermute(part, 'cp', [(g[m], g[m ^ k]) for g in GROUP_Q for m in range(8)])
                got.append(part)
            return got

        outs = []
        str_sum = []
        win_sum = None
        for u in range(TRIPLE):
            res = (-1 - (TRIPLE * x + u)) % STRIDE
            info = jnp.stack([4 * zp + y, 4 * (3 - zp) + y, core, half, res, 0, 0, 0]).astype(jnp.int32)
            o, dq, dkv, dkw = head_attention(info, q_r, do_r, gathered[u][0], gathered[u][1], kv_win, u)
            outs.append(swap(jnp.stack([o, dq], axis=1)))
            back = a2a(dkv, axis_index_groups=GROUP_ZYC)
            str_sum.append(jnp.sum(back, axis=0, dtype=F32))
            win_sum = dkw if win_sum is None else win_sum + dkw

        both = jnp.stack([jnp.stack(o) for o in outs], axis=1)
        both = jnp.stack([lax.dynamic_index_in_dim(both, member ^ j, axis=0, keepdims=False) for j in range(8)])
        both = both.reshape(2, NX, TRIPLE, 2, HALF, 128).transpose(3, 0, 4, 1, 2, 5).reshape(2, RUN, 12, 128)

        body = win_sum[:, :, HALO:].reshape(2, 2, NX, 2, RUN, 128).transpose(0, 2, 3, 1, 4, 5)
        head_part = win_sum[:, :, :HALO].reshape(2, 2, 2, NX, 128, 128).transpose(0, 3, 2, 1, 4, 5)
        wsend = jnp.concatenate([body, head_part], axis=4).reshape(16, 2, 640, 128).astype(BF16)
        wgot = a2a(wsend, axis_index_groups=GROUP_W).reshape(2, 2, 2, 2, 2, 640, 128)
        wtot = jnp.sum(wgot, axis=(0, 2, 3), dtype=F32)
        grads = wtot[:, :, :RUN]
        pieces = [lax.ppermute(wtot[:, :, RUN:], 'cp', halo_pairs(i, True)) for i in range(NX)]
        grads = grads + jnp.concatenate(pieces, axis=2)

        home = a2a(jnp.stack(str_sum).transpose(2, 0, 1, 3, 4), axis_index_groups=GROUP_X)
        by_kv = []
        for g in range(2):
            slots = [jnp.zeros((2, BLOCK, 128), F32)] * STRIDE
            for h in range(6 * g, 6 * g + 6):
                slots[residue(h)] = home[h // TRIPLE, h % TRIPLE]
            by_kv.append(jnp.concatenate(slots, axis=1))
        grads = (grads + jnp.stack(by_kv)).astype(BF16)
        grads = grads.transpose(1, 2, 0, 3)
        return both[0][None], both[1][None], grads[0][None], grads[1][None]

    return jax.shard_map(layer, mesh=mesh, in_specs=(spec, spec, spec, spec), out_specs=(spec, spec, spec, spec), check_vma=False)
```

time: 2720 us -> 749 us (0.28)
  the two profiles are of different devices: /device:TPU:85 before, /device:TPU:30 now
where the time goes in v1:
time: 749 us; the launch traced here: 748 us
  Pallas kernels  309 us (41%)
  waiting for transfers between devices  222 us (30%)
  starting transfers between devices  111 us (15%)
  local copies, waits for them, and re-layouts  44.7 us (6%)
  other arithmetic  35.5 us (5%)
  between operations  14.6 us (2%)
  blocking collectives  10.6 us (1%)
    pallas_call x3, Pallas kernels, head_attention(): pl.pallas_call(attn_kernel, grid_spec=pltpu.PrefetchScalarGridSpec(num_sc...  309 us
    ppermute x21, waiting for transfers between devices, swap(): lax.ppermute(part, 'cp', [(g[m], g[m ^ k]) for g in GROUP_Q for m in rang...  96.1 us
    all_gather x1, waiting for transfers between devices, layer(): allw = lax.all_gather(two, 'cp', axis=0, axis_index_groups=GROUP_WG)  66.9 us
    ppermute x21, starting transfers between devices, swap(): lax.ppermute(part, 'cp', [(g[m], g[m ^ k]) for g in GROUP_Q for m in rang...  46.7 us
    all_gather x3, waiting for transfers between devices, layer(): lax.all_gather(mine[:, u].transpose(1, 0, 2, 3), 'cp', axis=1, axis_index...  27.4 us
    all_to_all x3, starting transfers between devices, layer(): back = a2a(dkv, axis_index_groups=GROUP_ZYC)  21.6 us
    ppermute x4, waiting for transfers between devices, layer(): lax.ppermute(wtot[:, :, RUN:], 'cp', halo_pairs(i, True))  20.2 us
    slice x3, local copies, waits for them, and re-layouts, layer(): gathered[u][1]  15.6 us
  transfers between devices with their start and end apart: 41, of which 15 were waited for; matrix products, arithmetic and copies ran while one was open for 9% of the time, Pallas kernels for 41%

profile of v1, /device:TPU:30, one launch (start us, length us, event | category | flops | bytes accessed | tf_op | source)
XLA Modules:
  0.0 747.8 jit_solution(1055415474335820957)
XLA Ops:
  9.4 10.6 %all_to_all.40 = bf16[4,3,2,64,128]{4,3,2,1,0:T(8,128)(2,1)S(1)} all-to-all(bf16[4,3,2,64,128]{4,3,2,1,0:T(8,128)(2,1)S(1)} %pad_maximum_fusion.4), channel_id=1, replica_groups={{0,2,4,6},{1,3,5,7},{8,10,12,14},{9,11,13,15},{16,18,20,22},{17,19,21,2..., dimensions={0} | all-to-all | bytes 786432 | tf_op jit(solution)/shard_map/all_to_all | solution.py:239
  20.8 5.1 collective-permute-start.1
  26.0 3.5 collective-permute-start.3
  34.7 8.7 %collective-permute-done.4 = bf16[2,640,128]{2,1,0:T(8,128)(2,1)S(1)} collective-permute-done((bf16[2,640,128]{2,1,0:T(8,128)(2,1)S(1)}, bf16[2,640,128]{2,1,0:T(8,128)(2,1)S(1)}, u32[]{:S(2)}, u32[]{:S(2)}) %collective-permute-start.4) | collective-permute-done | bytes 327712 | tf_op jit(solution)/shard_map/ppermute | solution.py:252
  46.5 7.4 all-to-all-start
  55.9 27.3 %all-gather.15.cloned.1.call-done = bf16[2,128,64,128]{3,2,0,1:T(8,128)(2,1)} async-done(((bf16[2,4,64,128]{3,2,0,1:T(8,128)(2,1)}), bf16[2,128,64,128]{3,2,0,1:T(8,128)(2,1)}) %all-gather.15.cloned.1.call-update) | async-done | bytes 4194320 | tf_op jit(solution)/shard_map/all_gather | solution.py:242
  83.2 5.1 fusion.57
  88.4 5.4 all-to-all-start.1
  93.8 66.9 %all-gather.11.cloned.1.call-done = bf16[16,2,640,128]{3,2,1,0:T(8,128)(2,1)} async-done(((bf16[2,2,640,128]{3,2,1,0:T(8,128)(2,1)}), bf16[16,2,640,128]{3,2,1,0:T(8,128)(2,1)}) %all-gather.11.cloned.1.call-update) | async-done | bytes 5242896 | tf_op jit(solution)/shard_map/all_gather | solution.py:254
  167.6 103.0 %head_attention.5 = (bf16[8,256,128]{2,1,0:T(8,128)(2,1)}, bf16[8,256,128]{2,1,0:T(8,128)(2,1)}, bf16[32,2,4,64,128]{4,3,2,1,0:T(8,128)(2,1)}, f32[2,2,5120,128]{3,2,1,0:T(8,128)}) custom-call(s32[8]{0:T(128)} %stack.269.info, bf16[8,3,256,128]{3,2,1,0:T(8,128)(2,1)} %copy-done.9, bf16[8,3,256,128]{3,2,1,0:T(8,128)(2,1)} %all-to-all-done.1.do_ref, ...), custom_call_target="tpu_custom_call" | custom-call | flops 16986931200 | bytes 41943040 | tf_op jit(solution)/shard_map/head_attention/pallas_call | solution.py:181
  270.7 7.2 all-to-all-start.6
  278.5 5.2 fusion.56
  283.7 102.9 %head_attention.4 = (bf16[8,256,128]{2,1,0:T(8,128)(2,1)}, bf16[8,256,128]{2,1,0:T(8,128)(2,1)}, bf16[32,2,4,64,128]{4,3,2,1,0:T(8,128)(2,1)}, f32[2,2,5120,128]{3,2,1,0:T(8,128)}) custom-call(s32[8]{0:T(128)} %stack.255.info, bf16[8,3,256,128]{3,2,1,0:T(8,128)(2,1)} %copy-done.9, bf16[8,3,256,128]{3,2,1,0:T(8,128)(2,1)} %all-to-all-done.1.do_ref, ...), custom_call_target="tpu_custom_call" | custom-call | flops 16986931200 | bytes 41943040 | tf_op jit(solution)/shard_map/head_attention/pallas_call | solution.py:181
  386.7 7.2 all-to-all-start.5
  394.6 5.2 fusion.55
  399.9 103.0 %head_attention.3 = (bf16[8,256,128]{2,1,0:T(8,128)(2,1)}, bf16[8,256,128]{2,1,0:T(8,128)(2,1)}, bf16[32,2,4,64,128]{4,3,2,1,0:T(8,128)(2,1)}, f32[2,2,5120,128]{3,2,1,0:T(8,128)}) custom-call(s32[8]{0:T(128)} %stack.228.info, bf16[8,3,256,128]{3,2,1,0:T(8,128)(2,1)} %copy-done.9, bf16[8,3,256,128]{3,2,1,0:T(8,128)(2,1)} %all-to-all-done.1.do_ref, ...), custom_call_target="tpu_custom_call" | custom-call | flops 16986931200 | bytes 41943040 | tf_op jit(solution)/shard_map/head_attention/pallas_call | solution.py:181
  502.9 7.1 all-to-all-start.4
  510.0 10.7 %add_convert_fusion = bf16[2,2,5120,128]{3,2,1,0:T(8,128)(2,1)S(1)} fusion(f32[2,2,5120,128]{3,2,1,0:T(8,128)} %get-tuple-element.24, f32[2,2,5120,128]{3,2,1,0:T(8,128)} %get-tuple-element.22, f32[2,2,5120,128]{3,2,1,0:T(8,128)} %get-tuple-element.23), kind=kLoop, calls=%fused_computation.1 | loop fusion | flops 7864320 | bytes 36700160 | tf_op jit(solution)/shard_map/convert.8
  523.2 6.5 collective-permute-start.24
  534.1 4.5 collective-permute-start.20
  547.5 5.0 collective-permute-done.21
  554.1 18.7 %collective-permute-done.22 = bf16[2,256,128]{2,1,0:T(8,128)(2,1)S(1)} collective-permute-done((bf16[2,256,128]{2,1,0:T(8,128)(2,1)S(1)}, bf16[2,256,128]{2,1,0:T(8,128)(2,1)S(1)}, u32[]{:S(2)}, u32[]{:S(2)}) %collective-permute-start.22) | collective-permute-done | bytes 131104 | tf_op jit(solution)/shard_map/ppermute | solution.py:267
  574.9 4.9 collective-permute-start.18
  582.3 3.5 convert_reduce_fusion.1
  593.2 5.9 all-to-all-start.7
  602.3 7.8 %collective-permute-done.14 = bf16[2,256,128]{2,1,0:T(8,128)(2,1)S(1)} collective-permute-done((bf16[2,256,128]{2,1,0:T(8,128)(2,1)}, bf16[2,256,128]{2,1,0:T(8,128)(2,1)S(1)}, u32[]{:S(2)}, u32[]{:S(2)}) %collective-permute-start.14) | collective-permute-done | bytes 131104 | tf_op jit(solution)/shard_map/ppermute | solution.py:267
  616.7 5.4 all-to-all-start.3
  628.7 3.4 collective-permute-start.6
  633.0 60.1 %collective-permute-done.5 = bf16[2,256,128]{2,1,0:T(8,128)(2,1)S(1)} collective-permute-done((bf16[2,256,128]{2,1,0:T(8,128)(2,1)}, bf16[2,256,128]{2,1,0:T(8,128)(2,1)S(1)}, u32[]{:S(2)}, u32[]{:S(2)}) %collective-permute-start.5) | collective-permute-done | bytes 131104 | tf_op jit(solution)/shard_map/ppermute | solution.py:267
  708.3 3.4 convert_reduce_fusion
  711.7 3.2 collective-permute-start.29
  718.9 20.2 %collective-permute-done.29 = f32[2,2,128,128]{3,2,1,0:T(8,128)S(1)} collective-permute-done((f32[2,2,128,128]{3,2,1,0:T(8,128)S(1)}, f32[2,2,128,128]{3,2,1,0:T(8,128)S(1)}, u32[]{:S(2)}, u32[]{:S(2)}) %collective-permute-start.29) | collective-permute-done | bytes 262176 | tf_op jit(solution)/shard_map/ppermute | solution.py:293
  (177 shorter events, 88.8 us)
Async XLA Ops:
  7.2 76.1 %all-gather.15.cloned.1.call-start = ((), (), s32[]{:S(2)}) async-start(), calls=%async_computation.11 | async-start | bytes 4325376 | tf_op jit(solution)/shard_map/all_gather | solution.py:242
  20.7 140.0 %all-gather.11.cloned.1.call-start = ((), (), s32[]{:S(2)}) async-start(), calls=%async_computation.9 | async-start | bytes 5898240 | tf_op jit(solution)/shard_map/all_gather | solution.py:254
  44.5 234.0 %all-gather.13.cloned.1.call-start = ((), (), s32[]{:S(2)}) async-start(), calls=%async_computation.10 | async-start | bytes 4325376 | tf_op jit(solution)/shard_map/all_gather | solution.py:242
  46.5 41.9 %all-to-all-start = ((bf16[8,3,256,128]{3,2,1,0:T(8,128)(2,1)}), bf16[8,3,256,128]{3,2,1,0:T(8,128)(2,1)S(1)}, u32[]{:S(2)}, u32[]{:S(2)}) async-start(bf16[8,3,256,128]{3,2,1,0:T(8,128)(2,1)} %bitcast.7), calls=%async_computation | async-start | bytes 3145728 | tf_op jit(solution)/shard_map/all_to_all | solution.py:244
  54.0 340.7 %all-gather.9.cloned.1.call-start = ((), (), s32[]{:S(2)}) async-start(), calls=%async_computation.8 | async-start | bytes 4325376 | tf_op jit(solution)/shard_map/all_gather | solution.py:242
  88.4 79.3 %all-to-all-start.1 = ((bf16[8,3,256,128]{3,2,1,0:T(8,128)(2,1)}), bf16[8,3,256,128]{3,2,1,0:T(8,128)(2,1)}, u32[]{:S(2)}, u32[]{:S(2)}) async-start(bf16[8,3,256,128]{3,2,1,0:T(8,128)(2,1)} %bitcast.10), calls=%async_computation.1 | async-start | bytes 3145728 | tf_op jit(solution)/shard_map/all_to_all | solution.py:245
  270.7 116.0 %all-to-all-start.6 = ((bf16[32,2,4,64,128]{4,3,2,1,0:T(8,128)(2,1)}), bf16[32,2,4,64,128]{4,3,2,1,0:T(8,128)(2,1)}, u32[]{:S(2)}, u32[]{:S(2)}) async-start(bf16[32,2,4,64,128]{4,3,2,1,0:T(8,128)(2,1)} %get-tuple-element.27), calls=%async_computation.6 | async-start | bytes 8388608 | tf_op jit(solution)/shard_map/all_to_all | solution.py:279
  386.7 116.2 %all-to-all-start.5 = ((bf16[32,2,4,64,128]{4,3,2,1,0:T(8,128)(2,1)}), bf16[32,2,4,64,128]{4,3,2,1,0:T(8,128)(2,1)}, u32[]{:S(2)}, u32[]{:S(2)}) async-start(bf16[32,2,4,64,128]{4,3,2,1,0:T(8,128)(2,1)} %get-tuple-element.26), calls=%async_computation.5 | async-start | bytes 8388608 | tf_op jit(solution)/shard_map/all_to_all | solution.py:279
  502.9 86.2 %all-to-all-start.4 = ((bf16[32,2,4,64,128]{4,3,2,1,0:T(8,128)(2,1)}), bf16[32,2,4,64,128]{4,3,2,1,0:T(8,128)(2,1)}, u32[]{:S(2)}, u32[]{:S(2)}) async-start(bf16[32,2,4,64,128]{4,3,2,1,0:T(8,128)(2,1)} %get-tuple-element.25), calls=%async_computation.4 | async-start | bytes 8388608 | tf_op jit(solution)/shard_map/all_to_all | solution.py:279
  523.2 56.7 %collective-permute-start.24 = (bf16[2,256,128]{2,1,0:T(8,128)(2,1)S(1)}, bf16[2,256,128]{2,1,0:T(8,128)(2,1)S(1)}, u32[]{:S(2)}, u32[]{:S(2)}) collective-permute-start(bf16[2,256,128]{2,1,0:T(8,128)(2,1)S(1)} %get-tuple-element.66), channel_id=1, source_target_pairs={{0,100},{2,102},{4,96},{6,98},{96,4},{98,6},{100,0},{102,2},{1,101... | collective-permute-start | bytes 393224 | tf_op jit(solution)/shard_map/ppermute | solution.py:267
  529.7 45.2 %collective-permute-start.23 = (bf16[2,256,128]{2,1,0:T(8,128)(2,1)S(1)}, bf16[2,256,128]{2,1,0:T(8,128)(2,1)S(1)}, u32[]{:S(2)}, u32[]{:S(2)}) collective-permute-start(bf16[2,256,128]{2,1,0:T(8,128)(2,1)S(1)} %get-tuple-element.67), channel_id=1, source_target_pairs={{0,98},{2,96},{4,102},{6,100},{96,2},{98,0},{100,6},{102,4},{1,99}... | collective-permute-start | bytes 393224 | tf_op jit(solution)/shard_map/ppermute | solution.py:267
  531.6 50.3 %collective-permute-start.25 = (bf16[2,256,128]{2,1,0:T(8,128)(2,1)S(1)}, bf16[2,256,128]{2,1,0:T(8,128)(2,1)S(1)}, u32[]{:S(2)}, u32[]{:S(2)}) collective-permute-start(bf16[2,256,128]{2,1,0:T(8,128)(2,1)S(1)} %get-tuple-element.60), channel_id=1, source_target_pairs={{0,102},{2,100},{4,98},{6,96},{96,6},{98,4},{100,2},{102,0},{1,103... | collective-permute-start | bytes 393224 | tf_op jit(solution)/shard_map/ppermute | solution.py:267
  531.8 14.5 %collective-permute-start.19 = (bf16[2,256,128]{2,1,0:T(8,128)(2,1)S(1)}, bf16[2,256,128]{2,1,0:T(8,128)(2,1)S(1)}, u32[]{:S(2)}, u32[]{:S(2)}) collective-permute-start(bf16[2,256,128]{2,1,0:T(8,128)(2,1)S(1)} %get-tuple-element.62), channel_id=1, source_target_pairs={{0,2},{2,0},{4,6},{6,4},{96,98},{98,96},{100,102},{102,100},{1,3},... | collective-permute-start | bytes 393224 | tf_op jit(solution)/shard_map/ppermute | solution.py:267
  534.1 13.1 %collective-permute-start.20 = (bf16[2,256,128]{2,1,0:T(8,128)(2,1)S(1)}, bf16[2,256,128]{2,1,0:T(8,128)(2,1)S(1)}, u32[]{:S(2)}, u32[]{:S(2)}) collective-permute-start(bf16[2,256,128]{2,1,0:T(8,128)(2,1)S(1)} %get-tuple-element.63), channel_id=1, source_target_pairs={{0,4},{2,6},{4,0},{6,2},{96,100},{98,102},{100,96},{102,98},{1,5},... | collective-permute-start | bytes 393224 | tf_op jit(solution)/shard_map/ppermute | solution.py:267
  547.2 25.6 %collective-permute-start.22 = (bf16[2,256,128]{2,1,0:T(8,128)(2,1)S(1)}, bf16[2,256,128]{2,1,0:T(8,128)(2,1)S(1)}, u32[]{:S(2)}, u32[]{:S(2)}) collective-permute-start(bf16[2,256,128]{2,1,0:T(8,128)(2,1)S(1)} %get-tuple-element.65), channel_id=1, source_target_pairs={{0,96},{2,98},{4,100},{6,102},{96,0},{98,2},{100,4},{102,6},{1,97}... | collective-permute-start | bytes 393224 | tf_op jit(solution)/shard_map/ppermute | solution.py:267
  552.5 74.3 %collective-permute-start.17 = (bf16[2,256,128]{2,1,0:T(8,128)(2,1)}, bf16[2,256,128]{2,1,0:T(8,128)(2,1)}, u32[]{:S(2)}, u32[]{:S(2)}) collective-permute-start(bf16[2,256,128]{2,1,0:T(8,128)(2,1)} %get-tuple-element.58), channel_id=1, source_target_pairs={{0,100},{2,102},{4,96},{6,98},{96,4},{98,6},{100,0},{102,2},{1,101... | collective-permute-start | bytes 393224 | tf_op jit(solution)/shard_map/ppermute | solution.py:267
  572.8 50.4 %collective-permute-start.16 = (bf16[2,256,128]{2,1,0:T(8,128)(2,1)}, bf16[2,256,128]{2,1,0:T(8,128)(2,1)}, u32[]{:S(2)}, u32[]{:S(2)}) collective-permute-start(bf16[2,256,128]{2,1,0:T(8,128)(2,1)} %get-tuple-element.59), channel_id=1, source_target_pairs={{0,98},{2,96},{4,102},{6,100},{96,2},{98,0},{100,6},{102,4},{1,99}... | collective-permute-start | bytes 393224 | tf_op jit(solution)/shard_map/ppermute | solution.py:267
  574.9 53.8 %collective-permute-start.18 = (bf16[2,256,128]{2,1,0:T(8,128)(2,1)}, bf16[2,256,128]{2,1,0:T(8,128)(2,1)}, u32[]{:S(2)}, u32[]{:S(2)}) collective-permute-start(bf16[2,256,128]{2,1,0:T(8,128)(2,1)} %get-tuple-element.52), channel_id=1, source_target_pairs={{0,102},{2,100},{4,98},{6,96},{96,6},{98,4},{100,2},{102,0},{1,103... | collective-permute-start | bytes 393224 | tf_op jit(solution)/shard_map/ppermute | solution.py:267
  579.8 19.3 %collective-permute-start.12 = (bf16[2,256,128]{2,1,0:T(8,128)(2,1)}, bf16[2,256,128]{2,1,0:T(8,128)(2,1)}, u32[]{:S(2)}, u32[]{:S(2)}) collective-permute-start(bf16[2,256,128]{2,1,0:T(8,128)(2,1)} %get-tuple-element.54), channel_id=1, source_target_pairs={{0,2},{2,0},{4,6},{6,4},{96,98},{98,96},{100,102},{102,100},{1,3},... | collective-permute-start | bytes 393224 | tf_op jit(solution)/shard_map/ppermute | solution.py:267
  581.9 18.2 %collective-permute-start.13 = (bf16[2,256,128]{2,1,0:T(8,128)(2,1)}, bf16[2,256,128]{2,1,0:T(8,128)(2,1)}, u32[]{:S(2)}, u32[]{:S(2)}) collective-permute-start(bf16[2,256,128]{2,1,0:T(8,128)(2,1)} %get-tuple-element.55), channel_id=1, source_target_pairs={{0,4},{2,6},{4,0},{6,2},{96,100},{98,102},{100,96},{102,98},{1,5},... | collective-permute-start | bytes 393224 | tf_op jit(solution)/shard_map/ppermute | solution.py:267
  593.2 23.5 %all-to-all-start.7 = ((f32[4,3,2,64,128]{4,3,2,1,0:T(8,128)}), f32[4,3,2,64,128]{4,3,2,1,0:T(8,128)S(1)}, u32[]{:S(2)}, u32[]{:S(2)}) async-start(f32[4,3,2,64,128]{4,3,2,1,0:T(8,128)} %maximum_bitcast_fusion), calls=%async_computation.7 | async-start | bytes 1572864 | tf_op jit(solution)/shard_map/all_to_all | solution.py:296
  600.2 13.2 %collective-permute-start.15 = (bf16[2,256,128]{2,1,0:T(8,128)(2,1)}, bf16[2,256,128]{2,1,0:T(8,128)(2,1)S(1)}, u32[]{:S(2)}, u32[]{:S(2)}) collective-permute-start(bf16[2,256,128]{2,1,0:T(8,128)(2,1)} %get-tuple-element.57), channel_id=1, source_target_pairs={{0,96},{2,98},{4,100},{6,102},{96,0},{98,2},{100,4},{102,6},{1,97}... | collective-permute-start | bytes 393224 | tf_op jit(solution)/shard_map/ppermute | solution.py:267
  610.1 93.2 %collective-permute-start.10 = (bf16[2,256,128]{2,1,0:T(8,128)(2,1)S(1)}, bf16[2,256,128]{2,1,0:T(8,128)(2,1)}, u32[]{:S(2)}, u32[]{:S(2)}) collective-permute-start(bf16[2,256,128]{2,1,0:T(8,128)(2,1)S(1)} %get-tuple-element.50), channel_id=1, source_target_pairs={{0,100},{2,102},{4,96},{6,98},{96,4},{98,6},{100,0},{102,2},{1,101... | collective-permute-start | bytes 393224 | tf_op jit(solution)/shard_map/ppermute | solution.py:267
  614.0 88.4 %collective-permute-start.9 = (bf16[2,256,128]{2,1,0:T(8,128)(2,1)}, bf16[2,256,128]{2,1,0:T(8,128)(2,1)}, u32[]{:S(2)}, u32[]{:S(2)}) collective-permute-start(bf16[2,256,128]{2,1,0:T(8,128)(2,1)} %get-tuple-element.51), channel_id=1, source_target_pairs={{0,98},{2,96},{4,102},{6,100},{96,2},{98,0},{100,6},{102,4},{1,99}... | collective-permute-start | bytes 393224 | tf_op jit(solution)/shard_map/ppermute | solution.py:267
  616.7 91.5 %all-to-all-start.3 = ((bf16[16,2,640,128]{3,2,1,0:T(8,128)(2,1)}), bf16[16,2,640,128]{3,2,1,0:T(8,128)(2,1)}, u32[]{:S(2)}, u32[]{:S(2)}) async-start(bf16[16,2,640,128]{3,2,1,0:T(8,128)(2,1)} %bitcast.284), calls=%async_computation.3 | async-start | bytes 10485760 | tf_op jit(solution)/shard_map/all_to_all | solution.py:290
  623.1 81.1 %collective-permute-start.11 = (bf16[2,256,128]{2,1,0:T(8,128)(2,1)}, bf16[2,256,128]{2,1,0:T(8,128)(2,1)S(1)}, u32[]{:S(2)}, u32[]{:S(2)}) collective-permute-start(bf16[2,256,128]{2,1,0:T(8,128)(2,1)} %get-tuple-element.44), channel_id=1, source_target_pairs={{0,102},{2,100},{4,98},{6,96},{96,6},{98,4},{100,2},{102,0},{1,103... | collective-permute-start | bytes 393224 | tf_op jit(solution)/shard_map/ppermute | solution.py:267
  626.8 66.2 %collective-permute-start.5 = (bf16[2,256,128]{2,1,0:T(8,128)(2,1)}, bf16[2,256,128]{2,1,0:T(8,128)(2,1)S(1)}, u32[]{:S(2)}, u32[]{:S(2)}) collective-permute-start(bf16[2,256,128]{2,1,0:T(8,128)(2,1)} %get-tuple-element.46), channel_id=1, source_target_pairs={{0,2},{2,0},{4,6},{6,4},{96,98},{98,96},{100,102},{102,100},{1,3},... | collective-permute-start | bytes 393224 | tf_op jit(solution)/shard_map/ppermute | solution.py:267
  628.7 66.9 %collective-permute-start.6 = (bf16[2,256,128]{2,1,0:T(8,128)(2,1)}, bf16[2,256,128]{2,1,0:T(8,128)(2,1)S(1)}, u32[]{:S(2)}, u32[]{:S(2)}) collective-permute-start(bf16[2,256,128]{2,1,0:T(8,128)(2,1)} %get-tuple-element.47), channel_id=1, source_target_pairs={{0,4},{2,6},{4,0},{6,2},{96,100},{98,102},{100,96},{102,98},{1,5},... | collective-permute-start | bytes 393224 | tf_op jit(solution)/shard_map/ppermute | solution.py:267
  711.7 27.4 %collective-permute-start.29 = (f32[2,2,128,128]{3,2,1,0:T(8,128)S(1)}, f32[2,2,128,128]{3,2,1,0:T(8,128)S(1)}, u32[]{:S(2)}, u32[]{:S(2)}) collective-permute-start(f32[2,2,128,128]{3,2,1,0:T(8,128)S(1)} %slice.239), channel_id=1, source_target_pairs={{14,6},{15,7},{22,14},{23,15},{30,22},{31,23},{38,30},{39,31},{46,... | collective-permute-start | bytes 786440 | tf_op jit(solution)/shard_map/ppermute | solution.py:293
  714.9 24.1 %collective-permute-start.28 = (f32[2,2,128,128]{3,2,1,0:T(8,128)S(1)}, f32[2,2,128,128]{3,2,1,0:T(8,128)S(1)}, u32[]{:S(2)}, u32[]{:S(2)}) collective-permute-start(f32[2,2,128,128]{3,2,1,0:T(8,128)S(1)} %slice.239), channel_id=1, source_target_pairs={{12,6},{13,7},{20,14},{21,15},{28,22},{29,23},{36,30},{37,31},{44,... | collective-permute-start | bytes 786440 | tf_op jit(solution)/shard_map/ppermute | solution.py:293
  716.2 22.8 %collective-permute-start.27 = (f32[2,2,128,128]{3,2,1,0:T(8,128)S(1)}, f32[2,2,128,128]{3,2,1,0:T(8,128)S(1)}, u32[]{:S(2)}, u32[]{:S(2)}) collective-permute-start(f32[2,2,128,128]{3,2,1,0:T(8,128)S(1)} %slice.239), channel_id=1, source_target_pairs={{10,6},{11,7},{18,14},{19,15},{26,22},{27,23},{34,30},{35,31},{42,... | collective-permute-start | bytes 786440 | tf_op jit(solution)/shard_map/ppermute | solution.py:293
  717.5 21.6 %collective-permute-start.26 = (f32[2,2,128,128]{3,2,1,0:T(8,128)S(1)}, f32[2,2,128,128]{3,2,1,0:T(8,128)S(1)}, u32[]{:S(2)}, u32[]{:S(2)}) collective-permute-start(f32[2,2,128,128]{3,2,1,0:T(8,128)S(1)} %slice.239), channel_id=1, source_target_pairs={{8,6},{9,7},{16,14},{17,15},{24,22},{25,23},{32,30},{33,31},{40,38... | collective-permute-start | bytes 786440 | tf_op jit(solution)/shard_map/ppermute | solution.py:293
  (23 other events, 278.6 us)
Sparse Core Ops, SparseCore 0:
  20.9 62.3 all-gather.14
  84.9 75.8 all-gather.10
  163.0 49.2 all-gather.12
  215.0 45.5 all-gather.8

commit v2 on v1

v2 whole, which is shorter than its diff:
```python
import functools
import math

import jax
import jax.numpy as jnp
from jax import lax
from jax.experimental import pallas as pl
from jax.experimental.pallas import tpu as pltpu
from jax.sharding import PartitionSpec as P


BLOCK = 64
LOCAL = 16
STRIDE = 8
NX = 4
TRIPLE = 3
HALF = 256
RUN = 512
HALO = 1024
PER = 4
CHUNK = 512 * PER
SUBG = 1
SUB = 512 * SUBG
WIN = (LOCAL - 1) * BLOCK + HALF
WSUB = ((0, 7), (7, 13), (13, 19))
F32 = jnp.float32
BF16 = jnp.bfloat16


def dev(z, y, x, c):
    return ((z * 4 + y) * NX + x) * 2 + c


def zof(zp, zm):
    return zp if zm == 0 else 3 - zp


GROUP_Q = [[dev(zof(zp, zm), y, x, c) for zm in range(2) for x in range(NX)] for zp in range(2) for y in range(4) for c in range(2)]
GROUP_X = [[dev(z, y, x, c) for x in range(NX)] for z in range(4) for y in range(4) for c in range(2)]
GROUP_ZYC = [[dev(z, y, x, c) for z in range(4) for y in range(4) for c in range(2)] for x in range(NX)]
GROUP_WG = [[dev(zof(zp, zm), y, 2 * xh + xl, c) for zm in range(2) for xl in range(2)] for zp in range(2) for y in range(4) for xh in range(2) for c in range(2)]


def residue(head):
    return (-1 - head) % STRIDE


def nt(a, b):
    return lax.dot_general(a, b, (((1,), (1,)), ((), ())), preferred_element_type=F32)


def tn(a, b):
    return lax.dot_general(a, b, (((0,), (0,)), ((), ())), preferred_element_type=F32)


def nn(a, b):
    return lax.dot_general(a, b, (((1,), (0,)), ((), ())), preferred_element_type=F32)


def attn_kernel(chained, info, q_ref, do_ref, ks_ref, vs_ref, kw_ref, *refs):
    prev_ref = refs[0] if chained else None
    oq_ref, dkv_ref, dkw_ref, e_s, dp_s, m_s, e_l, dp_l, dk_s, dv_s = refs[chained:]
    tile = pl.program_id(0)
    member = tile // NX
    xsrc = tile % NX
    scale = 1.0 / 128
    cexp = scale * math.log2(math.e)
    group = info[member]
    core = info[2]
    half = info[3]
    res = info[4]
    t0 = RUN * (2 * xsrc + core) + HALF * half
    blk0 = group * 64 + t0 // BLOCK
    q = q_ref[0, 0]
    do = do_ref[0, 0]

    @pl.when(tile == 0)
    def _():
        dk_s[...] = jnp.zeros_like(dk_s)
        dv_s[...] = jnp.zeros_like(dv_s)

    @pl.when(xsrc == 0)
    def _():
        if chained:
            pltpu.sync_copy(prev_ref.at[member], dkw_ref.at[0])
        else:
            dkw_ref[...] = jnp.zeros_like(dkw_ref)

    qblk = lax.broadcasted_iota(jnp.int32, (1, HALF), 1) // BLOCK

    def mask_slots(s, masks):
        return jnp.concatenate([jnp.where(mk, s[BLOCK * i:BLOCK * (i + 1)], -jnp.inf) for i, mk in enumerate(masks)], axis=0)

    def stats(s, dp, m, l, d):
        m_new = jnp.maximum(m, jnp.max(s, axis=0, keepdims=True))
        e = jnp.exp2((s - m_new) * cexp)
        a = jnp.exp2((m - m_new) * cexp)
        l = l * a + jnp.sum(e, axis=0, keepdims=True)
        d = d * a + jnp.sum(e * dp, axis=0, keepdims=True)
        return e, m_new, l, d

    nb = WIN // BLOCK
    masks = [(qblk <= min(i, 4)) & (blk0 - (LOCAL - 1) + i >= 0) for i in range(nb)]
    kr = lax.broadcasted_iota(jnp.int32, (HALF, HALF), 0)
    qc = lax.broadcasted_iota(jnp.int32, (HALF, HALF), 1)
    m, l, d = jnp.full((1, HALF), -jnp.inf, F32), jnp.zeros((1, HALF), F32), jnp.zeros((1, HALF), F32)
    m_l = []
    for lo, hi in reversed(WSUB):
        rows = pl.ds(pl.multiple_of(t0 + BLOCK * (lo + 1), BLOCK), BLOCK * (hi - lo))
        s = nt(kw_ref[0, 0, rows], q)
        dp = nt(kw_ref[0, 1, rows], do)
        if hi == nb:
            cut = BLOCK * (hi - lo) - HALF
            s = jnp.concatenate([mask_slots(s[:cut], masks[lo:hi - 4]), jnp.where(kr <= qc, s[cut:], -jnp.inf)], axis=0)
        else:
            s = mask_slots(s, masks[lo:hi])
        e, m, l, d = stats(s, dp, m, l, d)
        e_l[BLOCK * lo:BLOCK * hi] = e
        dp_l[BLOCK * lo:BLOCK * hi] = dp
        m_l.append(m)
    m_l.reverse()

    limit = blk0 - LOCAL - res

    def keys(ref, i):
        return ref[pl.ds(2 * PER * i, 2 * PER), 0].reshape(CHUNK, 128)

    def part(ref, i, n):
        return ref[pl.ds(2 * PER * i + 2 * SUBG * n, 2 * SUBG), 0].reshape(SUB, 128)

    def score(i, carry, masked):
        m, l, d = carry
        for n in range(PER // SUBG):
            s = nt(part(ks_ref, i, n), q)
            dp = nt(part(vs_ref, i, n), do)
            if masked:
                first = [64 * (PER * i + SUBG * n + b // 8) + 8 * (2 * (b % NX) + b % 8 // NX) for b in range(SUB // BLOCK)]
                s = mask_slots(s, [qblk >= f - limit for f in first])
            e, m, l, d = stats(s, dp, m, l, d)
            e_s[i, n] = e
            dp_s[i, n] = dp
            m_s[i, n] = jnp.broadcast_to(m, (8, HALF))
        return m, l, d

    n_open = jnp.maximum(group - 1, 0) // PER
    n_all = (group + PER) // PER
    carry = lax.fori_loop(0, n_open, functools.partial(score, masked=False), (m, l, d))
    m, l, d = lax.fori_loop(n_open, n_all, functools.partial(score, masked=True), carry)
    inv = 1.0 / l
    delta = d * inv

    def weights(e, dp, m_old):
        p = e * (jnp.exp2((m_old - m) * cexp) * inv)
        return p.astype(BF16), (p * (dp - delta)).astype(BF16)

    win = pl.ds(pl.multiple_of(t0 + BLOCK, BLOCK), WIN)
    pairs = [weights(e_l[BLOCK * lo:BLOCK * hi], dp_l[BLOCK * lo:BLOCK * hi], m_l[n]) for n, (lo, hi) in enumerate(WSUB)]
    pb = jnp.concatenate([p for p, _ in pairs], axis=0)
    ds = jnp.concatenate([g for _, g in pairs], axis=0)
    ot = tn(kw_ref[0, 1, win], pb)
    dqt = tn(kw_ref[0, 0, win], ds)
    dkw_ref[0, 1, win] += nn(pb, do)
    dkw_ref[0, 0, win] += nn(ds, q) * scale

    def grad(i, carry):
        ot, dqt = carry
        pairs = [weights(e_s[i, n], dp_s[i, n], m_s[i, n][0:1]) for n in range(PER // SUBG)]
        pb = jnp.concatenate([p for p, _ in pairs], axis=0)
        ds = jnp.concatenate([g for _, g in pairs], axis=0)
        rows = pl.ds(pl.multiple_of(i * CHUNK, CHUNK), CHUNK)
        dv_s[rows] += nn(pb, do)
        dk_s[rows] += nn(ds, q)
        return ot + tn(keys(vs_ref, i), pb), dqt + tn(keys(ks_ref, i), ds)

    ot, dqt = lax.fori_loop(0, n_all, grad, (ot, dqt))
    oq_ref[0, 0] = ot.T.astype(BF16)
    oq_ref[0, 1] = (dqt * scale).T.astype(BF16)

    @pl.when(tile == pl.num_programs(0) - 1)
    def _():
        dkv_ref[:, 0] = (dk_s[...] * scale).astype(BF16).reshape(32, NX, BLOCK, 128)
        dkv_ref[:, 1] = dv_s[...].astype(BF16).reshape(32, NX, BLOCK, 128)


def head_attention(info, qd_r, kv_str, kv_win, prev, u):
    def whole(n):
        return pl.BlockSpec((32, 1, NX, BLOCK, 128), lambda t, s: (0, n, 0, 0, 0), pipeline_mode=pl.Buffered(1))

    def qspec(n):
        return pl.BlockSpec((1, 1, HALF, 128), lambda t, s: (t, n, 0, 0))

    wspec = pl.BlockSpec((1, 2, HALO + 4096, 128), lambda t, s: (t // NX, 0, 0, 0))
    pairs = 2048 * 5400
    chained = prev is not None
    return pl.pallas_call(
        functools.partial(attn_kernel, chained),
        grid_spec=pltpu.PrefetchScalarGridSpec(
            num_scalar_prefetch=1,
            grid=(8,),
            in_specs=[qspec(u), qspec(TRIPLE + u), whole(0), whole(1), wspec] + [pl.BlockSpec(memory_space=pl.ANY)] * chained,
            out_specs=[pl.BlockSpec((1, 2, HALF, 128), lambda t, s: (t ^ s[5], 0, 0, 0)),
                       pl.BlockSpec((32, 2, NX, BLOCK, 128), lambda t, s: (0, 0, 0, 0, 0)),
                       wspec],
            scratch_shapes=[
                pltpu.VMEM((16 // PER, PER // SUBG, SUB, HALF), F32),
                pltpu.VMEM((16 // PER, PER // SUBG, SUB, HALF), F32),
                pltpu.VMEM((16 // PER, PER // SUBG, 8, HALF), F32),
                pltpu.VMEM((WIN, HALF), F32),
                pltpu.VMEM((WIN, HALF), F32),
                pltpu.VMEM((8192, 128), F32),
                pltpu.VMEM((8192, 128), F32),
            ],
        ),
        out_shape=[jax.ShapeDtypeStruct((8, 2, HALF, 128), BF16),
                   jax.ShapeDtypeStruct((32, 2, NX, BLOCK, 128), BF16),
                   jax.ShapeDtypeStruct(kv_win.shape, F32)],
        compiler_params=pltpu.CompilerParams(vmem_limit_bytes=62 * 1024 * 1024),
        cost_estimate=pl.CostEstimate(flops=pairs * 6 * 256, bytes_accessed=40 * 1024 * 1024, transcendentals=pairs),
        name='head_attention',
    )(info, qd_r, qd_r, kv_str, kv_str, kv_win, *([prev] if chained else []))


def halo_pairs(i, back):
    pairs = []
    for g in range(15):
        for c in range(2):
            src, dst = g * 8 + 6 + c, (g + 1) * 8 + 2 * i + c
            pairs.append((dst, src) if back else (src, dst))
    return pairs


def solution(mesh):
    spec = P('dp', 'cp', None, None)

    def layer(q_rope, k_rope, values, d_out):
        me = lax.axis_index('cp')
        core, x, y, z = me % 2, (me // 2) % NX, (me // 8) % 4, me // 32
        half = jnp.where(z >= 2, 1, 0)
        zp = jnp.where(z >= 2, 3 - z, z)
        g_kv = x // 2
        a2a = functools.partial(lax.all_to_all, axis_name='cp', split_axis=0, concat_axis=0, tiled=True)

        mate = [(d, d ^ 1) for d in range(128)]

        def pack(a):
            a = a[0].reshape(2, HALF, NX, TRIPLE, 128)
            return a.transpose(0, 2, 3, 1, 4).reshape(8, TRIPLE, HALF, 128)

        kv = jnp.stack([k_rope[0], values[0]])
        kv = kv.transpose(2, 0, 1, 3)

        blocks = kv.reshape(2, 2, STRIDE, BLOCK, 128)
        sent = jnp.stack([jnp.stack([blocks[t // 2, :, residue(TRIPLE * t + u)] for u in range(TRIPLE)]) for t in range(NX)])
        mine = a2a(sent, axis_index_groups=GROUP_X)
        mate = [(dev_id, dev_id ^ 1) for dev_id in range(128)]

        gathered = []
        for u in range(TRIPLE):
            gathered.append(lax.all_gather(mine[:, u].transpose(1, 0, 2, 3), 'cp', axis=0, axis_index_groups=GROUP_ZYC))

        qd_r = a2a(jnp.concatenate([pack(q_rope), pack(d_out)], axis=1), axis_index_groups=GROUP_Q)

        piece = jnp.zeros((2, 2, 128, 128), BF16)
        for i in range(NX):
            piece = piece + lax.ppermute(kv[:, :, i * 128:(i + 1) * 128], 'cp', halo_pairs(i, False))
        ext = jnp.concatenate([kv, piece], axis=2)
        keep = lax.dynamic_index_in_dim(ext, g_kv, axis=0, keepdims=False)
        got = lax.ppermute(lax.dynamic_index_in_dim(ext, 1 - g_kv, axis=0, keepdims=False), 'cp', [(d, d ^ 4) for d in range(128)])
        two = jnp.stack([jnp.where(g_kv == 0, keep, got), jnp.where(g_kv == 0, got, keep)])
        spot = half * 2 + x % 2
        allw = jnp.stack([two] + [lax.ppermute(two, 'cp', [(g[m], g[m ^ k]) for g in GROUP_WG for m in range(4)]) for k in range(1, 4)])
        allw = jnp.stack([lax.dynamic_index_in_dim(allw, spot ^ j, axis=0, keepdims=False) for j in range(4)])
        mate_w = lax.ppermute(allw, 'cp', mate)
        sel = jnp.stack([jnp.where(core == 0, allw, mate_w), jnp.where(core == 0, mate_w, allw)], axis=1)
        sel = sel.reshape(2, 2, 2, 2, 2, 640, 128)
        body = sel[:, :, :, :, :, :RUN].transpose(0, 4, 3, 1, 2, 5, 6).reshape(2, 2, 4096, 128)
        head_part = sel[:, :, :, :, :, RUN:].transpose(0, 4, 2, 3, 1, 5, 6).reshape(2, 2, HALO, 128)
        kv_win = jnp.concatenate([head_part, body], axis=2)

        member = half * NX + x

        def swap(parts):
            return [parts[0]] + [lax.ppermute(parts[k], 'cp', [(g[m], g[m ^ k]) for g in GROUP_Q for m in range(8)]) for k in range(1, 8)]

        outs = []
        str_sum = []
        dkw = None
        for u in range(TRIPLE):
            res = (-1 - (TRIPLE * x + u)) % STRIDE
            info = jnp.stack([4 * zp + y, 4 * (3 - zp) + y, core, half, res, member, 0, 0]).astype(jnp.int32)
            oq, dkv, dkw = head_attention(info, qd_r, gathered[u], kv_win, dkw, u)
            back = a2a(dkv, axis_index_groups=GROUP_ZYC)
            str_sum.append(jnp.sum(back, axis=0, dtype=F32))
            outs.append(oq)

        first = swap([jnp.stack([outs[0][k], outs[1][k]]) for k in range(8)])
        last = swap([outs[2][k] for k in range(8)])
        both = jnp.stack([jnp.concatenate([f, t[None]]) for f, t in zip(first, last)])
        both = jnp.stack([lax.dynamic_index_in_dim(both, member ^ j, axis=0, keepdims=False) for j in range(8)])
        both = both.reshape(2, NX, TRIPLE, 2, HALF, 128).transpose(3, 0, 4, 1, 2, 5).reshape(2, RUN, 12, 128)

        def core_body(c):
            return lax.dynamic_index_in_dim(dkw[:, :, HALO:].reshape(2, 2, NX, 2, RUN, 128), c, axis=3, keepdims=False).transpose(0, 2, 1, 3, 4)

        def core_head(c):
            return lax.dynamic_index_in_dim(dkw[:, :, :HALO].reshape(2, 2, 2, NX, 128, 128), c, axis=2, keepdims=False).transpose(0, 2, 1, 3, 4)

        def owners(part, rows):
            other = lax.ppermute(part(1 - core).reshape(8, 2, rows, 128), 'cp', mate)
            total = (part(core).reshape(8, 2, rows, 128) + other).astype(BF16)
            got = swap([lax.dynamic_index_in_dim(total, member ^ k, axis=0, keepdims=False) for k in range(8)])
            same, cross = [sum(got[k].astype(F32) for k in range(8) if k // 2 % 2 == n) for n in range(2)]
            return jnp.stack([jnp.where(g_kv == 0, same, cross), jnp.where(g_kv == 0, cross, same)])

        head_sum = owners(core_head, 128)
        grads = owners(core_body, RUN)
        pieces = [lax.ppermute(head_sum, 'cp', halo_pairs(i, True)) for i in range(NX)]
        grads = grads + jnp.concatenate(pieces, axis=2)

        owned = jnp.stack(str_sum).transpose(2, 0, 1, 3, 4)
        owned = [lax.dynamic_index_in_dim(owned, x ^ k, axis=0, keepdims=False) for k in range(NX)]
        owned = jnp.stack([owned[0]] + [lax.ppermute(owned[k], 'cp', [(g[m], g[m ^ k]) for g in GROUP_X for m in range(NX)]) for k in range(1, NX)])
        home = [lax.dynamic_index_in_dim(owned, x ^ t, axis=0, keepdims=False) for t in range(NX)]
        by_kv = []
        for g in range(2):
            slots = [jnp.zeros((2, BLOCK, 128), F32)] * STRIDE
            for h in range(6 * g, 6 * g + 6):
                slots[residue(h)] = home[h // TRIPLE][h % TRIPLE]
            by_kv.append(jnp.concatenate(slots, axis=1))
        grads = (grads + jnp.stack(by_kv)).astype(BF16)
        grads = grads.transpose(1, 2, 0, 3)
        return both[0][None], both[1][None], grads[0][None], grads[1][None]

    return jax.shard_map(layer, mesh=mesh, in_specs=(spec, spec, spec, spec), out_specs=(spec, spec, spec, spec), check_vma=False)
```

time: 749 us -> 585 us (0.78)
  the two profiles are of different devices: /device:TPU:30 before, /device:TPU:62 now
where the time goes in v2:
time: 585 us; the launch traced here: 576 us
  Pallas kernels  204 us (35%)
  waiting for transfers between devices  171 us (29%)
  starting transfers between devices  111 us (19%)
  local copies, waits for them, and re-layouts  32.6 us (6%)
  other arithmetic  30.9 us (5%)
  between operations  15.2 us (3%)
  blocking collectives  10.6 us (2%)
    pallas_call x3, Pallas kernels, head_attention(): pl.pallas_call(functools.partial(attn_kernel, chained), grid_spec=pltpu.P...  204 us
    ppermute x28, waiting for transfers between devices, swap(): lax.ppermute(parts[k], 'cp', [(g[m], g[m ^ k]) for g in GROUP_Q for m in...  91.3 us
    ppermute x28, starting transfers between devices, swap(): lax.ppermute(parts[k], 'cp', [(g[m], g[m ^ k]) for g in GROUP_Q for m in...  41.9 us
    all_to_all x1, waiting for transfers between devices, layer(): a2a(jnp.concatenate([pack(q_rope), pack(d_out)], axis=1), axis_index_grou...  38.4 us
    all_to_all x3, starting transfers between devices, layer(): back = a2a(dkv, axis_index_groups=GROUP_ZYC)  35 us
    ppermute x3, waiting for transfers between devices, layer(): lax.ppermute(two, 'cp', [(g[m], g[m ^ k]) for g in GROUP_WG for m in rang...  29.8 us
  transfers between devices with their start and end apart: 53, of which 18 were waited for; matrix products, arithmetic and copies ran while one was open for 10% of the time, Pallas kernels for 35%

profile of v2, /device:TPU:62, one launch (start us, length us, event | category | flops | bytes accessed | tf_op | source)
XLA Modules:
  0.0 576.1 jit_solution(11194958952770156138)
XLA Ops:
  9.4 10.6 %all_to_all.25 = bf16[4,3,2,64,128]{4,3,2,1,0:T(8,128)(2,1)S(1)} all-to-all(bf16[4,3,2,64,128]{4,3,2,1,0:T(8,128)(2,1)S(1)} %pad_maximum_fusion.8), channel_id=1, replica_groups={{0,2,4,6},{1,3,5,7},{8,10,12,14},{9,11,13,15},{16,18,20,22},{17,19,21,2..., dimensions={0} | all-to-all | bytes 786432 | tf_op jit(solution)/shard_map/all_to_all | solution.py:254
  21.5 5.0 collective-permute-start.1
  26.5 3.5 collective-permute-start.3
  35.3 8.7 %collective-permute-done.4 = bf16[2,640,128]{2,1,0:T(8,128)(2,1)S(1)} collective-permute-done((bf16[2,640,128]{2,1,0:T(8,128)(2,1)S(1)}, bf16[2,640,128]{2,1,0:T(8,128)(2,1)S(1)}, u32[]{:S(2)}, u32[]{:S(2)}) %collective-permute-start.4) | collective-permute-done | bytes 327712 | tf_op jit(solution)/shard_map/ppermute | solution.py:268
  47.7 29.8 %collective-permute-done.6 = bf16[2,2,640,128]{3,2,1,0:T(8,128)(2,1)S(1)} collective-permute-done((bf16[2,2,640,128]{3,2,1,0:T(8,128)(2,1)S(1)}, bf16[2,2,640,128]{3,2,1,0:T(8,128)(2,1)S(1)}, u32[]{:S(2)}, u32[]{:S(2)}) %collective-permute-start.6) | collective-permute-done | bytes 655392 | tf_op jit(solution)/shard_map/ppermute | solution.py:271
  83.0 9.7 %all-to-all-start = ((bf16[8,6,256,128]{3,2,1,0:T(8,128)(2,1)}), bf16[8,6,256,128]{3,2,1,0:T(8,128)(2,1)}, u32[]{:S(2)}, u32[]{:S(2)}) async-start(bf16[8,6,256,128]{3,2,1,0:T(8,128)(2,1)} %pad_maximum_fusion.2), calls=%async_computation | async-start | bytes 6291456 | tf_op jit(solution)/shard_map/all_to_all | solution.py:261
  97.1 2.7 pad_maximum_fusion.kw_ref
  99.8 38.4 %all-to-all-done.q_ref.do_ref = bf16[8,6,256,128]{3,2,1,0:T(8,128)(2,1)} async-done(((bf16[8,6,256,128]{3,2,1,0:T(8,128)(2,1)}), bf16[8,6,256,128]{3,2,1,0:T(8,128)(2,1)}, u32[]{:S(2)}, u32[]{:S(2)}) %all-to-all-start) | async-done | bytes 3145760 | tf_op jit(solution)/shard_map/all_to_all | solution.py:261
  138.2 64.1 %head_attention.3 = (bf16[8,2,256,128]{3,2,1,0:T(8,128)(2,1)}, bf16[32,2,4,64,128]{4,3,2,1,0:T(8,128)(2,1)}, f32[2,2,5120,128]{3,2,1,0:T(8,128)}) custom-call(s32[8]{0:T(128)} %stack.230.info, bf16[8,6,256,128]{3,2,1,0:T(8,128)(2,1)} %all-to-all-done.q_ref.do_ref, bf16[8,6,256,128]{3,2,1,0:T(8,128)(2,1)} %all-to-all-done.q_ref.do_ref, ...), custom_call_target="tpu_custom_call" | custom-call | flops 16986931200 | bytes 41943040 | tf_op jit(solution)/shard_map/head_attention/pallas_call | solution.py:195
  202.3 21.0 %all-to-all-start.2 = ((bf16[32,2,4,64,128]{4,3,2,1,0:T(8,128)(2,1)}), bf16[32,2,4,64,128]{4,3,2,1,0:T(8,128)(2,1)}, u32[]{:S(2)}, u32[]{:S(2)}) async-start(bf16[32,2,4,64,128]{4,3,2,1,0:T(8,128)(2,1)} %get-tuple-element.19), calls=%async_computation.2 | async-start | bytes 8388608 | tf_op jit(solution)/shard_map/all_to_all | solution.py:292
  224.0 70.0 %head_attention.4 = (bf16[8,2,256,128]{3,2,1,0:T(8,128)(2,1)}, bf16[32,2,4,64,128]{4,3,2,1,0:T(8,128)(2,1)}, f32[2,2,5120,128]{3,2,1,0:T(8,128)}) custom-call(s32[8]{0:T(128)} %stack.254.info, bf16[8,6,256,128]{3,2,1,0:T(8,128)(2,1)} %all-to-all-done.q_ref.do_ref, bf16[8,6,256,128]{3,2,1,0:T(8,128)(2,1)} %all-to-all-done.q_ref.do_ref, ...), custom_call_target="tpu_custom_call" | custom-call | flops 16986931200 | bytes 41943040 | tf_op jit(solution)/shard_map/head_attention/pallas_call | solution.py:195
  294.0 7.5 %all-to-all-start.3 = ((bf16[32,2,4,64,128]{4,3,2,1,0:T(8,128)(2,1)}), bf16[32,2,4,64,128]{4,3,2,1,0:T(8,128)(2,1)}, u32[]{:S(2)}, u32[]{:S(2)}) async-start(bf16[32,2,4,64,128]{4,3,2,1,0:T(8,128)(2,1)} %get-tuple-element.20), calls=%async_computation.3 | async-start | bytes 8388608 | tf_op jit(solution)/shard_map/all_to_all | solution.py:292
  302.3 69.9 %head_attention.5 = (bf16[8,2,256,128]{3,2,1,0:T(8,128)(2,1)}, bf16[32,2,4,64,128]{4,3,2,1,0:T(8,128)(2,1)}, f32[2,2,5120,128]{3,2,1,0:T(8,128)}) custom-call(s32[8]{0:T(128)} %stack.256.info, bf16[8,6,256,128]{3,2,1,0:T(8,128)(2,1)} %all-to-all-done.q_ref.do_ref, bf16[8,6,256,128]{3,2,1,0:T(8,128)(2,1)} %all-to-all-done.q_ref.do_ref, ...), custom_call_target="tpu_custom_call" | custom-call | flops 16986931200 | bytes 41943040 | tf_op jit(solution)/shard_map/head_attention/pallas_call | solution.py:195
  374.0 4.1 slice.258
  381.3 2.9 collective-permute-start.18
  390.0 3.9 dynamic-slice_bitcast_fusion.1
  394.0 6.5 %all-to-all-start.4 = ((bf16[32,2,4,64,128]{4,3,2,1,0:T(8,128)(2,1)}), bf16[32,2,4,64,128]{4,3,2,1,0:T(8,128)(2,1)}, u32[]{:S(2)}, u32[]{:S(2)}) async-start(bf16[32,2,4,64,128]{4,3,2,1,0:T(8,128)(2,1)} %get-tuple-element.21), calls=%async_computation.4 | async-start | bytes 8388608 | tf_op jit(solution)/shard_map/all_to_all | solution.py:292
  401.5 4.8 copy.111
  418.6 2.9 collective-permute-start.19
  422.5 45.1 %collective-permute-done.16 = bf16[2,256,128]{2,1,0:T(8,128)(2,1)S(1)} collective-permute-done((bf16[2,256,128]{2,1,0:T(8,128)(2,1)S(1)}, bf16[2,256,128]{2,1,0:T(8,128)(2,1)S(1)}, u32[]{:S(2)}, u32[]{:S(2)}) %collective-permute-start.16) | collective-permute-done | bytes 131104 | tf_op jit(solution)/shard_map/ppermute | solution.py:283
  468.2 3.0 collective-permute-start.20
  475.7 7.9 %collective-permute-done.22 = bf16[2,256,128]{2,1,0:T(8,128)(2,1)S(1)} collective-permute-done((bf16[2,256,128]{2,1,0:T(8,128)(2,1)S(1)}, bf16[2,256,128]{2,1,0:T(8,128)(2,1)S(1)}, u32[]{:S(2)}, u32[]{:S(2)}) %collective-permute-start.22) | collective-permute-done | bytes 131104 | tf_op jit(solution)/shard_map/ppermute | solution.py:283
  484.7 4.6 collective-permute-start.37
  498.1 3.1 convert_reduce_fusion.2
  501.3 3.1 convert_reduce_fusion.1
  504.5 3.3 convert_reduce_fusion
  512.1 2.7 fusion.1
  515.8 2.9 collective-permute-start.30
  524.7 3.0 collective-permute-done.24
  528.8 9.0 %collective-permute-done.30 = bf16[2,512,128]{2,1,0:T(8,128)(2,1)S(1)} collective-permute-done((bf16[2,512,128]{2,1,0:T(8,128)(2,1)S(1)}, bf16[2,512,128]{2,1,0:T(8,128)(2,1)S(1)}, u32[]{:S(2)}, u32[]{:S(2)}) %collective-permute-start.30) | collective-permute-done | bytes 262176 | tf_op jit(solution)/shard_map/ppermute | solution.py:283
  543.0 6.9 %collective-permute-done.26 = bf16[2,512,128]{2,1,0:T(8,128)(2,1)S(1)} collective-permute-done((bf16[2,512,128]{2,1,0:T(8,128)(2,1)S(1)}, bf16[2,512,128]{2,1,0:T(8,128)(2,1)S(1)}, u32[]{:S(2)}, u32[]{:S(2)}) %collective-permute-start.26) | collective-permute-done | bytes 262176 | tf_op jit(solution)/shard_map/ppermute | solution.py:283
  551.1 15.5 %collective-permute-done.25 = bf16[2,512,128]{2,1,0:T(8,128)(2,1)S(1)} collective-permute-done((bf16[2,512,128]{2,1,0:T(8,128)(2,1)S(1)}, bf16[2,512,128]{2,1,0:T(8,128)(2,1)S(1)}, u32[]{:S(2)}, u32[]{:S(2)}) %collective-permute-start.25) | collective-permute-done | bytes 262176 | tf_op jit(solution)/shard_map/ppermute | solution.py:283
  (202 shorter events, 84.7 us)
Async XLA Ops:
  7.2 131.1 %all-gather.7.cloned.1.call-start = ((), (), s32[]{:S(2)}) async-start(), calls=%async_computation.5 | async-start | bytes 4325376 | tf_op jit(solution)/shard_map/all_gather | solution.py:259
  20.7 203.3 %all-gather.9.cloned.1.call-start = ((), (), s32[]{:S(2)}) async-start(), calls=%async_computation.6 | async-start | bytes 4325376 | tf_op jit(solution)/shard_map/all_gather | solution.py:259
  44.2 33.4 %collective-permute-start.6 = (bf16[2,2,640,128]{3,2,1,0:T(8,128)(2,1)S(1)}, bf16[2,2,640,128]{3,2,1,0:T(8,128)(2,1)S(1)}, u32[]{:S(2)}, u32[]{:S(2)}) collective-permute-start(bf16[2,2,640,128]{3,2,1,0:T(8,128)(2,1)S(1)} %get-tuple-element.92), channel_id=1, source_target_pairs={{0,96},{2,98},{96,0},{98,2},{1,97},{3,99},{97,1},{99,3},{4,100},{6... | collective-permute-start | bytes 1966088 | tf_op jit(solution)/shard_map/ppermute | solution.py:271
  45.9 31.7 %collective-permute-start.5 = (bf16[2,2,640,128]{3,2,1,0:T(8,128)(2,1)S(1)}, bf16[2,2,640,128]{3,2,1,0:T(8,128)(2,1)S(1)}, u32[]{:S(2)}, u32[]{:S(2)}) collective-permute-start(bf16[2,2,640,128]{3,2,1,0:T(8,128)(2,1)S(1)} %get-tuple-element.92), channel_id=1, source_target_pairs={{0,2},{2,0},{96,98},{98,96},{1,3},{3,1},{97,99},{99,97},{4,6},{6,4... | collective-permute-start | bytes 1966088 | tf_op jit(solution)/shard_map/ppermute | solution.py:271
  47.4 30.2 %collective-permute-start.7 = (bf16[2,2,640,128]{3,2,1,0:T(8,128)(2,1)S(1)}, bf16[2,2,640,128]{3,2,1,0:T(8,128)(2,1)S(1)}, u32[]{:S(2)}, u32[]{:S(2)}) collective-permute-start(bf16[2,2,640,128]{3,2,1,0:T(8,128)(2,1)S(1)} %get-tuple-element.92), channel_id=1, source_target_pairs={{0,98},{2,96},{96,2},{98,0},{1,99},{3,97},{97,3},{99,1},{4,102},{6... | collective-permute-start | bytes 1966088 | tf_op jit(solution)/shard_map/ppermute | solution.py:271
  79.9 14.3 %collective-permute-start.8 = (bf16[4,2,2,640,128]{4,3,2,1,0:T(8,128)(2,1)}, bf16[4,2,2,640,128]{4,3,2,1,0:T(8,128)(2,1)}, u32[]{:S(2)}, u32[]{:S(2)}) collective-permute-start(bf16[4,2,2,640,128]{4,3,2,1,0:T(8,128)(2,1)} %pad_maximum_fusion.4), channel_id=1, source_target_pairs={{0,1},{1,0},{2,3},{3,2},{4,5},{5,4},{6,7},{7,6},{8,9},{9,8},{10,11... | collective-permute-start | bytes 7864328 | tf_op jit(solution)/shard_map/ppermute | solution.py:273
  83.0 55.2 %all-to-all-start = ((bf16[8,6,256,128]{3,2,1,0:T(8,128)(2,1)}), bf16[8,6,256,128]{3,2,1,0:T(8,128)(2,1)}, u32[]{:S(2)}, u32[]{:S(2)}) async-start(bf16[8,6,256,128]{3,2,1,0:T(8,128)(2,1)} %pad_maximum_fusion.2), calls=%async_computation | async-start | bytes 6291456 | tf_op jit(solution)/shard_map/all_to_all | solution.py:261
  92.7 209.6 %all-gather.11.cloned.1.call-start = ((), (), s32[]{:S(2)}) async-start(), calls=%async_computation.7 | async-start | bytes 4325376 | tf_op jit(solution)/shard_map/all_gather | solution.py:259
  202.3 91.7 %all-to-all-start.2 = ((bf16[32,2,4,64,128]{4,3,2,1,0:T(8,128)(2,1)}), bf16[32,2,4,64,128]{4,3,2,1,0:T(8,128)(2,1)}, u32[]{:S(2)}, u32[]{:S(2)}) async-start(bf16[32,2,4,64,128]{4,3,2,1,0:T(8,128)(2,1)} %get-tuple-element.19), calls=%async_computation.2 | async-start | bytes 8388608 | tf_op jit(solution)/shard_map/all_to_all | solution.py:292
  294.0 99.9 %all-to-all-start.3 = ((bf16[32,2,4,64,128]{4,3,2,1,0:T(8,128)(2,1)}), bf16[32,2,4,64,128]{4,3,2,1,0:T(8,128)(2,1)}, u32[]{:S(2)}, u32[]{:S(2)}) async-start(bf16[32,2,4,64,128]{4,3,2,1,0:T(8,128)(2,1)} %get-tuple-element.20), calls=%async_computation.3 | async-start | bytes 8388608 | tf_op jit(solution)/shard_map/all_to_all | solution.py:292
  379.6 31.8 %collective-permute-start.9 = (bf16[2,2,256,128]{3,2,1,0:T(8,128)(2,1)}, bf16[2,2,256,128]{3,2,1,0:T(8,128)(2,1)}, u32[]{:S(2)}, u32[]{:S(2)}) collective-permute-start(bf16[2,2,256,128]{3,2,1,0:T(8,128)(2,1)} %pad_maximum_fusion.9), channel_id=1, source_target_pairs={{0,2},{2,0},{4,6},{6,4},{96,98},{98,96},{100,102},{102,100},{1,3},... | collective-permute-start | bytes 786440 | tf_op jit(solution)/shard_map/ppermute | solution.py:283
  380.4 36.3 %collective-permute-start.11 = (bf16[2,2,256,128]{3,2,1,0:T(8,128)(2,1)}, bf16[2,2,256,128]{3,2,1,0:T(8,128)(2,1)}, u32[]{:S(2)}, u32[]{:S(2)}) collective-permute-start(bf16[2,2,256,128]{3,2,1,0:T(8,128)(2,1)} %pad_maximum_fusion.10), channel_id=1, source_target_pairs={{0,4},{2,6},{4,0},{6,2},{96,100},{98,102},{100,96},{102,98},{1,5},... | collective-permute-start | bytes 786440 | tf_op jit(solution)/shard_map/ppermute | solution.py:283
  381.3 25.0 %collective-permute-start.18 = (bf16[2,256,128]{2,1,0:T(8,128)(2,1)}, bf16[2,256,128]{2,1,0:T(8,128)(2,1)}, u32[]{:S(2)}, u32[]{:S(2)}) collective-permute-start(bf16[2,256,128]{2,1,0:T(8,128)(2,1)} %get-tuple-element.69), channel_id=1, source_target_pairs={{0,98},{2,96},{4,102},{6,100},{96,2},{98,0},{100,6},{102,4},{1,99}... | collective-permute-start | bytes 393224 | tf_op jit(solution)/shard_map/ppermute | solution.py:283
  384.2 22.7 %collective-permute-start.14 = (bf16[2,256,128]{2,1,0:T(8,128)(2,1)}, bf16[2,256,128]{2,1,0:T(8,128)(2,1)}, u32[]{:S(2)}, u32[]{:S(2)}) collective-permute-start(bf16[2,256,128]{2,1,0:T(8,128)(2,1)} %get-tuple-element.71), channel_id=1, source_target_pairs={{0,6},{2,4},{4,2},{6,0},{96,102},{98,100},{100,98},{102,96},{1,7},... | collective-permute-start | bytes 393224 | tf_op jit(solution)/shard_map/ppermute | solution.py:283
  386.3 22.7 %collective-permute-start.10 = (bf16[2,256,128]{2,1,0:T(8,128)(2,1)}, bf16[2,256,128]{2,1,0:T(8,128)(2,1)}, u32[]{:S(2)}, u32[]{:S(2)}) collective-permute-start(bf16[2,256,128]{2,1,0:T(8,128)(2,1)} %get-tuple-element.73), channel_id=1, source_target_pairs={{0,2},{2,0},{4,6},{6,4},{96,98},{98,96},{100,102},{102,100},{1,3},... | collective-permute-start | bytes 393224 | tf_op jit(solution)/shard_map/ppermute | solution.py:283
  394.0 110.5 %all-to-all-start.4 = ((bf16[32,2,4,64,128]{4,3,2,1,0:T(8,128)(2,1)}), bf16[32,2,4,64,128]{4,3,2,1,0:T(8,128)(2,1)}, u32[]{:S(2)}, u32[]{:S(2)}) async-start(bf16[32,2,4,64,128]{4,3,2,1,0:T(8,128)(2,1)} %get-tuple-element.21), calls=%async_computation.4 | async-start | bytes 8388608 | tf_op jit(solution)/shard_map/all_to_all | solution.py:292
  409.0 103.1 %collective-permute-start.23 = (f32[8,2,512,128]{3,2,1,0:T(8,128)}, f32[8,2,512,128]{3,2,1,0:T(8,128)}, u32[]{:S(2)}, u32[]{:S(2)}) collective-permute-start(f32[8,2,512,128]{3,2,1,0:T(8,128)} %bitcast.88), channel_id=1, source_target_pairs={{0,1},{1,0},{2,3},{3,2},{4,5},{5,4},{6,7},{7,6},{8,9},{9,8},{10,11... | collective-permute-start | bytes 12582920 | tf_op jit(solution)/shard_map/ppermute | solution.py:309
  411.5 56.7 %collective-permute-start.15 = (bf16[2,2,256,128]{3,2,1,0:T(8,128)(2,1)S(1)}, bf16[2,2,256,128]{3,2,1,0:T(8,128)(2,1)S(1)}, u32[]{:S(2)}, u32[]{:S(2)}) collective-permute-start(bf16[2,2,256,128]{3,2,1,0:T(8,128)(2,1)S(1)} %pad_maximum_fusion.12), channel_id=1, source_target_pairs={{0,96},{2,98},{4,100},{6,102},{96,0},{98,2},{100,4},{102,6},{1,97}... | collective-permute-start | bytes 786440 | tf_op jit(solution)/shard_map/ppermute | solution.py:283
  414.2 57.0 %collective-permute-start.17 = (bf16[2,2,256,128]{3,2,1,0:T(8,128)(2,1)S(1)}, bf16[2,2,256,128]{3,2,1,0:T(8,128)(2,1)S(1)}, u32[]{:S(2)}, u32[]{:S(2)}) collective-permute-start(bf16[2,2,256,128]{3,2,1,0:T(8,128)(2,1)S(1)} %pad_maximum_fusion.13), channel_id=1, source_target_pairs={{0,98},{2,96},{4,102},{6,100},{96,2},{98,0},{100,6},{102,4},{1,99}... | collective-permute-start | bytes 786440 | tf_op jit(solution)/shard_map/ppermute | solution.py:283
  416.6 50.9 %collective-permute-start.16 = (bf16[2,256,128]{2,1,0:T(8,128)(2,1)S(1)}, bf16[2,256,128]{2,1,0:T(8,128)(2,1)S(1)}, u32[]{:S(2)}, u32[]{:S(2)}) collective-permute-start(bf16[2,256,128]{2,1,0:T(8,128)(2,1)S(1)} %copy-done.11), channel_id=1, source_target_pairs={{0,96},{2,98},{4,100},{6,102},{96,0},{98,2},{100,4},{102,6},{1,97}... | collective-permute-start | bytes 393224 | tf_op jit(solution)/shard_map/ppermute | solution.py:283
  418.6 57.0 %collective-permute-start.19 = (bf16[2,2,256,128]{3,2,1,0:T(8,128)(2,1)S(1)}, bf16[2,2,256,128]{3,2,1,0:T(8,128)(2,1)S(1)}, u32[]{:S(2)}, u32[]{:S(2)}) collective-permute-start(bf16[2,2,256,128]{3,2,1,0:T(8,128)(2,1)S(1)} %pad_maximum_fusion.14), channel_id=1, source_target_pairs={{0,100},{2,102},{4,96},{6,98},{96,4},{98,6},{100,0},{102,2},{1,101... | collective-permute-start | bytes 786440 | tf_op jit(solution)/shard_map/ppermute | solution.py:283
  467.6 16.0 %collective-permute-start.21 = (bf16[2,2,256,128]{3,2,1,0:T(8,128)(2,1)S(1)}, bf16[2,2,256,128]{3,2,1,0:T(8,128)(2,1)S(1)}, u32[]{:S(2)}, u32[]{:S(2)}) collective-permute-start(bf16[2,2,256,128]{3,2,1,0:T(8,128)(2,1)S(1)} %copy-done.8), channel_id=1, source_target_pairs={{0,102},{2,100},{4,98},{6,96},{96,6},{98,4},{100,2},{102,0},{1,103... | collective-permute-start | bytes 786440 | tf_op jit(solution)/shard_map/ppermute | solution.py:283
  515.8 22.0 %collective-permute-start.30 = (bf16[2,512,128]{2,1,0:T(8,128)(2,1)S(1)}, bf16[2,512,128]{2,1,0:T(8,128)(2,1)S(1)}, u32[]{:S(2)}, u32[]{:S(2)}) collective-permute-start(bf16[2,512,128]{2,1,0:T(8,128)(2,1)S(1)} %get-tuple-element.43), channel_id=1, source_target_pairs={{0,102},{2,100},{4,98},{6,96},{96,6},{98,4},{100,2},{102,0},{1,103... | collective-permute-start | bytes 786440 | tf_op jit(solution)/shard_map/ppermute | solution.py:283
  518.7 19.4 %collective-permute-start.29 = (bf16[2,512,128]{2,1,0:T(8,128)(2,1)S(1)}, bf16[2,512,128]{2,1,0:T(8,128)(2,1)S(1)}, u32[]{:S(2)}, u32[]{:S(2)}) collective-permute-start(bf16[2,512,128]{2,1,0:T(8,128)(2,1)S(1)} %get-tuple-element.44), channel_id=1, source_target_pairs={{0,100},{2,102},{4,96},{6,98},{96,4},{98,6},{100,0},{102,2},{1,101... | collective-permute-start | bytes 786440 | tf_op jit(solution)/shard_map/ppermute | solution.py:283
  520.0 20.3 %collective-permute-start.28 = (bf16[2,512,128]{2,1,0:T(8,128)(2,1)S(1)}, bf16[2,512,128]{2,1,0:T(8,128)(2,1)S(1)}, u32[]{:S(2)}, u32[]{:S(2)}) collective-permute-start(bf16[2,512,128]{2,1,0:T(8,128)(2,1)S(1)} %get-tuple-element.45), channel_id=1, source_target_pairs={{0,6},{2,4},{4,2},{6,0},{96,102},{98,100},{100,98},{102,96},{1,7},... | collective-permute-start | bytes 786440 | tf_op jit(solution)/shard_map/ppermute | solution.py:283
  522.1 19.6 %collective-permute-start.27 = (bf16[2,512,128]{2,1,0:T(8,128)(2,1)S(1)}, bf16[2,512,128]{2,1,0:T(8,128)(2,1)S(1)}, u32[]{:S(2)}, u32[]{:S(2)}) collective-permute-start(bf16[2,512,128]{2,1,0:T(8,128)(2,1)S(1)} %get-tuple-element.46), channel_id=1, source_target_pairs={{0,4},{2,6},{4,0},{6,2},{96,100},{98,102},{100,96},{102,98},{1,5},... | collective-permute-start | bytes 786440 | tf_op jit(solution)/shard_map/ppermute | solution.py:283
  527.7 22.2 %collective-permute-start.26 = (bf16[2,512,128]{2,1,0:T(8,128)(2,1)S(1)}, bf16[2,512,128]{2,1,0:T(8,128)(2,1)S(1)}, u32[]{:S(2)}, u32[]{:S(2)}) collective-permute-start(bf16[2,512,128]{2,1,0:T(8,128)(2,1)S(1)} %get-tuple-element.47), channel_id=1, source_target_pairs={{0,98},{2,96},{4,102},{6,100},{96,2},{98,0},{100,6},{102,4},{1,99}... | collective-permute-start | bytes 786440 | tf_op jit(solution)/shard_map/ppermute | solution.py:283
  537.8 28.8 %collective-permute-start.25 = (bf16[2,512,128]{2,1,0:T(8,128)(2,1)S(1)}, bf16[2,512,128]{2,1,0:T(8,128)(2,1)S(1)}, u32[]{:S(2)}, u32[]{:S(2)}) collective-permute-start(bf16[2,512,128]{2,1,0:T(8,128)(2,1)S(1)} %get-tuple-element.48), channel_id=1, source_target_pairs={{0,96},{2,98},{4,100},{6,102},{96,0},{98,2},{100,4},{102,6},{1,97}... | collective-permute-start | bytes 786440 | tf_op jit(solution)/shard_map/ppermute | solution.py:283
  538.1 28.9 %collective-permute-start.42 = (f32[2,2,128,128]{3,2,1,0:T(8,128)S(1)}, f32[2,2,128,128]{3,2,1,0:T(8,128)S(1)}, u32[]{:S(2)}, u32[]{:S(2)}) collective-permute-start(f32[2,2,128,128]{3,2,1,0:T(8,128)S(1)} %pad_maximum_fusion.16), channel_id=1, source_target_pairs={{14,6},{15,7},{22,14},{23,15},{30,22},{31,23},{38,30},{39,31},{46,... | collective-permute-start | bytes 786440 | tf_op jit(solution)/shard_map/ppermute | solution.py:317
  540.4 26.6 %collective-permute-start.41 = (f32[2,2,128,128]{3,2,1,0:T(8,128)S(1)}, f32[2,2,128,128]{3,2,1,0:T(8,128)S(1)}, u32[]{:S(2)}, u32[]{:S(2)}) collective-permute-start(f32[2,2,128,128]{3,2,1,0:T(8,128)S(1)} %pad_maximum_fusion.16), channel_id=1, source_target_pairs={{12,6},{13,7},{20,14},{21,15},{28,22},{29,23},{36,30},{37,31},{44,... | collective-permute-start | bytes 786440 | tf_op jit(solution)/shard_map/ppermute | solution.py:317
  541.7 25.3 %collective-permute-start.40 = (f32[2,2,128,128]{3,2,1,0:T(8,128)S(1)}, f32[2,2,128,128]{3,2,1,0:T(8,128)S(1)}, u32[]{:S(2)}, u32[]{:S(2)}) collective-permute-start(f32[2,2,128,128]{3,2,1,0:T(8,128)S(1)} %pad_maximum_fusion.16), channel_id=1, source_target_pairs={{10,6},{11,7},{18,14},{19,15},{26,22},{27,23},{34,30},{35,31},{42,... | collective-permute-start | bytes 786440 | tf_op jit(solution)/shard_map/ppermute | solution.py:317
  549.8 17.1 %collective-permute-start.39 = (f32[2,2,128,128]{3,2,1,0:T(8,128)S(1)}, f32[2,2,128,128]{3,2,1,0:T(8,128)S(1)}, u32[]{:S(2)}, u32[]{:S(2)}) collective-permute-start(f32[2,2,128,128]{3,2,1,0:T(8,128)S(1)} %pad_maximum_fusion.16), channel_id=1, source_target_pairs={{8,6},{9,7},{16,14},{17,15},{24,22},{25,23},{32,30},{33,31},{40,38... | collective-permute-start | bytes 786440 | tf_op jit(solution)/shard_map/ppermute | solution.py:317
  (34 other events, 393.8 us)
Sparse Core Ops, SparseCore 0:
  20.8 61.7 all-gather.6
  85.5 69.8 all-gather.8
  158.2 45.5 all-gather.10

commit v3 on v2

--- a/solution.py
+++ b/solution.py
@@ -59,7 +59,7 @@
 
 def attn_kernel(chained, info, q_ref, do_ref, ks_ref, vs_ref, kw_ref, *refs):
     prev_ref = refs[0] if chained else None
-    oq_ref, dkv_ref, dkw_ref, e_s, dp_s, m_s, e_l, dp_l, dk_s, dv_s = refs[chained:]
+    oq_ref, dkv_ref, dkw_ref, e_s, dp_s, m_s, e_l, dp_l, dk_s, dv_s, prev_sem = refs[chained:]
     tile = pl.program_id(0)
     member = tile // NX
     xsrc = tile % NX
@@ -82,7 +82,7 @@
     @pl.when(xsrc == 0)
     def _():
         if chained:
-            pltpu.sync_copy(prev_ref.at[member], dkw_ref.at[0])
+            pltpu.make_async_copy(prev_ref.at[member], dkw_ref.at[0], prev_sem).start()
         else:
             dkw_ref[...] = jnp.zeros_like(dkw_ref)
 
@@ -157,6 +157,11 @@
     pairs = [weights(e_l[BLOCK * lo:BLOCK * hi], dp_l[BLOCK * lo:BLOCK * hi], m_l[n]) for n, (lo, hi) in enumerate(WSUB)]
     pb = jnp.concatenate([p for p, _ in pairs], axis=0)
     ds = jnp.concatenate([g for _, g in pairs], axis=0)
+    if chained:
+        @pl.when(xsrc == 0)
+        def _():
+            pltpu.make_async_copy(prev_ref.at[member], dkw_ref.at[0], prev_sem).wait()
+
     ot = tn(kw_ref[0, 1, win], pb)
     dqt = tn(kw_ref[0, 0, win], ds)
     dkw_ref[0, 1, win] += nn(pb, do)
@@ -209,6 +214,7 @@
                 pltpu.VMEM((WIN, HALF), F32),
                 pltpu.VMEM((8192, 128), F32),
                 pltpu.VMEM((8192, 128), F32),
+                pltpu.SemaphoreType.DMA,
             ],
         ),
         out_shape=[jax.ShapeDtypeStruct((8, 2, HALF, 128), BF16),

time: 585 us -> 578 us (0.988)
  Pallas kernels: 204 us -> 196 us
    pallas_call x3, Pallas kernels: 204 us -> 196 us  [head_attention(): pl.pallas_call(functools.partial(attn_kernel, chained), grid_spec=pltpu.P...]
  transfers between devices with their start and end apart: 53 -> 53, of which waited for: 18 -> 18; matrix products, arithmetic and copies ran while one was open for 10% -> 10% of each run, Pallas kernels for 35% -> 34%
where the time goes in v3:
time: 578 us; the launch traced here: 569 us
  Pallas kernels  196 us (34%)
  waiting for transfers between devices  172 us (30%)
  starting transfers between devices  113 us (20%)
  local copies, waits for them, and re-layouts  32.6 us (6%)
  other arithmetic  30.9 us (5%)
  between operations  15.2 us (3%)
  blocking collectives  10.6 us (2%)
    pallas_call x3, Pallas kernels, head_attention(): pl.pallas_call(functools.partial(attn_kernel, chained), grid_spec=pltpu.P...  196 us
    ppermute x28, waiting for transfers between devices, swap(): lax.ppermute(parts[k], 'cp', [(g[m], g[m ^ k]) for g in GROUP_Q for m in...  91.5 us
    ppermute x28, starting transfers between devices, swap(): lax.ppermute(parts[k], 'cp', [(g[m], g[m ^ k]) for g in GROUP_Q for m in...  41.8 us
    all_to_all x1, waiting for transfers between devices, layer(): a2a(jnp.concatenate([pack(q_rope), pack(d_out)], axis=1), axis_index_grou...  38.4 us
    all_to_all x3, starting transfers between devices, layer(): back = a2a(dkv, axis_index_groups=GROUP_ZYC)  36.3 us
    ppermute x3, waiting for transfers between devices, layer(): lax.ppermute(two, 'cp', [(g[m], g[m ^ k]) for g in GROUP_WG for m in rang...  29.8 us
  transfers between devices with their start and end apart: 53, of which 18 were waited for; matrix products, arithmetic and copies ran while one was open for 10% of the time, Pallas kernels for 34%

profile of v3, /device:TPU:62, one launch (start us, length us, event | category | flops | bytes accessed | tf_op | source)
XLA Modules:
  0.0 569.0 jit_solution(12942186406031451388)
XLA Ops:
  9.4 10.6 %all_to_all.25 = bf16[4,3,2,64,128]{4,3,2,1,0:T(8,128)(2,1)S(1)} all-to-all(bf16[4,3,2,64,128]{4,3,2,1,0:T(8,128)(2,1)S(1)} %pad_maximum_fusion.8), channel_id=1, replica_groups={{0,2,4,6},{1,3,5,7},{8,10,12,14},{9,11,13,15},{16,18,20,22},{17,19,21,2..., dimensions={0} | all-to-all | bytes 786432 | tf_op jit(solution)/shard_map/all_to_all | solution.py:260
  21.5 5.0 collective-permute-start.1
  26.5 3.5 collective-permute-start.3
  35.3 8.7 %collective-permute-done.4 = bf16[2,640,128]{2,1,0:T(8,128)(2,1)S(1)} collective-permute-done((bf16[2,640,128]{2,1,0:T(8,128)(2,1)S(1)}, bf16[2,640,128]{2,1,0:T(8,128)(2,1)S(1)}, u32[]{:S(2)}, u32[]{:S(2)}) %collective-permute-start.4) | collective-permute-done | bytes 327712 | tf_op jit(solution)/shard_map/ppermute | solution.py:274
  47.7 29.8 %collective-permute-done.6 = bf16[2,2,640,128]{3,2,1,0:T(8,128)(2,1)S(1)} collective-permute-done((bf16[2,2,640,128]{3,2,1,0:T(8,128)(2,1)S(1)}, bf16[2,2,640,128]{3,2,1,0:T(8,128)(2,1)S(1)}, u32[]{:S(2)}, u32[]{:S(2)}) %collective-permute-start.6) | collective-permute-done | bytes 655392 | tf_op jit(solution)/shard_map/ppermute | solution.py:277
  83.0 9.7 %all-to-all-start = ((bf16[8,6,256,128]{3,2,1,0:T(8,128)(2,1)}), bf16[8,6,256,128]{3,2,1,0:T(8,128)(2,1)}, u32[]{:S(2)}, u32[]{:S(2)}) async-start(bf16[8,6,256,128]{3,2,1,0:T(8,128)(2,1)} %pad_maximum_fusion.2), calls=%async_computation | async-start | bytes 6291456 | tf_op jit(solution)/shard_map/all_to_all | solution.py:267
  97.1 2.7 pad_maximum_fusion.kw_ref
  99.8 38.4 %all-to-all-done.q_ref.do_ref = bf16[8,6,256,128]{3,2,1,0:T(8,128)(2,1)} async-done(((bf16[8,6,256,128]{3,2,1,0:T(8,128)(2,1)}), bf16[8,6,256,128]{3,2,1,0:T(8,128)(2,1)}, u32[]{:S(2)}, u32[]{:S(2)}) %all-to-all-start) | async-done | bytes 3145760 | tf_op jit(solution)/shard_map/all_to_all | solution.py:267
  138.2 64.1 %head_attention.3 = (bf16[8,2,256,128]{3,2,1,0:T(8,128)(2,1)}, bf16[32,2,4,64,128]{4,3,2,1,0:T(8,128)(2,1)}, f32[2,2,5120,128]{3,2,1,0:T(8,128)}) custom-call(s32[8]{0:T(128)} %stack.230.info, bf16[8,6,256,128]{3,2,1,0:T(8,128)(2,1)} %all-to-all-done.q_ref.do_ref, bf16[8,6,256,128]{3,2,1,0:T(8,128)(2,1)} %all-to-all-done.q_ref.do_ref, ...), custom_call_target="tpu_custom_call" | custom-call | flops 16986931200 | bytes 41943040 | tf_op jit(solution)/shard_map/head_attention/pallas_call | solution.py:200
  202.4 21.2 %all-to-all-start.2 = ((bf16[32,2,4,64,128]{4,3,2,1,0:T(8,128)(2,1)}), bf16[32,2,4,64,128]{4,3,2,1,0:T(8,128)(2,1)}, u32[]{:S(2)}, u32[]{:S(2)}) async-start(bf16[32,2,4,64,128]{4,3,2,1,0:T(8,128)(2,1)} %get-tuple-element.19), calls=%async_computation.2 | async-start | bytes 8388608 | tf_op jit(solution)/shard_map/all_to_all | solution.py:298
  224.2 65.7 %head_attention.4 = (bf16[8,2,256,128]{3,2,1,0:T(8,128)(2,1)}, bf16[32,2,4,64,128]{4,3,2,1,0:T(8,128)(2,1)}, f32[2,2,5120,128]{3,2,1,0:T(8,128)}) custom-call(s32[8]{0:T(128)} %stack.254.info, bf16[8,6,256,128]{3,2,1,0:T(8,128)(2,1)} %all-to-all-done.q_ref.do_ref, bf16[8,6,256,128]{3,2,1,0:T(8,128)(2,1)} %all-to-all-done.q_ref.do_ref, ...), custom_call_target="tpu_custom_call" | custom-call | flops 16986931200 | bytes 41943040 | tf_op jit(solution)/shard_map/head_attention/pallas_call | solution.py:200
  290.0 8.0 %all-to-all-start.3 = ((bf16[32,2,4,64,128]{4,3,2,1,0:T(8,128)(2,1)}), bf16[32,2,4,64,128]{4,3,2,1,0:T(8,128)(2,1)}, u32[]{:S(2)}, u32[]{:S(2)}) async-start(bf16[32,2,4,64,128]{4,3,2,1,0:T(8,128)(2,1)} %get-tuple-element.20), calls=%async_computation.3 | async-start | bytes 8388608 | tf_op jit(solution)/shard_map/all_to_all | solution.py:298
  298.8 65.7 %head_attention.5 = (bf16[8,2,256,128]{3,2,1,0:T(8,128)(2,1)}, bf16[32,2,4,64,128]{4,3,2,1,0:T(8,128)(2,1)}, f32[2,2,5120,128]{3,2,1,0:T(8,128)}) custom-call(s32[8]{0:T(128)} %stack.256.info, bf16[8,6,256,128]{3,2,1,0:T(8,128)(2,1)} %all-to-all-done.q_ref.do_ref, bf16[8,6,256,128]{3,2,1,0:T(8,128)(2,1)} %all-to-all-done.q_ref.do_ref, ...), custom_call_target="tpu_custom_call" | custom-call | flops 16986931200 | bytes 41943040 | tf_op jit(solution)/shard_map/head_attention/pallas_call | solution.py:200
  366.2 4.1 slice.258
  373.6 3.0 collective-permute-start.18
  382.4 3.9 dynamic-slice_bitcast_fusion.1
  386.3 7.0 %all-to-all-start.4 = ((bf16[32,2,4,64,128]{4,3,2,1,0:T(8,128)(2,1)}), bf16[32,2,4,64,128]{4,3,2,1,0:T(8,128)(2,1)}, u32[]{:S(2)}, u32[]{:S(2)}) async-start(bf16[32,2,4,64,128]{4,3,2,1,0:T(8,128)(2,1)} %get-tuple-element.21), calls=%async_computation.4 | async-start | bytes 8388608 | tf_op jit(solution)/shard_map/all_to_all | solution.py:298
  394.4 4.8 copy.111
  411.5 2.7 collective-permute-start.19
  415.2 45.3 %collective-permute-done.16 = bf16[2,256,128]{2,1,0:T(8,128)(2,1)S(1)} collective-permute-done((bf16[2,256,128]{2,1,0:T(8,128)(2,1)S(1)}, bf16[2,256,128]{2,1,0:T(8,128)(2,1)S(1)}, u32[]{:S(2)}, u32[]{:S(2)}) %collective-permute-start.16) | collective-permute-done | bytes 131104 | tf_op jit(solution)/shard_map/ppermute | solution.py:289
  461.1 2.9 collective-permute-start.20
  465.8 2.7 collective-permute-done.20
  468.6 7.9 %collective-permute-done.22 = bf16[2,256,128]{2,1,0:T(8,128)(2,1)S(1)} collective-permute-done((bf16[2,256,128]{2,1,0:T(8,128)(2,1)S(1)}, bf16[2,256,128]{2,1,0:T(8,128)(2,1)S(1)}, u32[]{:S(2)}, u32[]{:S(2)}) %collective-permute-start.22) | collective-permute-done | bytes 131104 | tf_op jit(solution)/shard_map/ppermute | solution.py:289
  477.6 4.6 collective-permute-start.37
  491.0 3.1 convert_reduce_fusion.2
  494.2 3.1 convert_reduce_fusion.1
  497.4 3.3 convert_reduce_fusion
  508.7 2.9 collective-permute-start.30
  517.6 3.0 collective-permute-done.24
  521.7 9.0 %collective-permute-done.30 = bf16[2,512,128]{2,1,0:T(8,128)(2,1)S(1)} collective-permute-done((bf16[2,512,128]{2,1,0:T(8,128)(2,1)S(1)}, bf16[2,512,128]{2,1,0:T(8,128)(2,1)S(1)}, u32[]{:S(2)}, u32[]{:S(2)}) %collective-permute-start.30) | collective-permute-done | bytes 262176 | tf_op jit(solution)/shard_map/ppermute | solution.py:289
  535.9 6.9 %collective-permute-done.26 = bf16[2,512,128]{2,1,0:T(8,128)(2,1)S(1)} collective-permute-done((bf16[2,512,128]{2,1,0:T(8,128)(2,1)S(1)}, bf16[2,512,128]{2,1,0:T(8,128)(2,1)S(1)}, u32[]{:S(2)}, u32[]{:S(2)}) %collective-permute-start.26) | collective-permute-done | bytes 262176 | tf_op jit(solution)/shard_map/ppermute | solution.py:289
  544.0 15.5 %collective-permute-done.25 = bf16[2,512,128]{2,1,0:T(8,128)(2,1)S(1)} collective-permute-done((bf16[2,512,128]{2,1,0:T(8,128)(2,1)S(1)}, bf16[2,512,128]{2,1,0:T(8,128)(2,1)S(1)}, u32[]{:S(2)}, u32[]{:S(2)}) %collective-permute-start.25) | collective-permute-done | bytes 262176 | tf_op jit(solution)/shard_map/ppermute | solution.py:289
  (202 shorter events, 84.7 us)
Async XLA Ops:
  7.2 131.1 %all-gather.7.cloned.1.call-start = ((), (), s32[]{:S(2)}) async-start(), calls=%async_computation.5 | async-start | bytes 4325376 | tf_op jit(solution)/shard_map/all_gather | solution.py:265
  20.7 203.5 %all-gather.9.cloned.1.call-start = ((), (), s32[]{:S(2)}) async-start(), calls=%async_computation.6 | async-start | bytes 4325376 | tf_op jit(solution)/shard_map/all_gather | solution.py:265
  44.2 33.4 %collective-permute-start.6 = (bf16[2,2,640,128]{3,2,1,0:T(8,128)(2,1)S(1)}, bf16[2,2,640,128]{3,2,1,0:T(8,128)(2,1)S(1)}, u32[]{:S(2)}, u32[]{:S(2)}) collective-permute-start(bf16[2,2,640,128]{3,2,1,0:T(8,128)(2,1)S(1)} %get-tuple-element.92), channel_id=1, source_target_pairs={{0,96},{2,98},{96,0},{98,2},{1,97},{3,99},{97,1},{99,3},{4,100},{6... | collective-permute-start | bytes 1966088 | tf_op jit(solution)/shard_map/ppermute | solution.py:277
  45.9 31.7 %collective-permute-start.5 = (bf16[2,2,640,128]{3,2,1,0:T(8,128)(2,1)S(1)}, bf16[2,2,640,128]{3,2,1,0:T(8,128)(2,1)S(1)}, u32[]{:S(2)}, u32[]{:S(2)}) collective-permute-start(bf16[2,2,640,128]{3,2,1,0:T(8,128)(2,1)S(1)} %get-tuple-element.92), channel_id=1, source_target_pairs={{0,2},{2,0},{96,98},{98,96},{1,3},{3,1},{97,99},{99,97},{4,6},{6,4... | collective-permute-start | bytes 1966088 | tf_op jit(solution)/shard_map/ppermute | solution.py:277
  47.4 30.2 %collective-permute-start.7 = (bf16[2,2,640,128]{3,2,1,0:T(8,128)(2,1)S(1)}, bf16[2,2,640,128]{3,2,1,0:T(8,128)(2,1)S(1)}, u32[]{:S(2)}, u32[]{:S(2)}) collective-permute-start(bf16[2,2,640,128]{3,2,1,0:T(8,128)(2,1)S(1)} %get-tuple-element.92), channel_id=1, source_target_pairs={{0,98},{2,96},{96,2},{98,0},{1,99},{3,97},{97,3},{99,1},{4,102},{6... | collective-permute-start | bytes 1966088 | tf_op jit(solution)/shard_map/ppermute | solution.py:277
  79.9 14.3 %collective-permute-start.8 = (bf16[4,2,2,640,128]{4,3,2,1,0:T(8,128)(2,1)}, bf16[4,2,2,640,128]{4,3,2,1,0:T(8,128)(2,1)}, u32[]{:S(2)}, u32[]{:S(2)}) collective-permute-start(bf16[4,2,2,640,128]{4,3,2,1,0:T(8,128)(2,1)} %pad_maximum_fusion.4), channel_id=1, source_target_pairs={{0,1},{1,0},{2,3},{3,2},{4,5},{5,4},{6,7},{7,6},{8,9},{9,8},{10,11... | collective-permute-start | bytes 7864328 | tf_op jit(solution)/shard_map/ppermute | solution.py:279
  83.0 55.2 %all-to-all-start = ((bf16[8,6,256,128]{3,2,1,0:T(8,128)(2,1)}), bf16[8,6,256,128]{3,2,1,0:T(8,128)(2,1)}, u32[]{:S(2)}, u32[]{:S(2)}) async-start(bf16[8,6,256,128]{3,2,1,0:T(8,128)(2,1)} %pad_maximum_fusion.2), calls=%async_computation | async-start | bytes 6291456 | tf_op jit(solution)/shard_map/all_to_all | solution.py:267
  92.7 206.0 %all-gather.11.cloned.1.call-start = ((), (), s32[]{:S(2)}) async-start(), calls=%async_computation.7 | async-start | bytes 4325376 | tf_op jit(solution)/shard_map/all_gather | solution.py:265
  202.4 87.6 %all-to-all-start.2 = ((bf16[32,2,4,64,128]{4,3,2,1,0:T(8,128)(2,1)}), bf16[32,2,4,64,128]{4,3,2,1,0:T(8,128)(2,1)}, u32[]{:S(2)}, u32[]{:S(2)}) async-start(bf16[32,2,4,64,128]{4,3,2,1,0:T(8,128)(2,1)} %get-tuple-element.19), calls=%async_computation.2 | async-start | bytes 8388608 | tf_op jit(solution)/shard_map/all_to_all | solution.py:298
  290.0 96.4 %all-to-all-start.3 = ((bf16[32,2,4,64,128]{4,3,2,1,0:T(8,128)(2,1)}), bf16[32,2,4,64,128]{4,3,2,1,0:T(8,128)(2,1)}, u32[]{:S(2)}, u32[]{:S(2)}) async-start(bf16[32,2,4,64,128]{4,3,2,1,0:T(8,128)(2,1)} %get-tuple-element.20), calls=%async_computation.3 | async-start | bytes 8388608 | tf_op jit(solution)/shard_map/all_to_all | solution.py:298
  371.9 32.4 %collective-permute-start.9 = (bf16[2,2,256,128]{3,2,1,0:T(8,128)(2,1)}, bf16[2,2,256,128]{3,2,1,0:T(8,128)(2,1)}, u32[]{:S(2)}, u32[]{:S(2)}) collective-permute-start(bf16[2,2,256,128]{3,2,1,0:T(8,128)(2,1)} %pad_maximum_fusion.9), channel_id=1, source_target_pairs={{0,2},{2,0},{4,6},{6,4},{96,98},{98,96},{100,102},{102,100},{1,3},... | collective-permute-start | bytes 786440 | tf_op jit(solution)/shard_map/ppermute | solution.py:289
  372.6 36.9 %collective-permute-start.11 = (bf16[2,2,256,128]{3,2,1,0:T(8,128)(2,1)}, bf16[2,2,256,128]{3,2,1,0:T(8,128)(2,1)}, u32[]{:S(2)}, u32[]{:S(2)}) collective-permute-start(bf16[2,2,256,128]{3,2,1,0:T(8,128)(2,1)} %pad_maximum_fusion.10), channel_id=1, source_target_pairs={{0,4},{2,6},{4,0},{6,2},{96,100},{98,102},{100,96},{102,98},{1,5},... | collective-permute-start | bytes 786440 | tf_op jit(solution)/shard_map/ppermute | solution.py:289
  373.6 25.6 %collective-permute-start.18 = (bf16[2,256,128]{2,1,0:T(8,128)(2,1)}, bf16[2,256,128]{2,1,0:T(8,128)(2,1)}, u32[]{:S(2)}, u32[]{:S(2)}) collective-permute-start(bf16[2,256,128]{2,1,0:T(8,128)(2,1)} %get-tuple-element.69), channel_id=1, source_target_pairs={{0,98},{2,96},{4,102},{6,100},{96,2},{98,0},{100,6},{102,4},{1,99}... | collective-permute-start | bytes 393224 | tf_op jit(solution)/shard_map/ppermute | solution.py:289
  376.6 23.2 %collective-permute-start.14 = (bf16[2,256,128]{2,1,0:T(8,128)(2,1)}, bf16[2,256,128]{2,1,0:T(8,128)(2,1)}, u32[]{:S(2)}, u32[]{:S(2)}) collective-permute-start(bf16[2,256,128]{2,1,0:T(8,128)(2,1)} %get-tuple-element.71), channel_id=1, source_target_pairs={{0,6},{2,4},{4,2},{6,0},{96,102},{98,100},{100,98},{102,96},{1,7},... | collective-permute-start | bytes 393224 | tf_op jit(solution)/shard_map/ppermute | solution.py:289
  378.6 23.2 %collective-permute-start.10 = (bf16[2,256,128]{2,1,0:T(8,128)(2,1)}, bf16[2,256,128]{2,1,0:T(8,128)(2,1)}, u32[]{:S(2)}, u32[]{:S(2)}) collective-permute-start(bf16[2,256,128]{2,1,0:T(8,128)(2,1)} %get-tuple-element.73), channel_id=1, source_target_pairs={{0,2},{2,0},{4,6},{6,4},{96,98},{98,96},{100,102},{102,100},{1,3},... | collective-permute-start | bytes 393224 | tf_op jit(solution)/shard_map/ppermute | solution.py:289
  386.3 111.0 %all-to-all-start.4 = ((bf16[32,2,4,64,128]{4,3,2,1,0:T(8,128)(2,1)}), bf16[32,2,4,64,128]{4,3,2,1,0:T(8,128)(2,1)}, u32[]{:S(2)}, u32[]{:S(2)}) async-start(bf16[32,2,4,64,128]{4,3,2,1,0:T(8,128)(2,1)} %get-tuple-element.21), calls=%async_computation.4 | async-start | bytes 8388608 | tf_op jit(solution)/shard_map/all_to_all | solution.py:298
  401.8 103.2 %collective-permute-start.23 = (f32[8,2,512,128]{3,2,1,0:T(8,128)}, f32[8,2,512,128]{3,2,1,0:T(8,128)}, u32[]{:S(2)}, u32[]{:S(2)}) collective-permute-start(f32[8,2,512,128]{3,2,1,0:T(8,128)} %bitcast.88), channel_id=1, source_target_pairs={{0,1},{1,0},{2,3},{3,2},{4,5},{5,4},{6,7},{7,6},{8,9},{9,8},{10,11... | collective-permute-start | bytes 12582920 | tf_op jit(solution)/shard_map/ppermute | solution.py:315
  404.3 56.8 %collective-permute-start.15 = (bf16[2,2,256,128]{3,2,1,0:T(8,128)(2,1)S(1)}, bf16[2,2,256,128]{3,2,1,0:T(8,128)(2,1)S(1)}, u32[]{:S(2)}, u32[]{:S(2)}) collective-permute-start(bf16[2,2,256,128]{3,2,1,0:T(8,128)(2,1)S(1)} %pad_maximum_fusion.12), channel_id=1, source_target_pairs={{0,96},{2,98},{4,100},{6,102},{96,0},{98,2},{100,4},{102,6},{1,97}... | collective-permute-start | bytes 786440 | tf_op jit(solution)/shard_map/ppermute | solution.py:289
  407.0 57.0 %collective-permute-start.17 = (bf16[2,2,256,128]{3,2,1,0:T(8,128)(2,1)S(1)}, bf16[2,2,256,128]{3,2,1,0:T(8,128)(2,1)S(1)}, u32[]{:S(2)}, u32[]{:S(2)}) collective-permute-start(bf16[2,2,256,128]{3,2,1,0:T(8,128)(2,1)S(1)} %pad_maximum_fusion.13), channel_id=1, source_target_pairs={{0,98},{2,96},{4,102},{6,100},{96,2},{98,0},{100,6},{102,4},{1,99}... | collective-permute-start | bytes 786440 | tf_op jit(solution)/shard_map/ppermute | solution.py:289
  409.5 50.9 %collective-permute-start.16 = (bf16[2,256,128]{2,1,0:T(8,128)(2,1)S(1)}, bf16[2,256,128]{2,1,0:T(8,128)(2,1)S(1)}, u32[]{:S(2)}, u32[]{:S(2)}) collective-permute-start(bf16[2,256,128]{2,1,0:T(8,128)(2,1)S(1)} %copy-done.11), channel_id=1, source_target_pairs={{0,96},{2,98},{4,100},{6,102},{96,0},{98,2},{100,4},{102,6},{1,97}... | collective-permute-start | bytes 393224 | tf_op jit(solution)/shard_map/ppermute | solution.py:289
  411.5 57.0 %collective-permute-start.19 = (bf16[2,2,256,128]{3,2,1,0:T(8,128)(2,1)S(1)}, bf16[2,2,256,128]{3,2,1,0:T(8,128)(2,1)S(1)}, u32[]{:S(2)}, u32[]{:S(2)}) collective-permute-start(bf16[2,2,256,128]{3,2,1,0:T(8,128)(2,1)S(1)} %pad_maximum_fusion.14), channel_id=1, source_target_pairs={{0,100},{2,102},{4,96},{6,98},{96,4},{98,6},{100,0},{102,2},{1,101... | collective-permute-start | bytes 786440 | tf_op jit(solution)/shard_map/ppermute | solution.py:289
  460.4 16.0 %collective-permute-start.21 = (bf16[2,2,256,128]{3,2,1,0:T(8,128)(2,1)S(1)}, bf16[2,2,256,128]{3,2,1,0:T(8,128)(2,1)S(1)}, u32[]{:S(2)}, u32[]{:S(2)}) collective-permute-start(bf16[2,2,256,128]{3,2,1,0:T(8,128)(2,1)S(1)} %copy-done.8), channel_id=1, source_target_pairs={{0,102},{2,100},{4,98},{6,96},{96,6},{98,4},{100,2},{102,0},{1,103... | collective-permute-start | bytes 786440 | tf_op jit(solution)/shard_map/ppermute | solution.py:289
  508.7 22.0 %collective-permute-start.30 = (bf16[2,512,128]{2,1,0:T(8,128)(2,1)S(1)}, bf16[2,512,128]{2,1,0:T(8,128)(2,1)S(1)}, u32[]{:S(2)}, u32[]{:S(2)}) collective-permute-start(bf16[2,512,128]{2,1,0:T(8,128)(2,1)S(1)} %get-tuple-element.43), channel_id=1, source_target_pairs={{0,102},{2,100},{4,98},{6,96},{96,6},{98,4},{100,2},{102,0},{1,103... | collective-permute-start | bytes 786440 | tf_op jit(solution)/shard_map/ppermute | solution.py:289
  511.6 19.4 %collective-permute-start.29 = (bf16[2,512,128]{2,1,0:T(8,128)(2,1)S(1)}, bf16[2,512,128]{2,1,0:T(8,128)(2,1)S(1)}, u32[]{:S(2)}, u32[]{:S(2)}) collective-permute-start(bf16[2,512,128]{2,1,0:T(8,128)(2,1)S(1)} %get-tuple-element.44), channel_id=1, source_target_pairs={{0,100},{2,102},{4,96},{6,98},{96,4},{98,6},{100,0},{102,2},{1,101... | collective-permute-start | bytes 786440 | tf_op jit(solution)/shard_map/ppermute | solution.py:289
  512.9 20.3 %collective-permute-start.28 = (bf16[2,512,128]{2,1,0:T(8,128)(2,1)S(1)}, bf16[2,512,128]{2,1,0:T(8,128)(2,1)S(1)}, u32[]{:S(2)}, u32[]{:S(2)}) collective-permute-start(bf16[2,512,128]{2,1,0:T(8,128)(2,1)S(1)} %get-tuple-element.45), channel_id=1, source_target_pairs={{0,6},{2,4},{4,2},{6,0},{96,102},{98,100},{100,98},{102,96},{1,7},... | collective-permute-start | bytes 786440 | tf_op jit(solution)/shard_map/ppermute | solution.py:289
  515.0 19.6 %collective-permute-start.27 = (bf16[2,512,128]{2,1,0:T(8,128)(2,1)S(1)}, bf16[2,512,128]{2,1,0:T(8,128)(2,1)S(1)}, u32[]{:S(2)}, u32[]{:S(2)}) collective-permute-start(bf16[2,512,128]{2,1,0:T(8,128)(2,1)S(1)} %get-tuple-element.46), channel_id=1, source_target_pairs={{0,4},{2,6},{4,0},{6,2},{96,100},{98,102},{100,96},{102,98},{1,5},... | collective-permute-start | bytes 786440 | tf_op jit(solution)/shard_map/ppermute | solution.py:289
  520.6 22.2 %collective-permute-start.26 = (bf16[2,512,128]{2,1,0:T(8,128)(2,1)S(1)}, bf16[2,512,128]{2,1,0:T(8,128)(2,1)S(1)}, u32[]{:S(2)}, u32[]{:S(2)}) collective-permute-start(bf16[2,512,128]{2,1,0:T(8,128)(2,1)S(1)} %get-tuple-element.47), channel_id=1, source_target_pairs={{0,98},{2,96},{4,102},{6,100},{96,2},{98,0},{100,6},{102,4},{1,99}... | collective-permute-start | bytes 786440 | tf_op jit(solution)/shard_map/ppermute | solution.py:289
  530.7 28.8 %collective-permute-start.25 = (bf16[2,512,128]{2,1,0:T(8,128)(2,1)S(1)}, bf16[2,512,128]{2,1,0:T(8,128)(2,1)S(1)}, u32[]{:S(2)}, u32[]{:S(2)}) collective-permute-start(bf16[2,512,128]{2,1,0:T(8,128)(2,1)S(1)} %get-tuple-element.48), channel_id=1, source_target_pairs={{0,96},{2,98},{4,100},{6,102},{96,0},{98,2},{100,4},{102,6},{1,97}... | collective-permute-start | bytes 786440 | tf_op jit(solution)/shard_map/ppermute | solution.py:289
  531.0 28.9 %collective-permute-start.42 = (f32[2,2,128,128]{3,2,1,0:T(8,128)S(1)}, f32[2,2,128,128]{3,2,1,0:T(8,128)S(1)}, u32[]{:S(2)}, u32[]{:S(2)}) collective-permute-start(f32[2,2,128,128]{3,2,1,0:T(8,128)S(1)} %pad_maximum_fusion.16), channel_id=1, source_target_pairs={{14,6},{15,7},{22,14},{23,15},{30,22},{31,23},{38,30},{39,31},{46,... | collective-permute-start | bytes 786440 | tf_op jit(solution)/shard_map/ppermute | solution.py:323
  533.3 26.6 %collective-permute-start.41 = (f32[2,2,128,128]{3,2,1,0:T(8,128)S(1)}, f32[2,2,128,128]{3,2,1,0:T(8,128)S(1)}, u32[]{:S(2)}, u32[]{:S(2)}) collective-permute-start(f32[2,2,128,128]{3,2,1,0:T(8,128)S(1)} %pad_maximum_fusion.16), channel_id=1, source_target_pairs={{12,6},{13,7},{20,14},{21,15},{28,22},{29,23},{36,30},{37,31},{44,... | collective-permute-start | bytes 786440 | tf_op jit(solution)/shard_map/ppermute | solution.py:323
  534.6 25.3 %collective-permute-start.40 = (f32[2,2,128,128]{3,2,1,0:T(8,128)S(1)}, f32[2,2,128,128]{3,2,1,0:T(8,128)S(1)}, u32[]{:S(2)}, u32[]{:S(2)}) collective-permute-start(f32[2,2,128,128]{3,2,1,0:T(8,128)S(1)} %pad_maximum_fusion.16), channel_id=1, source_target_pairs={{10,6},{11,7},{18,14},{19,15},{26,22},{27,23},{34,30},{35,31},{42,... | collective-permute-start | bytes 786440 | tf_op jit(solution)/shard_map/ppermute | solution.py:323
  542.7 17.1 %collective-permute-start.39 = (f32[2,2,128,128]{3,2,1,0:T(8,128)S(1)}, f32[2,2,128,128]{3,2,1,0:T(8,128)S(1)}, u32[]{:S(2)}, u32[]{:S(2)}) collective-permute-start(f32[2,2,128,128]{3,2,1,0:T(8,128)S(1)} %pad_maximum_fusion.16), channel_id=1, source_target_pairs={{8,6},{9,7},{16,14},{17,15},{24,22},{25,23},{32,30},{33,31},{40,38... | collective-permute-start | bytes 786440 | tf_op jit(solution)/shard_map/ppermute | solution.py:323
  (34 other events, 394.0 us)
Sparse Core Ops, SparseCore 0:
  20.8 61.7 all-gather.6
  85.5 69.8 all-gather.8
  158.2 45.5 all-gather.10

commit v4 on v3

--- a/solution.py
+++ b/solution.py
@@ -202,7 +202,7 @@
         grid_spec=pltpu.PrefetchScalarGridSpec(
             num_scalar_prefetch=1,
             grid=(8,),
-            in_specs=[qspec(u), qspec(TRIPLE + u), whole(0), whole(1), wspec] + [pl.BlockSpec(memory_space=pl.ANY)] * chained,
+            in_specs=[qspec(max(u - 1, 0)), qspec(u + 1), whole(0), whole(1), wspec] + [pl.BlockSpec(memory_space=pl.ANY)] * chained,
             out_specs=[pl.BlockSpec((1, 2, HALF, 128), lambda t, s: (t ^ s[5], 0, 0, 0)),
                        pl.BlockSpec((32, 2, NX, BLOCK, 128), lambda t, s: (0, 0, 0, 0, 0)),
                        wspec],
@@ -264,7 +264,9 @@
         for u in range(TRIPLE):
             gathered.append(lax.all_gather(mine[:, u].transpose(1, 0, 2, 3), 'cp', axis=0, axis_index_groups=GROUP_ZYC))
 
-        qd_r = a2a(jnp.concatenate([pack(q_rope), pack(d_out)], axis=1), axis_index_groups=GROUP_Q)
+        packed = jnp.stack([pack(q_rope), pack(d_out)], axis=1)
+        qd_0 = a2a(packed[:, :, 0], axis_index_groups=GROUP_Q)
+        qd_12 = a2a(packed[:, :, 1:].reshape(8, 4, HALF, 128), axis_index_groups=GROUP_Q)
 
         piece = jnp.zeros((2, 2, 128, 128), BF16)
         for i in range(NX):
@@ -294,7 +296,7 @@
         for u in range(TRIPLE):
             res = (-1 - (TRIPLE * x + u)) % STRIDE
             info = jnp.stack([4 * zp + y, 4 * (3 - zp) + y, core, half, res, member, 0, 0]).astype(jnp.int32)
-            oq, dkv, dkw = head_attention(info, qd_r, gathered[u], kv_win, dkw, u)
+            oq, dkv, dkw = head_attention(info, qd_12 if u else qd_0, gathered[u], kv_win, dkw, u)
             back = a2a(dkv, axis_index_groups=GROUP_ZYC)
             str_sum.append(jnp.sum(back, axis=0, dtype=F32))
             outs.append(oq)
@@ -305,21 +307,18 @@
         both = jnp.stack([lax.dynamic_index_in_dim(both, member ^ j, axis=0, keepdims=False) for j in range(8)])
         both = both.reshape(2, NX, TRIPLE, 2, HALF, 128).transpose(3, 0, 4, 1, 2, 5).reshape(2, RUN, 12, 128)
 
-        def core_body(c):
-            return lax.dynamic_index_in_dim(dkw[:, :, HALO:].reshape(2, 2, NX, 2, RUN, 128), c, axis=3, keepdims=False).transpose(0, 2, 1, 3, 4)
-
-        def core_head(c):
-            return lax.dynamic_index_in_dim(dkw[:, :, :HALO].reshape(2, 2, 2, NX, 128, 128), c, axis=2, keepdims=False).transpose(0, 2, 1, 3, 4)
-
-        def owners(part, rows):
-            other = lax.ppermute(part(1 - core).reshape(8, 2, rows, 128), 'cp', mate)
-            total = (part(core).reshape(8, 2, rows, 128) + other).astype(BF16)
+        by_pair = dkw.reshape(2, 2, 5, 2, RUN, 128)
+
+        other = lax.ppermute(lax.dynamic_index_in_dim(by_pair, 1 - core, axis=3, keepdims=False), 'cp', mate)
+        total = (lax.dynamic_index_in_dim(by_pair, core, axis=3, keepdims=False) + other).astype(BF16)
+
+        def owners(total):
             got = swap([lax.dynamic_index_in_dim(total, member ^ k, axis=0, keepdims=False) for k in range(8)])
             same, cross = [sum(got[k].astype(F32) for k in range(8) if k // 2 % 2 == n) for n in range(2)]
             return jnp.stack([jnp.where(g_kv == 0, same, cross), jnp.where(g_kv == 0, cross, same)])
 
-        head_sum = owners(core_head, 128)
-        grads = owners(core_body, RUN)
+        head_sum = owners(total[:, :, 0].reshape(2, 2, NX, 128, 128).transpose(0, 2, 1, 3, 4).reshape(8, 2, 128, 128))
+        grads = owners(total[:, :, 1:].transpose(0, 2, 1, 3, 4).reshape(8, 2, RUN, 128))
         pieces = [lax.ppermute(head_sum, 'cp', halo_pairs(i, True)) for i in range(NX)]
         grads = grads + jnp.concatenate(pieces, axis=2)
 

time: 578 us -> 537 us (0.929)
  the two profiles are of different devices: /device:TPU:62 before, /device:TPU:31 now
where the time goes in v4:
time: 537 us; the launch traced here: 531 us
  Pallas kernels  197 us (37%)
  waiting for transfers between devices  144 us (27%)
  starting transfers between devices  117 us (22%)
  other arithmetic  26 us (5%)
  local copies, waits for them, and re-layouts  22.8 us (4%)
  between operations  15.1 us (3%)
  blocking collectives  9.44 us (2%)
    pallas_call x3, Pallas kernels, head_attention(): pl.pallas_call(functools.partial(attn_kernel, chained), grid_spec=pltpu.P...  197 us
    ppermute x28, waiting for transfers between devices, swap(): lax.ppermute(parts[k], 'cp', [(g[m], g[m ^ k]) for g in GROUP_Q for m in...  77.4 us
    ppermute x28, starting transfers between devices, swap(): lax.ppermute(parts[k], 'cp', [(g[m], g[m ^ k]) for g in GROUP_Q for m in...  38.6 us
    ppermute x3, waiting for transfers between devices, layer(): lax.ppermute(two, 'cp', [(g[m], g[m ^ k]) for g in GROUP_WG for m in rang...  26.5 us
    all_to_all x3, starting transfers between devices, layer(): back = a2a(dkv, axis_index_groups=GROUP_ZYC)  26.2 us
    ppermute x4, waiting for transfers between devices, layer(): lax.ppermute(head_sum, 'cp', halo_pairs(i, True))  20.1 us
    all_to_all x1, starting transfers between devices, layer(): qd_0 = a2a(packed[:, :, 0], axis_index_groups=GROUP_Q)  12 us
  transfers between devices with their start and end apart: 53, of which 24 were waited for; matrix products, arithmetic and copies ran while one was open for 8% of the time, Pallas kernels for 37%

profile of v4, /device:TPU:31, one launch (start us, length us, event | category | flops | bytes accessed | tf_op | source)
XLA Modules:
  0.0 531.5 jit_solution(11317472886666015656)
XLA Ops:
  9.4 9.4 %all_to_all.30 = bf16[4,3,2,64,128]{4,3,2,1,0:T(8,128)(2,1)S(1)} all-to-all(bf16[4,3,2,64,128]{4,3,2,1,0:T(8,128)(2,1)S(1)} %pad_maximum_fusion.8), channel_id=1, replica_groups={{0,2,4,6},{1,3,5,7},{8,10,12,14},{9,11,13,15},{16,18,20,22},{17,19,21,2..., dimensions={0} | all-to-all | bytes 786432 | tf_op jit(solution)/shard_map/all_to_all | solution.py:260
  20.3 4.7 collective-permute-start.1
  33.0 7.8 %collective-permute-done.4 = bf16[2,640,128]{2,1,0:T(8,128)(2,1)S(1)} collective-permute-done((bf16[2,640,128]{2,1,0:T(8,128)(2,1)S(1)}, bf16[2,640,128]{2,1,0:T(8,128)(2,1)S(1)}, u32[]{:S(2)}, u32[]{:S(2)}) %collective-permute-start.4) | collective-permute-done | bytes 327712 | tf_op jit(solution)/shard_map/ppermute | solution.py:276
  45.0 9.8 %collective-permute-done.6 = bf16[2,2,640,128]{3,2,1,0:T(8,128)(2,1)S(1)} collective-permute-done((bf16[2,2,640,128]{3,2,1,0:T(8,128)(2,1)S(1)}, bf16[2,2,640,128]{3,2,1,0:T(8,128)(2,1)S(1)}, u32[]{:S(2)}, u32[]{:S(2)}) %collective-permute-start.6) | collective-permute-done | bytes 655392 | tf_op jit(solution)/shard_map/ppermute | solution.py:279
  55.9 15.6 %collective-permute-done.7 = bf16[2,2,640,128]{3,2,1,0:T(8,128)(2,1)S(1)} collective-permute-done((bf16[2,2,640,128]{3,2,1,0:T(8,128)(2,1)S(1)}, bf16[2,2,640,128]{3,2,1,0:T(8,128)(2,1)S(1)}, u32[]{:S(2)}, u32[]{:S(2)}) %collective-permute-start.7) | collective-permute-done | bytes 655392 | tf_op jit(solution)/shard_map/ppermute | solution.py:279
  74.1 5.4 %collective-permute-start.8 = (bf16[4,2,2,640,128]{4,3,2,1,0:T(8,128)(2,1)}, bf16[4,2,2,640,128]{4,3,2,1,0:T(8,128)(2,1)}, u32[]{:S(2)}, u32[]{:S(2)}) collective-permute-start(bf16[4,2,2,640,128]{4,3,2,1,0:T(8,128)(2,1)} %pad_maximum_fusion.3), channel_id=1, source_target_pairs={{0,1},{1,0},{2,3},{3,2},{4,5},{5,4},{6,7},{7,6},{8,9},{9,8},{10,11... | collective-permute-start | bytes 7864328 | tf_op jit(solution)/shard_map/ppermute | solution.py:281
  80.8 12.0 %all-to-all-start = ((bf16[8,2,256,128]{3,2,1,0:T(8,128)(2,1)}), bf16[8,2,256,128]{3,2,1,0:T(8,128)(2,1)}, u32[]{:S(2)}, u32[]{:S(2)}) async-start(bf16[8,2,256,128]{3,2,1,0:T(8,128)(2,1)} %maximum_bitcast_fusion.1), calls=%async_computation | async-start | bytes 2097152 | tf_op jit(solution)/shard_map/all_to_all | solution.py:268
  100.8 4.0 all-to-all-done.q_ref.do_ref
  104.8 9.7 %all-to-all-start.2 = ((bf16[8,4,256,128]{3,2,1,0:T(8,128)(2,1)}), bf16[8,4,256,128]{3,2,1,0:T(8,128)(2,1)}, u32[]{:S(2)}, u32[]{:S(2)}) async-start(bf16[8,4,256,128]{3,2,1,0:T(8,128)(2,1)} %bitcast.49), calls=%async_computation.2 | async-start | bytes 4194304 | tf_op jit(solution)/shard_map/all_to_all | solution.py:269
  114.6 4.9 pad_maximum_fusion.kw_ref
  119.5 63.8 %head_attention.3 = (bf16[8,2,256,128]{3,2,1,0:T(8,128)(2,1)}, bf16[32,2,4,64,128]{4,3,2,1,0:T(8,128)(2,1)}, f32[2,2,5120,128]{3,2,1,0:T(8,128)}) custom-call(s32[8]{0:T(128)} %stack.233.info, bf16[8,2,256,128]{3,2,1,0:T(8,128)(2,1)} %all-to-all-done.q_ref.do_ref, bf16[8,2,256,128]{3,2,1,0:T(8,128)(2,1)} %all-to-all-done.q_ref.do_ref, ...), custom_call_target="tpu_custom_call" | custom-call | flops 16986931200 | bytes 41943040 | tf_op jit(solution)/shard_map/head_attention/pallas_call | solution.py:200
  183.3 11.2 %all-to-all-start.3 = ((bf16[32,2,4,64,128]{4,3,2,1,0:T(8,128)(2,1)}), bf16[32,2,4,64,128]{4,3,2,1,0:T(8,128)(2,1)}, u32[]{:S(2)}, u32[]{:S(2)}) async-start(bf16[32,2,4,64,128]{4,3,2,1,0:T(8,128)(2,1)} %get-tuple-element.19), calls=%async_computation.3 | async-start | bytes 8388608 | tf_op jit(solution)/shard_map/all_to_all | solution.py:300
  195.1 66.7 %head_attention.4 = (bf16[8,2,256,128]{3,2,1,0:T(8,128)(2,1)}, bf16[32,2,4,64,128]{4,3,2,1,0:T(8,128)(2,1)}, f32[2,2,5120,128]{3,2,1,0:T(8,128)}) custom-call(s32[8]{0:T(128)} %stack.258.info, bf16[8,4,256,128]{3,2,1,0:T(8,128)(2,1)} %all-to-all-done.2.q_ref.do_ref, bf16[8,4,256,128]{3,2,1,0:T(8,128)(2,1)} %all-to-all-done.2.q_ref.do_ref, ...), custom_call_target="tpu_custom_call" | custom-call | flops 16986931200 | bytes 41943040 | tf_op jit(solution)/shard_map/head_attention/pallas_call | solution.py:200
  261.9 7.7 %all-to-all-start.4 = ((bf16[32,2,4,64,128]{4,3,2,1,0:T(8,128)(2,1)}), bf16[32,2,4,64,128]{4,3,2,1,0:T(8,128)(2,1)}, u32[]{:S(2)}, u32[]{:S(2)}) async-start(bf16[32,2,4,64,128]{4,3,2,1,0:T(8,128)(2,1)} %get-tuple-element.20), calls=%async_computation.4 | async-start | bytes 8388608 | tf_op jit(solution)/shard_map/all_to_all | solution.py:300
  271.1 66.6 %head_attention.5 = (bf16[8,2,256,128]{3,2,1,0:T(8,128)(2,1)}, bf16[32,2,4,64,128]{4,3,2,1,0:T(8,128)(2,1)}, f32[2,2,5120,128]{3,2,1,0:T(8,128)}) custom-call(s32[8]{0:T(128)} %stack.260.info, bf16[8,4,256,128]{3,2,1,0:T(8,128)(2,1)} %all-to-all-done.2.q_ref.do_ref, bf16[8,4,256,128]{3,2,1,0:T(8,128)(2,1)} %all-to-all-done.2.q_ref.do_ref, ...), custom_call_target="tpu_custom_call" | custom-call | flops 16986931200 | bytes 41943040 | tf_op jit(solution)/shard_map/head_attention/pallas_call | solution.py:200
  337.7 7.3 %all-to-all-start.5 = ((bf16[32,2,4,64,128]{4,3,2,1,0:T(8,128)(2,1)}), bf16[32,2,4,64,128]{4,3,2,1,0:T(8,128)(2,1)}, u32[]{:S(2)}, u32[]{:S(2)}) async-start(bf16[32,2,4,64,128]{4,3,2,1,0:T(8,128)(2,1)} %get-tuple-element.21), calls=%async_computation.5 | async-start | bytes 8388608 | tf_op jit(solution)/shard_map/all_to_all | solution.py:300
  345.9 5.4 %dynamic-slice_bitcast_fusion = f32[2,2,5,512,128]{4,3,2,1,0:T(8,128)} fusion(f32[2,2,5,2,512,128]{5,4,3,2,1,0:T(8,128)} %bitcast.319, s32[]{:T(128)S(6)} %select_n.221), kind=kLoop, calls=%fused_computation.6 | loop fusion | bytes 10485764 | tf_op jit(solution)/shard_map/jit(dynamic_index_in_dim)/squeeze | solution.py:312
  356.2 7.7 %collective-permute-done.18 = bf16[2,256,128]{2,1,0:T(8,128)(2,1)S(1)} collective-permute-done((bf16[2,256,128]{2,1,0:T(8,128)(2,1)S(1)}, bf16[2,256,128]{2,1,0:T(8,128)(2,1)S(1)}, u32[]{:S(2)}, u32[]{:S(2)}) %collective-permute-start.18) | collective-permute-done | bytes 131104 | tf_op jit(solution)/shard_map/ppermute | solution.py:291
  370.3 4.0 collective-permute-done.12
  377.8 4.4 collective-permute-done.13
  382.2 3.4 collective-permute-start.19
  385.7 30.0 %collective-permute-done.16 = bf16[2,256,128]{2,1,0:T(8,128)(2,1)S(1)} collective-permute-done((bf16[2,256,128]{2,1,0:T(8,128)(2,1)S(1)}, bf16[2,256,128]{2,1,0:T(8,128)(2,1)S(1)}, u32[]{:S(2)}, u32[]{:S(2)}) %collective-permute-start.16) | collective-permute-done | bytes 131104 | tf_op jit(solution)/shard_map/ppermute | solution.py:291
  415.8 4.4 collective-permute-start.20
  423.4 9.0 %collective-permute-done.22 = bf16[2,256,128]{2,1,0:T(8,128)(2,1)S(1)} collective-permute-done((bf16[2,256,128]{2,1,0:T(8,128)(2,1)S(1)}, bf16[2,256,128]{2,1,0:T(8,128)(2,1)S(1)}, u32[]{:S(2)}, u32[]{:S(2)}) %collective-permute-start.22) | collective-permute-done | bytes 131104 | tf_op jit(solution)/shard_map/ppermute | solution.py:291
  436.2 3.9 convert_reduce_fusion.1
  449.7 5.8 %collective-permute-done.44 = f32[3,2,64,128]{3,2,1,0:T(8,128)S(1)} collective-permute-done((f32[3,2,64,128]{3,2,1,0:T(8,128)S(1)}, f32[3,2,64,128]{3,2,1,0:T(8,128)S(1)}, u32[]{:S(2)}, u32[]{:S(2)}) %collective-permute-start.44) | collective-permute-done | bytes 196640 | tf_op jit(solution)/shard_map/ppermute | solution.py:327
  461.1 4.9 collective-permute-start.37
  466.3 5.3 collective-permute-done.37
  489.1 9.1 %collective-permute-done.28 = bf16[2,512,128]{2,1,0:T(8,128)(2,1)S(1)} collective-permute-done((bf16[2,512,128]{2,1,0:T(8,128)(2,1)S(1)}, bf16[2,512,128]{2,1,0:T(8,128)(2,1)S(1)}, u32[]{:S(2)}, u32[]{:S(2)}) %collective-permute-start.28) | collective-permute-done | bytes 262176 | tf_op jit(solution)/shard_map/ppermute | solution.py:291
  502.4 8.6 %collective-permute-done.40 = f32[2,2,128,128]{3,2,1,0:T(8,128)S(1)} collective-permute-done((f32[2,2,128,128]{3,2,1,0:T(8,128)S(1)}, f32[2,2,128,128]{3,2,1,0:T(8,128)S(1)}, u32[]{:S(2)}, u32[]{:S(2)}) %collective-permute-start.40) | collective-permute-done | bytes 262176 | tf_op jit(solution)/shard_map/ppermute | solution.py:322
  511.1 4.2 collective-permute-done.39
  515.3 7.2 %collective-permute-done.38 = f32[2,2,128,128]{3,2,1,0:T(8,128)S(1)} collective-permute-done((f32[2,2,128,128]{3,2,1,0:T(8,128)S(1)}, f32[2,2,128,128]{3,2,1,0:T(8,128)S(1)}, u32[]{:S(2)}, u32[]{:S(2)}) %collective-permute-start.38) | collective-permute-done | bytes 262176 | tf_op jit(solution)/shard_map/ppermute | solution.py:322
  (211 shorter events, 92.3 us)
Async XLA Ops:
  7.2 112.3 %all-gather.7.cloned.1.call-start = ((), (), s32[]{:S(2)}) async-start(), calls=%async_computation.6 | async-start | bytes 4325376 | tf_op jit(solution)/shard_map/all_gather | solution.py:265
  19.5 175.6 %all-gather.9.cloned.1.call-start = ((), (), s32[]{:S(2)}) async-start(), calls=%async_computation.7 | async-start | bytes 4325376 | tf_op jit(solution)/shard_map/all_gather | solution.py:265
  41.0 13.8 %collective-permute-start.6 = (bf16[2,2,640,128]{3,2,1,0:T(8,128)(2,1)S(1)}, bf16[2,2,640,128]{3,2,1,0:T(8,128)(2,1)S(1)}, u32[]{:S(2)}, u32[]{:S(2)}) collective-permute-start(bf16[2,2,640,128]{3,2,1,0:T(8,128)(2,1)S(1)} %get-tuple-element.88), channel_id=1, source_target_pairs={{0,96},{2,98},{96,0},{98,2},{1,97},{3,99},{97,1},{99,3},{4,100},{6... | collective-permute-start | bytes 1966088 | tf_op jit(solution)/shard_map/ppermute | solution.py:279
  41.5 14.4 %collective-permute-start.5 = (bf16[2,2,640,128]{3,2,1,0:T(8,128)(2,1)S(1)}, bf16[2,2,640,128]{3,2,1,0:T(8,128)(2,1)S(1)}, u32[]{:S(2)}, u32[]{:S(2)}) collective-permute-start(bf16[2,2,640,128]{3,2,1,0:T(8,128)(2,1)S(1)} %get-tuple-element.88), channel_id=1, source_target_pairs={{0,2},{2,0},{96,98},{98,96},{1,3},{3,1},{97,99},{99,97},{4,6},{6,4... | collective-permute-start | bytes 1966088 | tf_op jit(solution)/shard_map/ppermute | solution.py:279
  44.6 26.9 %collective-permute-start.7 = (bf16[2,2,640,128]{3,2,1,0:T(8,128)(2,1)S(1)}, bf16[2,2,640,128]{3,2,1,0:T(8,128)(2,1)S(1)}, u32[]{:S(2)}, u32[]{:S(2)}) collective-permute-start(bf16[2,2,640,128]{3,2,1,0:T(8,128)(2,1)S(1)} %get-tuple-element.88), channel_id=1, source_target_pairs={{0,98},{2,96},{96,2},{98,0},{1,99},{3,97},{97,3},{99,1},{4,102},{6... | collective-permute-start | bytes 1966088 | tf_op jit(solution)/shard_map/ppermute | solution.py:279
  74.1 21.7 %collective-permute-start.8 = (bf16[4,2,2,640,128]{4,3,2,1,0:T(8,128)(2,1)}, bf16[4,2,2,640,128]{4,3,2,1,0:T(8,128)(2,1)}, u32[]{:S(2)}, u32[]{:S(2)}) collective-permute-start(bf16[4,2,2,640,128]{4,3,2,1,0:T(8,128)(2,1)} %pad_maximum_fusion.3), channel_id=1, source_target_pairs={{0,1},{1,0},{2,3},{3,2},{4,5},{5,4},{6,7},{7,6},{8,9},{9,8},{10,11... | collective-permute-start | bytes 7864328 | tf_op jit(solution)/shard_map/ppermute | solution.py:281
  80.8 24.0 %all-to-all-start = ((bf16[8,2,256,128]{3,2,1,0:T(8,128)(2,1)}), bf16[8,2,256,128]{3,2,1,0:T(8,128)(2,1)}, u32[]{:S(2)}, u32[]{:S(2)}) async-start(bf16[8,2,256,128]{3,2,1,0:T(8,128)(2,1)} %maximum_bitcast_fusion.1), calls=%async_computation | async-start | bytes 2097152 | tf_op jit(solution)/shard_map/all_to_all | solution.py:268
  92.8 178.3 %all-gather.11.cloned.1.call-start = ((), (), s32[]{:S(2)}) async-start(), calls=%async_computation.8 | async-start | bytes 4325376 | tf_op jit(solution)/shard_map/all_gather | solution.py:265
  104.8 78.5 %all-to-all-start.2 = ((bf16[8,4,256,128]{3,2,1,0:T(8,128)(2,1)}), bf16[8,4,256,128]{3,2,1,0:T(8,128)(2,1)}, u32[]{:S(2)}, u32[]{:S(2)}) async-start(bf16[8,4,256,128]{3,2,1,0:T(8,128)(2,1)} %bitcast.49), calls=%async_computation.2 | async-start | bytes 4194304 | tf_op jit(solution)/shard_map/all_to_all | solution.py:269
  183.3 78.6 %all-to-all-start.3 = ((bf16[32,2,4,64,128]{4,3,2,1,0:T(8,128)(2,1)}), bf16[32,2,4,64,128]{4,3,2,1,0:T(8,128)(2,1)}, u32[]{:S(2)}, u32[]{:S(2)}) async-start(bf16[32,2,4,64,128]{4,3,2,1,0:T(8,128)(2,1)} %get-tuple-element.19), calls=%async_computation.3 | async-start | bytes 8388608 | tf_op jit(solution)/shard_map/all_to_all | solution.py:300
  261.9 75.8 %all-to-all-start.4 = ((bf16[32,2,4,64,128]{4,3,2,1,0:T(8,128)(2,1)}), bf16[32,2,4,64,128]{4,3,2,1,0:T(8,128)(2,1)}, u32[]{:S(2)}, u32[]{:S(2)}) async-start(bf16[32,2,4,64,128]{4,3,2,1,0:T(8,128)(2,1)} %get-tuple-element.20), calls=%async_computation.4 | async-start | bytes 8388608 | tf_op jit(solution)/shard_map/all_to_all | solution.py:300
  337.7 102.3 %all-to-all-start.5 = ((bf16[32,2,4,64,128]{4,3,2,1,0:T(8,128)(2,1)}), bf16[32,2,4,64,128]{4,3,2,1,0:T(8,128)(2,1)}, u32[]{:S(2)}, u32[]{:S(2)}) async-start(bf16[32,2,4,64,128]{4,3,2,1,0:T(8,128)(2,1)} %get-tuple-element.21), calls=%async_computation.5 | async-start | bytes 8388608 | tf_op jit(solution)/shard_map/all_to_all | solution.py:300
  345.2 22.1 %collective-permute-start.9 = (bf16[2,2,256,128]{3,2,1,0:T(8,128)(2,1)S(1)}, bf16[2,2,256,128]{3,2,1,0:T(8,128)(2,1)S(1)}, u32[]{:S(2)}, u32[]{:S(2)}) collective-permute-start(bf16[2,2,256,128]{3,2,1,0:T(8,128)(2,1)S(1)} %pad_maximum_fusion.9), channel_id=1, source_target_pairs={{0,2},{2,0},{4,6},{6,4},{96,98},{98,96},{100,102},{102,100},{1,3},... | collective-permute-start | bytes 786440 | tf_op jit(solution)/shard_map/ppermute | solution.py:291
  351.3 104.4 %collective-permute-start.23 = (f32[2,2,5,512,128]{4,3,2,1,0:T(8,128)}, f32[2,2,5,512,128]{4,3,2,1,0:T(8,128)}, u32[]{:S(2)}, u32[]{:S(2)}) collective-permute-start(f32[2,2,5,512,128]{4,3,2,1,0:T(8,128)} %dynamic-slice_bitcast_fusion), channel_id=1, source_target_pairs={{0,1},{1,0},{2,3},{3,2},{4,5},{5,4},{6,7},{7,6},{8,9},{9,8},{10,11... | collective-permute-start | bytes 15728648 | tf_op jit(solution)/shard_map/ppermute | solution.py:312
  363.9 13.8 %collective-permute-start.11 = (bf16[2,2,256,128]{3,2,1,0:T(8,128)(2,1)S(1)}, bf16[2,2,256,128]{3,2,1,0:T(8,128)(2,1)S(1)}, u32[]{:S(2)}, u32[]{:S(2)}) collective-permute-start(bf16[2,2,256,128]{3,2,1,0:T(8,128)(2,1)S(1)} %pad_maximum_fusion.10), channel_id=1, source_target_pairs={{0,4},{2,6},{4,0},{6,2},{96,100},{98,102},{100,96},{102,98},{1,5},... | collective-permute-start | bytes 786440 | tf_op jit(solution)/shard_map/ppermute | solution.py:291
  364.7 17.5 %collective-permute-start.13 = (bf16[2,2,256,128]{3,2,1,0:T(8,128)(2,1)S(1)}, bf16[2,2,256,128]{3,2,1,0:T(8,128)(2,1)S(1)}, u32[]{:S(2)}, u32[]{:S(2)}) collective-permute-start(bf16[2,2,256,128]{3,2,1,0:T(8,128)(2,1)S(1)} %pad_maximum_fusion.11), channel_id=1, source_target_pairs={{0,6},{2,4},{4,2},{6,0},{96,102},{98,100},{100,98},{102,96},{1,7},... | collective-permute-start | bytes 786440 | tf_op jit(solution)/shard_map/ppermute | solution.py:291
  367.3 48.5 %collective-permute-start.15 = (bf16[2,2,256,128]{3,2,1,0:T(8,128)(2,1)S(1)}, bf16[2,2,256,128]{3,2,1,0:T(8,128)(2,1)S(1)}, u32[]{:S(2)}, u32[]{:S(2)}) collective-permute-start(bf16[2,2,256,128]{3,2,1,0:T(8,128)(2,1)S(1)} %pad_maximum_fusion.12), channel_id=1, source_target_pairs={{0,96},{2,98},{4,100},{6,102},{96,0},{98,2},{100,4},{102,6},{1,97}... | collective-permute-start | bytes 786440 | tf_op jit(solution)/shard_map/ppermute | solution.py:291
  374.3 45.9 %collective-permute-start.17 = (bf16[2,2,256,128]{3,2,1,0:T(8,128)(2,1)S(1)}, bf16[2,2,256,128]{3,2,1,0:T(8,128)(2,1)S(1)}, u32[]{:S(2)}, u32[]{:S(2)}) collective-permute-start(bf16[2,2,256,128]{3,2,1,0:T(8,128)(2,1)S(1)} %pad_maximum_fusion.13), channel_id=1, source_target_pairs={{0,98},{2,96},{4,102},{6,100},{96,2},{98,0},{100,6},{102,4},{1,99}... | collective-permute-start | bytes 786440 | tf_op jit(solution)/shard_map/ppermute | solution.py:291
  377.7 38.0 %collective-permute-start.16 = (bf16[2,256,128]{2,1,0:T(8,128)(2,1)S(1)}, bf16[2,256,128]{2,1,0:T(8,128)(2,1)S(1)}, u32[]{:S(2)}, u32[]{:S(2)}) collective-permute-start(bf16[2,256,128]{2,1,0:T(8,128)(2,1)S(1)} %get-tuple-element.66), channel_id=1, source_target_pairs={{0,96},{2,98},{4,100},{6,102},{96,0},{98,2},{100,4},{102,6},{1,97}... | collective-permute-start | bytes 393224 | tf_op jit(solution)/shard_map/ppermute | solution.py:291
  382.2 41.2 %collective-permute-start.19 = (bf16[2,2,256,128]{3,2,1,0:T(8,128)(2,1)S(1)}, bf16[2,2,256,128]{3,2,1,0:T(8,128)(2,1)S(1)}, u32[]{:S(2)}, u32[]{:S(2)}) collective-permute-start(bf16[2,2,256,128]{3,2,1,0:T(8,128)(2,1)S(1)} %pad_maximum_fusion.14), channel_id=1, source_target_pairs={{0,100},{2,102},{4,96},{6,98},{96,4},{98,6},{100,0},{102,2},{1,101... | collective-permute-start | bytes 786440 | tf_op jit(solution)/shard_map/ppermute | solution.py:291
  415.7 16.7 %collective-permute-start.21 = (bf16[2,2,256,128]{3,2,1,0:T(8,128)(2,1)S(1)}, bf16[2,2,256,128]{3,2,1,0:T(8,128)(2,1)S(1)}, u32[]{:S(2)}, u32[]{:S(2)}) collective-permute-start(bf16[2,2,256,128]{3,2,1,0:T(8,128)(2,1)S(1)} %pad_maximum_fusion.15), channel_id=1, source_target_pairs={{0,102},{2,100},{4,98},{6,96},{96,6},{98,4},{100,2},{102,0},{1,103... | collective-permute-start | bytes 786440 | tf_op jit(solution)/shard_map/ppermute | solution.py:291
  420.2 12.2 %collective-permute-start.22 = (bf16[2,256,128]{2,1,0:T(8,128)(2,1)S(1)}, bf16[2,256,128]{2,1,0:T(8,128)(2,1)S(1)}, u32[]{:S(2)}, u32[]{:S(2)}) collective-permute-start(bf16[2,256,128]{2,1,0:T(8,128)(2,1)S(1)} %get-tuple-element.63), channel_id=1, source_target_pairs={{0,102},{2,100},{4,98},{6,96},{96,6},{98,4},{100,2},{102,0},{1,103... | collective-permute-start | bytes 393224 | tf_op jit(solution)/shard_map/ppermute | solution.py:291
  459.6 21.5 %collective-permute-start.24 = (bf16[2,512,128]{2,1,0:T(8,128)(2,1)S(1)}, bf16[2,512,128]{2,1,0:T(8,128)(2,1)S(1)}, u32[]{:S(2)}, u32[]{:S(2)}) collective-permute-start(bf16[2,512,128]{2,1,0:T(8,128)(2,1)S(1)} %get-tuple-element.40), channel_id=1, source_target_pairs={{0,2},{2,0},{4,6},{6,4},{96,98},{98,96},{100,102},{102,100},{1,3},... | collective-permute-start | bytes 786440 | tf_op jit(solution)/shard_map/ppermute | solution.py:291
  461.1 21.1 %collective-permute-start.30 = (bf16[2,512,128]{2,1,0:T(8,128)(2,1)S(1)}, bf16[2,512,128]{2,1,0:T(8,128)(2,1)S(1)}, u32[]{:S(2)}, u32[]{:S(2)}) collective-permute-start(bf16[2,512,128]{2,1,0:T(8,128)(2,1)S(1)} %get-tuple-element.41), channel_id=1, source_target_pairs={{0,102},{2,100},{4,98},{6,96},{96,6},{98,4},{100,2},{102,0},{1,103... | collective-permute-start | bytes 786440 | tf_op jit(solution)/shard_map/ppermute | solution.py:291
  478.0 20.2 %collective-permute-start.28 = (bf16[2,512,128]{2,1,0:T(8,128)(2,1)S(1)}, bf16[2,512,128]{2,1,0:T(8,128)(2,1)S(1)}, u32[]{:S(2)}, u32[]{:S(2)}) collective-permute-start(bf16[2,512,128]{2,1,0:T(8,128)(2,1)S(1)} %get-tuple-element.43), channel_id=1, source_target_pairs={{0,6},{2,4},{4,2},{6,0},{96,102},{98,100},{100,98},{102,96},{1,7},... | collective-permute-start | bytes 786440 | tf_op jit(solution)/shard_map/ppermute | solution.py:291
  479.0 20.5 %collective-permute-start.27 = (bf16[2,512,128]{2,1,0:T(8,128)(2,1)S(1)}, bf16[2,512,128]{2,1,0:T(8,128)(2,1)S(1)}, u32[]{:S(2)}, u32[]{:S(2)}) collective-permute-start(bf16[2,512,128]{2,1,0:T(8,128)(2,1)S(1)} %get-tuple-element.44), channel_id=1, source_target_pairs={{0,4},{2,6},{4,0},{6,2},{96,100},{98,102},{100,96},{102,98},{1,5},... | collective-permute-start | bytes 786440 | tf_op jit(solution)/shard_map/ppermute | solution.py:291
  481.1 19.7 %collective-permute-start.26 = (bf16[2,512,128]{2,1,0:T(8,128)(2,1)S(1)}, bf16[2,512,128]{2,1,0:T(8,128)(2,1)S(1)}, u32[]{:S(2)}, u32[]{:S(2)}) collective-permute-start(bf16[2,512,128]{2,1,0:T(8,128)(2,1)S(1)} %get-tuple-element.45), channel_id=1, source_target_pairs={{0,98},{2,96},{4,102},{6,100},{96,2},{98,0},{100,6},{102,4},{1,99}... | collective-permute-start | bytes 786440 | tf_op jit(solution)/shard_map/ppermute | solution.py:291
  482.2 19.9 %collective-permute-start.25 = (bf16[2,512,128]{2,1,0:T(8,128)(2,1)S(1)}, bf16[2,512,128]{2,1,0:T(8,128)(2,1)S(1)}, u32[]{:S(2)}, u32[]{:S(2)}) collective-permute-start(bf16[2,512,128]{2,1,0:T(8,128)(2,1)S(1)} %get-tuple-element.46), channel_id=1, source_target_pairs={{0,96},{2,98},{4,100},{6,102},{96,0},{98,2},{100,4},{102,6},{1,97}... | collective-permute-start | bytes 786440 | tf_op jit(solution)/shard_map/ppermute | solution.py:291
  486.1 16.4 %collective-permute-start.41 = (f32[2,2,128,128]{3,2,1,0:T(8,128)S(1)}, f32[2,2,128,128]{3,2,1,0:T(8,128)S(1)}, u32[]{:S(2)}, u32[]{:S(2)}) collective-permute-start(f32[2,2,128,128]{3,2,1,0:T(8,128)S(1)} %pad_maximum_fusion.16), channel_id=1, source_target_pairs={{14,6},{15,7},{22,14},{23,15},{30,22},{31,23},{38,30},{39,31},{46,... | collective-permute-start | bytes 786440 | tf_op jit(solution)/shard_map/ppermute | solution.py:322
  498.2 12.9 %collective-permute-start.40 = (f32[2,2,128,128]{3,2,1,0:T(8,128)S(1)}, f32[2,2,128,128]{3,2,1,0:T(8,128)S(1)}, u32[]{:S(2)}, u32[]{:S(2)}) collective-permute-start(f32[2,2,128,128]{3,2,1,0:T(8,128)S(1)} %pad_maximum_fusion.16), channel_id=1, source_target_pairs={{12,6},{13,7},{20,14},{21,15},{28,22},{29,23},{36,30},{37,31},{44,... | collective-permute-start | bytes 786440 | tf_op jit(solution)/shard_map/ppermute | solution.py:322
  499.5 15.8 %collective-permute-start.39 = (f32[2,2,128,128]{3,2,1,0:T(8,128)S(1)}, f32[2,2,128,128]{3,2,1,0:T(8,128)S(1)}, u32[]{:S(2)}, u32[]{:S(2)}) collective-permute-start(f32[2,2,128,128]{3,2,1,0:T(8,128)S(1)} %pad_maximum_fusion.16), channel_id=1, source_target_pairs={{10,6},{11,7},{18,14},{19,15},{26,22},{27,23},{34,30},{35,31},{42,... | collective-permute-start | bytes 786440 | tf_op jit(solution)/shard_map/ppermute | solution.py:322
  500.8 21.7 %collective-permute-start.38 = (f32[2,2,128,128]{3,2,1,0:T(8,128)S(1)}, f32[2,2,128,128]{3,2,1,0:T(8,128)S(1)}, u32[]{:S(2)}, u32[]{:S(2)}) collective-permute-start(f32[2,2,128,128]{3,2,1,0:T(8,128)S(1)} %pad_maximum_fusion.16), channel_id=1, source_target_pairs={{8,6},{9,7},{16,14},{17,15},{24,22},{25,23},{32,30},{33,31},{40,38... | collective-permute-start | bytes 786440 | tf_op jit(solution)/shard_map/ppermute | solution.py:322
  (39 other events, 293.1 us)
Sparse Core Ops, SparseCore 0:
  19.7 65.7 all-gather.6
  88.2 67.7 all-gather.8
  158.9 66.0 all-gather.10
